TPU v7x, 128 devices: a whole 4x4x4 slice. The times are simulated.
128 devices in a mesh: gx: 32 (over x, y, core), gy: 4 (over z).
Axes of the slice: x: 4, y: 4, z: 4, core: 2. Of those that a mesh axis runs over, the one named last changes fastest.
Arguments:
- signals: float32 [64, 32, 16, 128], P('gx', 'gy'), may hold values from -6 to 6
- tiles: bfloat16 [64, 32, 4, 128, 128], P('gx', 'gy'), may hold values from 0 to 0.00390625
- tile_dir: int32 [64, 32, 4], P('gx', 'gy'), may hold values from 0 to 8
- tile_mask: int32 [64, 32, 4], P('gx', 'gy'), may hold values 0 or 1
- live_rows: int32 [64, 32], P('gx', 'gy'), may hold values from 32 to 128
- bound_rows: int32 [64, 32], P('gx', 'gy'), may hold values from 1 to 32, as said below
- scale_coeffs: float32 [6, 5], replicated, may hold values from -1 to 1
- spectral_bound: float32 [1], replicated, may hold values from 2.5 to 4
Outputs:
- coefficients: float32 [6, 64, 32, 16, 128], P(None, 'gx', 'gy')
- energy: float32 [6, 16], replicated
Inputs may be any that keep to these rules, and one draw needn't show every extreme that they name: `bound_rows`: in every draw, some blocks on every device have exactly 32 boundary rows.
All inputs are finite; a program needn't handle non-finite values. No bound on the sum of `tile_mask` on one device may be relied on, other than what follows from the above.
Results may differ from a plain program's by a relative error of at most 0.0003.
Values may be sent and summed in bfloat16 or wider, within the bound.
A program may use at most 64 MiB of HBM per device.

v0:
```python
import jax
import jax.numpy as jnp
from jax import lax
from jax.sharding import Mesh
from jax.sharding import PartitionSpec as P

DEG = 4
GX_GY = ("gx_0", "gx_1", "gx_2", "gy")
GX = ("gx_0", "gx_1", "gx_2")


def with_halo(array, sides, width):
    for axis, dim in sides:
        devices, length = (lax.axis_size(axis), array.shape[dim])
        up = [(i, (i + 1) % devices) for i in range(devices - 1)]
        down = [(j, i) for i, j in up]
        last = lax.slice_in_dim(array, length - width, length, axis=dim)
        first = lax.slice_in_dim(array, 0, width, axis=dim)
        before = lax.ppermute(last, axis, up)
        after = lax.ppermute(first, axis, down)
        array = jnp.concatenate([before, array, after], axis=dim)
    return array


def over_axes(array, axes):
    for axis in axes:
        array = lax.psum(array, axis)
    return array


def scaled_laplacian(values, adjacent, degree, factor):
    return factor * (degree * values - adjacent) - values


def shards(
    signals, tiles, tile_dir, tile_mask, live_rows, bound_rows, scale_coeffs, spectral_bound
):
    tile_size = signals.shape[3]
    extent_x = signals.shape[0]
    extent_y = signals.shape[1]
    slot_count = tiles.shape[2]
    block_count = extent_x * extent_y
    positions = lax.broadcasted_iota(jnp.int32, (1, 1, tile_size), 2)
    live_ind = (positions < live_rows[:, :, None]).astype(jnp.float32)
    bound_ind = (positions < bound_rows[:, :, None]).astype(jnp.float32)
    flat_tiles = tiles.reshape(block_count, slot_count, tile_size, tile_size)

    def adjacency(values):
        own_rows = values.astype(jnp.bfloat16)
        edge_rows = (values * bound_ind[:, :, None, :]).astype(jnp.bfloat16)
        padded = with_halo(edge_rows, ((GX, 0), ("gy", 1)), 1)
        slot_list = []
        for slot_index in range(slot_count):
            picked = jnp.zeros_like(own_rows)
            for direction in range(9):
                step_x = direction // 3 - 1
                step_y = direction % 3 - 1
                if direction == 4:
                    source = own_rows
                else:
                    source = padded[
                        1 + step_x : 1 + step_x + extent_x, 1 + step_y : 1 + step_y + extent_y
                    ]
                matches = (tile_dir[:, :, slot_index] == direction)[:, :, None, None]
                picked = jnp.where(matches, source, picked)
            kept = (tile_mask[:, :, slot_index] == 1)[:, :, None, None]
            picked = jnp.where(kept, picked, jnp.zeros_like(picked))
            slot_list.append(picked)
        inputs = jnp.stack(slot_list, axis=1 + 1)
        flat_inputs = inputs.reshape(block_count, slot_count, inputs.shape[3], tile_size)
        product = lax.dot_general(
            flat_inputs,
            flat_tiles,
            (((1, 3), (1, 3)), ((0,), (0,))),
            preferred_element_type=jnp.float32,
        )
        product = product.reshape(extent_x, extent_y, inputs.shape[3], tile_size)
        return product * live_ind[:, :, None, :]

    channels = signals.shape[2]
    initial = signals * live_ind[:, :, None, :]
    joined = jnp.concatenate([initial, live_ind[:, :, None, :]], axis=2)
    first_pass = adjacency(joined)
    degree = first_pass[:, :, channels:, :]
    factor = 2.0 / spectral_bound[0]
    previous = initial
    current = scaled_laplacian(initial, first_pass[:, :, :channels, :], degree, factor)
    totals = 0.5 * scale_coeffs[:, 0][:, None, None, None, None] * initial[None]
    totals = totals + scale_coeffs[:, 1][:, None, None, None, None] * current[None]
    for degree_index in range(2, DEG + 1):
        adjacent = adjacency(current)
        following = 2.0 * scaled_laplacian(current, adjacent, degree, factor) - previous
        previous = current
        current = following
        totals = totals + scale_coeffs[:, degree_index][:, None, None, None, None] * current[None]
    nodes = extent_x * extent_y * tile_size * lax.axis_size(GX) * lax.axis_size("gy")
    local_sums = jnp.sum(totals * totals, axis=(1, 2, 4))
    energy = over_axes(local_sums, GX_GY) / nodes
    return (totals, energy)


def solution(mesh):
    torus = Mesh(mesh.devices.reshape(4, 4, 2, mesh.shape["gy"]), ("gx_0", "gx_1", "gx_2", "gy"))
    placed = (
        P(GX, "gy", None, None),
        P(GX, "gy", None, None, None),
        P(GX, "gy", None),
        P(GX, "gy", None),
        P(GX, "gy"),
        P(GX, "gy"),
        P(),
        P(),
    )
    return jax.shard_map(
        shards,
        mesh=torus,
        in_specs=placed,
        out_specs=(P(None, GX, "gy", None, None), P()),
        check_vma=False,
    )
```

profile of v0, /device:TPU:1, one launch (start us, length us, event | category | flops | bytes accessed | tf_op | source)
XLA Modules:
  0.0 113.1 jit_solution(3090985521356103053)
XLA Ops:
  0.6 0.9 compare_convert_fusion
  1.6 0.8 fusion.35
  2.3 0.9 broadcast_multiply_fusion.1
  3.3 4.6 %collective-permute-start = (bf16[1,8,17,128]{3,2,1,0:T(8,128)(2,1)S(1)}, bf16[1,8,17,128]{3,2,1,0:T(8,128)(2,1)S(1)}, u32[]{:S(2)}, u32[]{:S(2)}) collective-permute-start(bf16[1,8,17,128]{3,2,1,0:T(8,128)(2,1)S(1)} %get-tuple-element.37), channel_id=1, source_target_pairs={{0,4},{4,8},{8,12},{12,16},{16,20},{20,24},{24,28},{28,32},{32,36}... | collective-permute-start | bytes 104456 | tf_op jit(solution)/shard_map/ppermute | solution.py:19
  7.9 1.9 %collective-permute-start.1 = (bf16[1,8,17,128]{3,2,1,0:T(8,128)(2,1)S(1)}, bf16[1,8,17,128]{3,2,1,0:T(8,128)(2,1)S(1)}, u32[]{:S(2)}, u32[]{:S(2)}) collective-permute-start(bf16[1,8,17,128]{3,2,1,0:T(8,128)(2,1)S(1)} %get-tuple-element.38), channel_id=1, source_target_pairs={{4,0},{8,4},{12,8},{16,12},{20,16},{24,20},{28,24},{32,28},{36,32}... | collective-permute-start | bytes 104456 | tf_op jit(solution)/shard_map/ppermute | solution.py:20
  9.8 0.8 broadcast_compare_fusion.30
  10.7 0.8 broadcast_compare_fusion.31
  11.5 0.8 slice_compare_fusion.3
  12.6 0.7 collective-permute-done.1
  13.3 1.3 %collective-permute-start.2 = (bf16[4,1,17,128]{3,2,1,0:T(8,128)(2,1)S(1)}, bf16[4,1,17,128]{3,2,1,0:T(8,128)(2,1)S(1)}, u32[]{:S(2)}, u32[]{:S(2)}) collective-permute-start(bf16[4,1,17,128]{3,2,1,0:T(8,128)(2,1)S(1)} %get-tuple-element.23), channel_id=1, source_target_pairs={{1,0},{2,1},{3,2},{5,4},{6,5},{7,6},{9,8},{10,9},{11,10},{13,12},{... | collective-permute-start | bytes 52232 | tf_op jit(solution)/shard_map/ppermute | solution.py:20
  14.6 4.2 %collective-permute-start.3 = (bf16[4,1,17,128]{3,2,1,0:T(8,128)(2,1)S(1)}, bf16[4,1,17,128]{3,2,1,0:T(8,128)(2,1)S(1)}, u32[]{:S(2)}, u32[]{:S(2)}) collective-permute-start(bf16[4,1,17,128]{3,2,1,0:T(8,128)(2,1)S(1)} %get-tuple-element.24), channel_id=1, source_target_pairs={{0,1},{1,2},{2,3},{4,5},{5,6},{6,7},{8,9},{9,10},{10,11},{12,13},{... | collective-permute-start | bytes 52232 | tf_op jit(solution)/shard_map/ppermute | solution.py:19
  19.8 0.2 select_select_fusion
  20.1 0.2 select_select_fusion.3
  20.3 0.2 select_select_fusion.2
  20.6 0.2 select_select_fusion.1
  20.9 0.7 fusion
  21.7 3.9 %collective-permute-start.4 = (bf16[1,8,16,128]{3,2,1,0:T(8,128)(2,1)S(1)}, bf16[1,8,16,128]{3,2,1,0:T(8,128)(2,1)S(1)}, u32[]{:S(2)}, u32[]{:S(2)}) collective-permute-start(bf16[1,8,16,128]{3,2,1,0:T(8,128)(2,1)S(1)} %get-tuple-element.43), channel_id=1, source_target_pairs={{0,4},{4,8},{8,12},{12,16},{16,20},{20,24},{24,28},{28,32},{32,36}... | collective-permute-start | bytes 98312 | tf_op jit(solution)/shard_map/ppermute | solution.py:19
  25.6 1.9 %collective-permute-start.5 = (bf16[1,8,16,128]{3,2,1,0:T(8,128)(2,1)S(1)}, bf16[1,8,16,128]{3,2,1,0:T(8,128)(2,1)S(1)}, u32[]{:S(2)}, u32[]{:S(2)}) collective-permute-start(bf16[1,8,16,128]{3,2,1,0:T(8,128)(2,1)S(1)} %get-tuple-element.44), channel_id=1, source_target_pairs={{4,0},{8,4},{12,8},{16,12},{20,16},{24,20},{28,24},{32,28},{36,32}... | collective-permute-start | bytes 98312 | tf_op jit(solution)/shard_map/ppermute | solution.py:20
  27.5 3.3 %collective-permute-done.5 = bf16[1,8,16,128]{3,2,1,0:T(8,128)(2,1)S(1)} collective-permute-done((bf16[1,8,16,128]{3,2,1,0:T(8,128)(2,1)S(1)}, bf16[1,8,16,128]{3,2,1,0:T(8,128)(2,1)S(1)}, u32[]{:S(2)}, u32[]{:S(2)}) %collective-permute-start.5) | collective-permute-done | bytes 32800 | tf_op jit(solution)/shard_map/ppermute | solution.py:20
  30.8 1.3 %collective-permute-start.6 = (bf16[4,1,16,128]{3,2,1,0:T(8,128)(2,1)S(1)}, bf16[4,1,16,128]{3,2,1,0:T(8,128)(2,1)S(1)}, u32[]{:S(2)}, u32[]{:S(2)}) collective-permute-start(bf16[4,1,16,128]{3,2,1,0:T(8,128)(2,1)S(1)} %get-tuple-element.35), channel_id=1, source_target_pairs={{1,0},{2,1},{3,2},{5,4},{6,5},{7,6},{9,8},{10,9},{11,10},{13,12},{... | collective-permute-start | bytes 49160 | tf_op jit(solution)/shard_map/ppermute | solution.py:20
  32.1 4.6 %collective-permute-start.7 = (bf16[4,1,16,128]{3,2,1,0:T(8,128)(2,1)S(1)}, bf16[4,1,16,128]{3,2,1,0:T(8,128)(2,1)S(1)}, u32[]{:S(2)}, u32[]{:S(2)}) collective-permute-start(bf16[4,1,16,128]{3,2,1,0:T(8,128)(2,1)S(1)} %get-tuple-element.36), channel_id=1, source_target_pairs={{0,1},{1,2},{2,3},{4,5},{5,6},{6,7},{8,9},{9,10},{10,11},{12,13},{... | collective-permute-start | bytes 49160 | tf_op jit(solution)/shard_map/ppermute | solution.py:19
  36.7 0.8 collective-permute-done.7
  37.6 0.2 select_select_fusion.15
  37.8 0.2 select_select_fusion.13
  38.3 0.2 select_select_fusion.12
  38.6 0.6 fusion.8
  39.3 2.8 %collective-permute-start.8 = (bf16[1,8,16,128]{3,2,1,0:T(8,128)(2,1)S(1)}, bf16[1,8,16,128]{3,2,1,0:T(8,128)(2,1)S(1)}, u32[]{:S(2)}, u32[]{:S(2)}) collective-permute-start(bf16[1,8,16,128]{3,2,1,0:T(8,128)(2,1)S(1)} %get-tuple-element.41), channel_id=1, source_target_pairs={{0,4},{4,8},{8,12},{12,16},{16,20},{20,24},{24,28},{28,32},{32,36}... | collective-permute-start | bytes 98312 | tf_op jit(solution)/shard_map/ppermute | solution.py:19
  42.1 1.9 %collective-permute-start.9 = (bf16[1,8,16,128]{3,2,1,0:T(8,128)(2,1)S(1)}, bf16[1,8,16,128]{3,2,1,0:T(8,128)(2,1)S(1)}, u32[]{:S(2)}, u32[]{:S(2)}) collective-permute-start(bf16[1,8,16,128]{3,2,1,0:T(8,128)(2,1)S(1)} %get-tuple-element.42), channel_id=1, source_target_pairs={{4,0},{8,4},{12,8},{16,12},{20,16},{24,20},{28,24},{32,28},{36,32}... | collective-permute-start | bytes 98312 | tf_op jit(solution)/shard_map/ppermute | solution.py:20
  44.0 3.3 %collective-permute-done.9 = bf16[1,8,16,128]{3,2,1,0:T(8,128)(2,1)S(1)} collective-permute-done((bf16[1,8,16,128]{3,2,1,0:T(8,128)(2,1)S(1)}, bf16[1,8,16,128]{3,2,1,0:T(8,128)(2,1)S(1)}, u32[]{:S(2)}, u32[]{:S(2)}) %collective-permute-start.9) | collective-permute-done | bytes 32800 | tf_op jit(solution)/shard_map/ppermute | solution.py:20
  47.3 1.3 %collective-permute-start.10 = (bf16[4,1,16,128]{3,2,1,0:T(8,128)(2,1)S(1)}, bf16[4,1,16,128]{3,2,1,0:T(8,128)(2,1)S(1)}, u32[]{:S(2)}, u32[]{:S(2)}) collective-permute-start(bf16[4,1,16,128]{3,2,1,0:T(8,128)(2,1)S(1)} %get-tuple-element.31), channel_id=1, source_target_pairs={{1,0},{2,1},{3,2},{5,4},{6,5},{7,6},{9,8},{10,9},{11,10},{13,12},{... | collective-permute-start | bytes 49160 | tf_op jit(solution)/shard_map/ppermute | solution.py:20
  48.6 4.5 %collective-permute-start.11 = (bf16[4,1,16,128]{3,2,1,0:T(8,128)(2,1)S(1)}, bf16[4,1,16,128]{3,2,1,0:T(8,128)(2,1)S(1)}, u32[]{:S(2)}, u32[]{:S(2)}) collective-permute-start(bf16[4,1,16,128]{3,2,1,0:T(8,128)(2,1)S(1)} %get-tuple-element.32), channel_id=1, source_target_pairs={{0,1},{1,2},{2,3},{4,5},{5,6},{6,7},{8,9},{9,10},{10,11},{12,13},{... | collective-permute-start | bytes 49160 | tf_op jit(solution)/shard_map/ppermute | solution.py:19
  53.2 0.8 collective-permute-done.11
  54.0 0.2 select_select_fusion.11
  55.1 0.6 fusion.16
  55.8 2.8 %collective-permute-start.12 = (bf16[1,8,16,128]{3,2,1,0:T(8,128)(2,1)S(1)}, bf16[1,8,16,128]{3,2,1,0:T(8,128)(2,1)S(1)}, u32[]{:S(2)}, u32[]{:S(2)}) collective-permute-start(bf16[1,8,16,128]{3,2,1,0:T(8,128)(2,1)S(1)} %get-tuple-element.39), channel_id=1, source_target_pairs={{0,4},{4,8},{8,12},{12,16},{16,20},{20,24},{24,28},{28,32},{32,36}... | collective-permute-start | bytes 98312 | tf_op jit(solution)/shard_map/ppermute | solution.py:19
  58.6 1.9 %collective-permute-start.13 = (bf16[1,8,16,128]{3,2,1,0:T(8,128)(2,1)S(1)}, bf16[1,8,16,128]{3,2,1,0:T(8,128)(2,1)S(1)}, u32[]{:S(2)}, u32[]{:S(2)}) collective-permute-start(bf16[1,8,16,128]{3,2,1,0:T(8,128)(2,1)S(1)} %get-tuple-element.40), channel_id=1, source_target_pairs={{4,0},{8,4},{12,8},{16,12},{20,16},{24,20},{28,24},{32,28},{36,32}... | collective-permute-start | bytes 98312 | tf_op jit(solution)/shard_map/ppermute | solution.py:20
  60.5 3.3 %collective-permute-done.13 = bf16[1,8,16,128]{3,2,1,0:T(8,128)(2,1)S(1)} collective-permute-done((bf16[1,8,16,128]{3,2,1,0:T(8,128)(2,1)S(1)}, bf16[1,8,16,128]{3,2,1,0:T(8,128)(2,1)S(1)}, u32[]{:S(2)}, u32[]{:S(2)}) %collective-permute-start.13) | collective-permute-done | bytes 32800 | tf_op jit(solution)/shard_map/ppermute | solution.py:20
  63.8 1.3 %collective-permute-start.14 = (bf16[4,1,16,128]{3,2,1,0:T(8,128)(2,1)S(1)}, bf16[4,1,16,128]{3,2,1,0:T(8,128)(2,1)S(1)}, u32[]{:S(2)}, u32[]{:S(2)}) collective-permute-start(bf16[4,1,16,128]{3,2,1,0:T(8,128)(2,1)S(1)} %get-tuple-element.27), channel_id=1, source_target_pairs={{1,0},{2,1},{3,2},{5,4},{6,5},{7,6},{9,8},{10,9},{11,10},{13,12},{... | collective-permute-start | bytes 49160 | tf_op jit(solution)/shard_map/ppermute | solution.py:20
  65.1 4.5 %collective-permute-start.15 = (bf16[4,1,16,128]{3,2,1,0:T(8,128)(2,1)S(1)}, bf16[4,1,16,128]{3,2,1,0:T(8,128)(2,1)S(1)}, u32[]{:S(2)}, u32[]{:S(2)}) collective-permute-start(bf16[4,1,16,128]{3,2,1,0:T(8,128)(2,1)S(1)} %get-tuple-element.28), channel_id=1, source_target_pairs={{0,1},{1,2},{2,3},{4,5},{5,6},{6,7},{8,9},{9,10},{10,11},{12,13},{... | collective-permute-start | bytes 49160 | tf_op jit(solution)/shard_map/ppermute | solution.py:19
  69.9 0.6 collective-permute-done.15
  70.5 0.2 select_select_fusion.7
  71.5 0.6 fusion.24
  72.2 1.3 %multiply_reduce_fusion = (f32[6,16]{1,0:T(8,128)S(1)}, f32[6,2,8,16,128]{4,3,2,1,0:T(8,128)}) fusion(f32[2,8,16,128]{3,2,1,0:T(8,128)S(1)} %multiply_subtract_fusion, f32[6]{0:T(128)S(1)} %get-tuple-element.5, f32[2,8,16,128]{3,2,1,0:T(8,128)S(1)} %get-tuple-element.12, f32[6]{0:T(128)S(1)} %get-tuple-element.6, f32[2,8,16,128]{3,2,1,0:T(8,128)S(1)} %get-tuple-element.16, ...), kind=kLoop, calls=%fused_computation | loop fusion | flops 2162592 | bytes 1442296 | tf_op jit(solution)/shard_map/reduce_sum | solution.py:97
  73.5 11.1 %psum.28 = f32[6,16]{1,0:T(8,128)S(1)} all-reduce(f32[6,16]{1,0:T(8,128)S(1)} %get-tuple-element.7), channel_id=1, replica_groups=mesh['gx_0'=4,'gx_1'=4,'gx_2'=2,'gy'=4] {'gx_0'}, use_global_device_ids=true, to_apply=%region_1.2 | all-reduce | flops 96 | bytes 768 | tf_op jit(solution)/shard_map/psum | solution.py:27
  84.6 12.8 %psum.29 = f32[6,16]{1,0:T(8,128)S(1)} all-reduce(f32[6,16]{1,0:T(8,128)S(1)} %psum.28), channel_id=1, replica_groups=mesh['gx_0'=4,'gx_1'=4,'gx_2'=2,'gy'=4] {'gx_1'}, use_global_device_ids=true, to_apply=%region_2.3 | all-reduce | flops 96 | bytes 768 | tf_op jit(solution)/shard_map/psum | solution.py:27
  97.4 4.5 %psum.30 = f32[6,16]{1,0:T(8,128)S(1)} all-reduce(f32[6,16]{1,0:T(8,128)S(1)} %psum.29), channel_id=1, replica_groups=mesh['gx_0'=4,'gx_1'=4,'gx_2'=2,'gy'=4] {'gx_2'}, use_global_device_ids=true, to_apply=%region_3.4 | all-reduce | flops 96 | bytes 768 | tf_op jit(solution)/shard_map/psum | solution.py:27
  101.9 10.6 %psum.31 = f32[6,16]{1,0:T(8,128)S(1)} all-reduce(f32[6,16]{1,0:T(8,128)S(1)} %psum.30), channel_id=1, replica_groups=mesh['gx_0'=4,'gx_1'=4,'gx_2'=2,'gy'=4] {'gy'}, use_global_device_ids=true, to_apply=%region_4.5 | all-reduce | flops 96 | bytes 768 | tf_op jit(solution)/shard_map/psum | solution.py:27
  112.5 0.6 broadcast_multiply_fusion.2
  (63 shorter events, 2.8 us)
Async XLA Ops:
  0.6 20.2 %copy-start = (bf16[2,8,4,128,128]{4,3,2,1,0:T(8,128)(2,1)S(1)}, bf16[2,8,4,128,128]{4,3,2,1,0:T(8,128)(2,1)}, u32[]{:S(2)}) copy-start(bf16[2,8,4,128,128]{4,3,2,1,0:T(8,128)(2,1)} %param.9) | copy-start | bytes 6291460
  3.3 9.3 %collective-permute-start = (bf16[1,8,17,128]{3,2,1,0:T(8,128)(2,1)S(1)}, bf16[1,8,17,128]{3,2,1,0:T(8,128)(2,1)S(1)}, u32[]{:S(2)}, u32[]{:S(2)}) collective-permute-start(bf16[1,8,17,128]{3,2,1,0:T(8,128)(2,1)S(1)} %get-tuple-element.37), channel_id=1, source_target_pairs={{0,4},{4,8},{8,12},{12,16},{16,20},{20,24},{24,28},{28,32},{32,36}... | collective-permute-start | bytes 104456 | tf_op jit(solution)/shard_map/ppermute | solution.py:19
  7.9 5.4 %collective-permute-start.1 = (bf16[1,8,17,128]{3,2,1,0:T(8,128)(2,1)S(1)}, bf16[1,8,17,128]{3,2,1,0:T(8,128)(2,1)S(1)}, u32[]{:S(2)}, u32[]{:S(2)}) collective-permute-start(bf16[1,8,17,128]{3,2,1,0:T(8,128)(2,1)S(1)} %get-tuple-element.38), channel_id=1, source_target_pairs={{4,0},{8,4},{12,8},{16,12},{20,16},{24,20},{28,24},{32,28},{36,32}... | collective-permute-start | bytes 104456 | tf_op jit(solution)/shard_map/ppermute | solution.py:20
  13.3 6.2 %collective-permute-start.2 = (bf16[4,1,17,128]{3,2,1,0:T(8,128)(2,1)S(1)}, bf16[4,1,17,128]{3,2,1,0:T(8,128)(2,1)S(1)}, u32[]{:S(2)}, u32[]{:S(2)}) collective-permute-start(bf16[4,1,17,128]{3,2,1,0:T(8,128)(2,1)S(1)} %get-tuple-element.23), channel_id=1, source_target_pairs={{1,0},{2,1},{3,2},{5,4},{6,5},{7,6},{9,8},{10,9},{11,10},{13,12},{... | collective-permute-start | bytes 52232 | tf_op jit(solution)/shard_map/ppermute | solution.py:20
  14.6 5.1 %collective-permute-start.3 = (bf16[4,1,17,128]{3,2,1,0:T(8,128)(2,1)S(1)}, bf16[4,1,17,128]{3,2,1,0:T(8,128)(2,1)S(1)}, u32[]{:S(2)}, u32[]{:S(2)}) collective-permute-start(bf16[4,1,17,128]{3,2,1,0:T(8,128)(2,1)S(1)} %get-tuple-element.24), channel_id=1, source_target_pairs={{0,1},{1,2},{2,3},{4,5},{5,6},{6,7},{8,9},{9,10},{10,11},{12,13},{... | collective-permute-start | bytes 52232 | tf_op jit(solution)/shard_map/ppermute | solution.py:19
  20.6 1.0 copy-start.1
  21.7 5.9 %collective-permute-start.4 = (bf16[1,8,16,128]{3,2,1,0:T(8,128)(2,1)S(1)}, bf16[1,8,16,128]{3,2,1,0:T(8,128)(2,1)S(1)}, u32[]{:S(2)}, u32[]{:S(2)}) collective-permute-start(bf16[1,8,16,128]{3,2,1,0:T(8,128)(2,1)S(1)} %get-tuple-element.43), channel_id=1, source_target_pairs={{0,4},{4,8},{8,12},{12,16},{16,20},{20,24},{24,28},{28,32},{32,36}... | collective-permute-start | bytes 98312 | tf_op jit(solution)/shard_map/ppermute | solution.py:19
  25.6 5.2 %collective-permute-start.5 = (bf16[1,8,16,128]{3,2,1,0:T(8,128)(2,1)S(1)}, bf16[1,8,16,128]{3,2,1,0:T(8,128)(2,1)S(1)}, u32[]{:S(2)}, u32[]{:S(2)}) collective-permute-start(bf16[1,8,16,128]{3,2,1,0:T(8,128)(2,1)S(1)} %get-tuple-element.44), channel_id=1, source_target_pairs={{4,0},{8,4},{12,8},{16,12},{20,16},{24,20},{28,24},{32,28},{36,32}... | collective-permute-start | bytes 98312 | tf_op jit(solution)/shard_map/ppermute | solution.py:20
  30.8 5.9 %collective-permute-start.6 = (bf16[4,1,16,128]{3,2,1,0:T(8,128)(2,1)S(1)}, bf16[4,1,16,128]{3,2,1,0:T(8,128)(2,1)S(1)}, u32[]{:S(2)}, u32[]{:S(2)}) collective-permute-start(bf16[4,1,16,128]{3,2,1,0:T(8,128)(2,1)S(1)} %get-tuple-element.35), channel_id=1, source_target_pairs={{1,0},{2,1},{3,2},{5,4},{6,5},{7,6},{9,8},{10,9},{11,10},{13,12},{... | collective-permute-start | bytes 49160 | tf_op jit(solution)/shard_map/ppermute | solution.py:20
  32.1 5.4 %collective-permute-start.7 = (bf16[4,1,16,128]{3,2,1,0:T(8,128)(2,1)S(1)}, bf16[4,1,16,128]{3,2,1,0:T(8,128)(2,1)S(1)}, u32[]{:S(2)}, u32[]{:S(2)}) collective-permute-start(bf16[4,1,16,128]{3,2,1,0:T(8,128)(2,1)S(1)} %get-tuple-element.36), channel_id=1, source_target_pairs={{0,1},{1,2},{2,3},{4,5},{5,6},{6,7},{8,9},{9,10},{10,11},{12,13},{... | collective-permute-start | bytes 49160 | tf_op jit(solution)/shard_map/ppermute | solution.py:19
  39.3 4.7 %collective-permute-start.8 = (bf16[1,8,16,128]{3,2,1,0:T(8,128)(2,1)S(1)}, bf16[1,8,16,128]{3,2,1,0:T(8,128)(2,1)S(1)}, u32[]{:S(2)}, u32[]{:S(2)}) collective-permute-start(bf16[1,8,16,128]{3,2,1,0:T(8,128)(2,1)S(1)} %get-tuple-element.41), channel_id=1, source_target_pairs={{0,4},{4,8},{8,12},{12,16},{16,20},{20,24},{24,28},{28,32},{32,36}... | collective-permute-start | bytes 98312 | tf_op jit(solution)/shard_map/ppermute | solution.py:19
  42.1 5.2 %collective-permute-start.9 = (bf16[1,8,16,128]{3,2,1,0:T(8,128)(2,1)S(1)}, bf16[1,8,16,128]{3,2,1,0:T(8,128)(2,1)S(1)}, u32[]{:S(2)}, u32[]{:S(2)}) collective-permute-start(bf16[1,8,16,128]{3,2,1,0:T(8,128)(2,1)S(1)} %get-tuple-element.42), channel_id=1, source_target_pairs={{4,0},{8,4},{12,8},{16,12},{20,16},{24,20},{28,24},{32,28},{36,32}... | collective-permute-start | bytes 98312 | tf_op jit(solution)/shard_map/ppermute | solution.py:20
  47.3 5.8 %collective-permute-start.10 = (bf16[4,1,16,128]{3,2,1,0:T(8,128)(2,1)S(1)}, bf16[4,1,16,128]{3,2,1,0:T(8,128)(2,1)S(1)}, u32[]{:S(2)}, u32[]{:S(2)}) collective-permute-start(bf16[4,1,16,128]{3,2,1,0:T(8,128)(2,1)S(1)} %get-tuple-element.31), channel_id=1, source_target_pairs={{1,0},{2,1},{3,2},{5,4},{6,5},{7,6},{9,8},{10,9},{11,10},{13,12},{... | collective-permute-start | bytes 49160 | tf_op jit(solution)/shard_map/ppermute | solution.py:20
  48.6 5.4 %collective-permute-start.11 = (bf16[4,1,16,128]{3,2,1,0:T(8,128)(2,1)S(1)}, bf16[4,1,16,128]{3,2,1,0:T(8,128)(2,1)S(1)}, u32[]{:S(2)}, u32[]{:S(2)}) collective-permute-start(bf16[4,1,16,128]{3,2,1,0:T(8,128)(2,1)S(1)} %get-tuple-element.32), channel_id=1, source_target_pairs={{0,1},{1,2},{2,3},{4,5},{5,6},{6,7},{8,9},{9,10},{10,11},{12,13},{... | collective-permute-start | bytes 49160 | tf_op jit(solution)/shard_map/ppermute | solution.py:19
  54.8 14.9 %copy-start.2 = (f32[6,5]{1,0:T(8,128)S(1)}, f32[6,5]{1,0:T(8,128)}, u32[]{:S(2)}) copy-start(f32[6,5]{1,0:T(8,128)} %param.14) | copy-start | bytes 364
  55.8 4.7 %collective-permute-start.12 = (bf16[1,8,16,128]{3,2,1,0:T(8,128)(2,1)S(1)}, bf16[1,8,16,128]{3,2,1,0:T(8,128)(2,1)S(1)}, u32[]{:S(2)}, u32[]{:S(2)}) collective-permute-start(bf16[1,8,16,128]{3,2,1,0:T(8,128)(2,1)S(1)} %get-tuple-element.39), channel_id=1, source_target_pairs={{0,4},{4,8},{8,12},{12,16},{16,20},{20,24},{24,28},{28,32},{32,36}... | collective-permute-start | bytes 98312 | tf_op jit(solution)/shard_map/ppermute | solution.py:19
  58.6 5.2 %collective-permute-start.13 = (bf16[1,8,16,128]{3,2,1,0:T(8,128)(2,1)S(1)}, bf16[1,8,16,128]{3,2,1,0:T(8,128)(2,1)S(1)}, u32[]{:S(2)}, u32[]{:S(2)}) collective-permute-start(bf16[1,8,16,128]{3,2,1,0:T(8,128)(2,1)S(1)} %get-tuple-element.40), channel_id=1, source_target_pairs={{4,0},{8,4},{12,8},{16,12},{20,16},{24,20},{28,24},{32,28},{36,32}... | collective-permute-start | bytes 98312 | tf_op jit(solution)/shard_map/ppermute | solution.py:20
  63.8 6.1 %collective-permute-start.14 = (bf16[4,1,16,128]{3,2,1,0:T(8,128)(2,1)S(1)}, bf16[4,1,16,128]{3,2,1,0:T(8,128)(2,1)S(1)}, u32[]{:S(2)}, u32[]{:S(2)}) collective-permute-start(bf16[4,1,16,128]{3,2,1,0:T(8,128)(2,1)S(1)} %get-tuple-element.27), channel_id=1, source_target_pairs={{1,0},{2,1},{3,2},{5,4},{6,5},{7,6},{9,8},{10,9},{11,10},{13,12},{... | collective-permute-start | bytes 49160 | tf_op jit(solution)/shard_map/ppermute | solution.py:20
  65.1 5.4 %collective-permute-start.15 = (bf16[4,1,16,128]{3,2,1,0:T(8,128)(2,1)S(1)}, bf16[4,1,16,128]{3,2,1,0:T(8,128)(2,1)S(1)}, u32[]{:S(2)}, u32[]{:S(2)}) collective-permute-start(bf16[4,1,16,128]{3,2,1,0:T(8,128)(2,1)S(1)} %get-tuple-element.28), channel_id=1, source_target_pairs={{0,1},{1,2},{2,3},{4,5},{5,6},{6,7},{8,9},{9,10},{10,11},{12,13},{... | collective-permute-start | bytes 49160 | tf_op jit(solution)/shard_map/ppermute | solution.py:19
where the time goes:
time: 115 us; the launch traced here: 113 us
  starting transfers between devices  44.7 us (39%)
  blocking collectives  39 us (34%)
  waiting for transfers between devices  13.1 us (11%)
  other arithmetic  11.6 us (10%)
  matrix products  2.6 us (2%)
  between operations  1.97 us (2%)
    psum x4, blocking collectives, over_axes(): array = lax.psum(array, axis)  39 us
    ppermute x8, starting transfers between devices, with_halo(): before = lax.ppermute(last, axis, up)  31.9 us
    ppermute x8, starting transfers between devices, with_halo(): after = lax.ppermute(first, axis, down)  12.8 us
    ppermute x8, waiting for transfers between devices, with_halo(): after = lax.ppermute(first, axis, down)  10.6 us
    select_n x16, other arithmetic, adjacency(): picked = jnp.where(kept, picked, jnp.zeros_like(picked))  3.91 us
    dot_general x4, matrix products, adjacency(): lax.dot_general(flat_inputs, flat_tiles, (((1, 3), (1, 3)), ((0,), (0,)))...  2.6 us
    ppermute x8, waiting for transfers between devices, with_halo(): before = lax.ppermute(last, axis, up)  2.49 us
  transfers between devices with their start and end apart: 16, of which 8 were waited for; matrix products, arithmetic and copies ran while one was open for 3% of the time, Pallas kernels for 0%

commit v1 on v0

v1 whole, which is shorter than its diff:
```python
import functools

import jax
import jax.numpy as jnp
from jax import lax
from jax.experimental import pallas as pl
from jax.experimental.pallas import tpu as pltpu
from jax.sharding import Mesh
from jax.sharding import PartitionSpec as P

MESH = pl.DeviceIdType.MESH
SIG, SCALES, DEG, SLOTS, TILE = 16, 6, 4, 4, 128
BX, BY = 2, 8
NB = BX * BY
GXN, GYN = 32, 4
ZERO = NB + (BX + 2) * (BY + 2)
NX = ZERO + 1
NODES = 64 * 32 * 128
DIRS = [(-1, 0), (1, 0), (0, -1), (0, 1), (-1, -1), (-1, 1), (1, -1), (1, 1)]
OPP = [DIRS.index((-dx, -dy)) for dx, dy in DIRS]


def coords(gx, gy):
    return (gx // 8, (gx // 2) % 4, gx % 2, gy)


def kernel(sig_h, til_h, dir_s, msk_s, liv_s, bnd_s, cof_s, spb_s,
           out_h, en_ref,
           sig, til, idx, x1, x2, x3, x4, cheb, tot, amul, op1, op2, op3, op4,
           rv1, rv2, rv3, rv4, ga, gb,
           ld_sem, snd, rcv, sa, ra, sb, rb, o_sem):
    x, y, c, z = (lax.axis_index(a) for a in ("gx_0", "gx_1", "gx_2", "gy"))
    gx = (x * 4 + y) * 2 + c
    gy = z
    sig_cp = pltpu.make_async_copy(sig_h, sig, ld_sem.at[NB])
    sig_cp.start()
    til_cp = []
    for b in range(NB):
        cp = pltpu.make_async_copy(til_h.at[b // BY, b % BY], til.at[b], ld_sem.at[b])
        cp.start()
        til_cp.append(cp)

    def exists(d):
        dx, dy = DIRS[d]
        ok = None
        for step, pos, n in ((dx, gx, GXN), (dy, gy, GYN)):
            if step == 0:
                continue
            this = pos > 0 if step < 0 else pos < n - 1
            ok = this if ok is None else jnp.logical_and(ok, this)
        return ok

    have = [exists(d) for d in range(8)]
    peer = [coords(gx + dx, gy + dy) for dx, dy in DIRS]
    xy = x * 4 + y
    zc = z * 2 + c
    a_peer = []
    for o in range(1, 8):
        t = (zc + o) % 8
        a_peer.append((x, y, t % 2, t // 2))
    b_peer = []
    for o in range(1, 16):
        t = (xy + o) % 16
        b_peer.append((t // 4, t % 4, c, z))

    recvs = (rv1, rv2, rv3, rv4)
    for rv in recvs:
        rv[...] = jnp.zeros_like(rv)
    bar = pltpu.get_barrier_semaphore()
    for d in range(8):
        @pl.when(have[d])
        def _(d=d):
            pl.semaphore_signal(bar, inc=1, device_id=peer[d], device_id_type=MESH)
    for p in a_peer + b_peer:
        pl.semaphore_signal(bar, inc=1, device_id=p, device_id_type=MESH)
    count = jnp.int32(22)
    for d in range(8):
        count = count + have[d].astype(jnp.int32)

    lane = lax.broadcasted_iota(jnp.int32, (1, TILE), 1)
    low = lane < 32
    f = 2.0 / spb_s[0, 0]

    for b in range(NB):
        i, j = b // BY, b % BY
        for s in range(SLOTS):
            d = dir_s[i, s, j]
            r = (d * 11) >> 5
            off = NB + (i + r) * (BY + 2) + (j + d - 3 * r)
            off = jnp.where(d == 4, b, off)
            idx[b * SLOTS + s] = jnp.where(msk_s[i, s, j] == 1, off, ZERO)

    def live_of(b):
        return (lane < liv_s[b // BY, b % BY]).astype(jnp.float32)

    def edge_of(b):
        return (lane < bnd_s[b // BY, b % BY]).astype(jnp.float32)

    for xb in (x1, x2, x3, x4):
        xb[ZERO] = jnp.zeros(xb.shape[1:], xb.dtype)

    def place(b, v, xb, packs):
        i, j = b // BY, b % BY
        xb[b] = v.astype(jnp.bfloat16)
        e = v * edge_of(b)
        xb[NB + (i + 1) * (BY + 2) + j + 1] = e.astype(jnp.bfloat16)
        jj = j + 2
        t, q = jj // 4, jj % 4
        e = pltpu.roll(e, 32 * q, 1) if q else e
        key = (i, t)
        packs[key] = e if key not in packs else packs[key] + e

    def flush(packs, op):
        for (i, t), v in packs.items():
            op[i, t] = v.astype(jnp.bfloat16)

    def copies(k, op, rv, d):
        dx, dy = DIRS[d]
        o = OPP[d]
        rows = {-1: pl.ds(0, 1), 1: pl.ds(1, 1), 0: pl.ds(0, 2)}[dx]
        cols = {-1: pl.ds(0, 1), 1: pl.ds(2, 1), 0: pl.ds(0, 3)}[dy]
        return pltpu.make_async_remote_copy(
            src_ref=op.at[rows, cols], dst_ref=rv.at[o, rows, cols],
            send_sem=snd.at[k, d], recv_sem=rcv.at[k, o],
            device_id=peer[d], device_id_type=MESH)

    def send(k, op, rv):
        for d in range(8):
            @pl.when(have[d])
            def _(d=d):
                copies(k, op, rv, d).start()

    def wait_recv(k, op, rv):
        for d in range(8):
            @pl.when(have[d])
            def _(d=d):
                dx, dy = DIRS[d]
                rows = {-1: pl.ds(1, 1), 1: pl.ds(0, 1), 0: pl.ds(0, 2)}[dx]
                cols = {-1: pl.ds(2, 1), 1: pl.ds(0, 1), 0: pl.ds(0, 3)}[dy]
                pltpu.make_async_remote_copy(
                    src_ref=op.at[rows, cols], dst_ref=rv.at[d, rows, cols],
                    send_sem=snd.at[k, d], recv_sem=rcv.at[k, d],
                    device_id=peer[d], device_id_type=MESH).wait_recv()

    def unpack(rv, xb):
        U, D, L, R, UL, UR, DL, DR = range(8)
        f32 = lambda a: a.astype(jnp.float32)
        rows = []
        rows.append((0, {0: f32(rv[U, 1, 0]) + f32(rv[UL, 1, 2]), 1: f32(rv[U, 1, 1]),
                         2: f32(rv[U, 1, 2]) + f32(rv[UR, 1, 0])}, range(1, 11)))
        for i in range(2):
            rows.append((i + 1, {0: f32(rv[L, i, 2]), 2: f32(rv[R, i, 0])}, (1, 10)))
        rows.append((3, {0: f32(rv[D, 0, 0]) + f32(rv[DL, 0, 2]), 1: f32(rv[D, 0, 1]),
                         2: f32(rv[D, 0, 2]) + f32(rv[DR, 0, 0])}, range(1, 11)))
        for r, tiles, cols in rows:
            for jj in cols:
                t, q = jj // 4, jj % 4
                v = tiles[t]
                v = pltpu.roll(v, TILE - 32 * q, 1) if q else v
                xb[NB + r * (BY + 2) + jj - 1] = jnp.where(low, v, 0.0).astype(jnp.bfloat16)

    def product(b, xb):
        acc = None
        for h in range(2):
            lhs = jnp.concatenate([xb[idx[b * SLOTS + 2 * h]], xb[idx[b * SLOTS + 2 * h + 1]]], axis=1)
            rhs = jnp.concatenate([til[b, 2 * h], til[b, 2 * h + 1]], axis=1)
            p = lax.dot_general(lhs, rhs, (((1,), (1,)), ((), ())), preferred_element_type=jnp.float32)
            acc = p if acc is None else acc + p
        return acc

    sig_cp.wait()
    packs = {}
    pad = lax.broadcasted_iota(jnp.int32, (16, TILE), 0) == 0
    for b in range(NB):
        live = live_of(b)
        v = sig[b // BY, b % BY] * live
        cheb[0, b] = v
        v32 = jnp.concatenate([v, jnp.where(pad, live, 0.0)], axis=0)
        place(b, v32, x1, packs)
    flush(packs, op1)
    pl.semaphore_wait(bar, count)
    send(0, op1, rv1)

    def add_totals(k):
        for s in range(SCALES):
            a = cof_s[s, k] * 0.5 if k == 0 else cof_s[s, k]
            for b in range(NB):
                t = a * cheb[k, b]
                tot[s, b] = t if k == 0 else tot[s, b] + t

    add_totals(0)
    for b in range(NB):
        til_cp[b].wait()
    wait_recv(0, op1, rv1)
    unpack(rv1, x1)
    packs = {}
    for b in range(NB):
        acc = product(b, x1)
        live = live_of(b)
        v = cheb[0, b]
        am = f * (acc[SIG:SIG + 1] * live) - 1.0
        amul[b] = jnp.broadcast_to(am, (8, TILE))
        cur = am * v - (f * live) * acc[:SIG]
        cheb[1, b] = cur
        place(b, cur, x2, packs)
    flush(packs, op2)
    send(1, op2, rv2)

    stages = ((1, x2, op2, rv2, x3, op3, rv3), (2, x3, op3, rv3, x4, op4, rv4), (3, x4, op4, rv4, None, None, None))
    for k, xb, op, rv, xn, opn, rvn in stages:
        add_totals(k)
        wait_recv(k, op, rv)
        unpack(rv, xb)
        packs = {}
        sq = [None] * SCALES
        for b in range(NB):
            acc = product(b, xb)
            am = amul[b]
            am = 2.0 * jnp.concatenate([am, am], axis=0)
            cur = am * cheb[k, b] - (2.0 * f * live_of(b)) * acc - cheb[k - 1, b]
            if k < 3:
                cheb[k + 1, b] = cur
                place(b, cur, xn, packs)
            else:
                for s in range(SCALES):
                    t = tot[s, b] + cof_s[s, 4] * cur
                    tot[s, b] = t
                    sq[s] = t * t if sq[s] is None else sq[s] + t * t
        if k < 3:
            flush(packs, opn)
            send(k + 1, opn, rvn)

    out_cp = pltpu.make_async_copy(tot, out_h, o_sem)
    out_cp.start()

    m = jnp.concatenate(sq, axis=0)
    hi = m.astype(jnp.bfloat16)
    r1 = m - hi.astype(jnp.float32)
    mid = r1.astype(jnp.bfloat16)
    lo = (r1 - mid.astype(jnp.float32)).astype(jnp.bfloat16)
    ones = jnp.ones((16, TILE), jnp.bfloat16)
    row = None
    for part in (lo, mid, hi):
        p = lax.dot_general(ones, part, (((1,), (1,)), ((), ())), preferred_element_type=jnp.float32)
        row = p if row is None else row + p
    row = jnp.concatenate([row[0:1], jnp.zeros((1, TILE - SCALES * SIG), jnp.float32)], axis=1)

    def phase(buf, mine, n, peers, s_sem, r_sem, value):
        buf[mine] = value
        for o, p in enumerate(peers):
            pltpu.make_async_remote_copy(
                src_ref=buf.at[mine], dst_ref=buf.at[mine], send_sem=s_sem.at[o],
                recv_sem=r_sem.at[mine], device_id=p, device_id_type=MESH).start()
        for o, p in enumerate(peers):
            src = (mine + o + 1) % n
            pltpu.make_async_remote_copy(
                src_ref=buf.at[mine], dst_ref=buf.at[src], send_sem=s_sem.at[o],
                recv_sem=r_sem.at[src], device_id=p, device_id_type=MESH).wait_recv()
        total = buf[0]
        for q in range(1, n):
            total = total + buf[q]
        return total

    part = phase(ga, zc, 8, a_peer, sa, ra, row)
    full = phase(gb, xy, 16, b_peer, sb, rb, part) * (1.0 / NODES)
    res = jnp.zeros((8, TILE), jnp.float32)
    sub = lax.broadcasted_iota(jnp.int32, (8, TILE), 0)
    full8 = jnp.broadcast_to(full, (8, TILE))
    for s in range(SCALES):
        v = pltpu.roll(full8, TILE - 16 * s, 1) if s else full8
        res = jnp.where(sub == s, v, res)
    en_ref[...] = res[:SCALES, :SIG]

    out_cp.wait()
    for k, (op, rv) in enumerate(((op1, rv1), (op2, rv2), (op3, rv3), (op4, rv4))):
        for d in range(8):
            @pl.when(have[d])
            def _(k=k, op=op, rv=rv, d=d):
                copies(k, op, rv, d).wait_send()
    for o, p in enumerate(a_peer):
        pltpu.make_async_remote_copy(
            src_ref=ga.at[zc], dst_ref=ga.at[zc], send_sem=sa.at[o], recv_sem=ra.at[zc],
            device_id=p, device_id_type=MESH).wait_send()
    for o, p in enumerate(b_peer):
        pltpu.make_async_remote_copy(
            src_ref=gb.at[xy], dst_ref=gb.at[xy], send_sem=sb.at[o], recv_sem=rb.at[xy],
            device_id=p, device_id_type=MESH).wait_send()


def shards(signals, tiles, tile_dir, tile_mask, live_rows, bound_rows, scale_coeffs, spectral_bound):
    bf, f32 = jnp.bfloat16, jnp.float32
    vm = pltpu.VMEM
    smem = pl.BlockSpec(memory_space=pltpu.SMEM)
    hbm = pl.BlockSpec(memory_space=pl.ANY)
    dma = pltpu.SemaphoreType.DMA
    out, energy = pl.pallas_call(
        kernel,
        out_shape=(jax.ShapeDtypeStruct((SCALES, NB, SIG, TILE), f32),
                   jax.ShapeDtypeStruct((SCALES, SIG), f32)),
        in_specs=[hbm, hbm] + [smem] * 6,
        out_specs=(hbm, pl.BlockSpec(memory_space=pltpu.VMEM)),
        scratch_shapes=[
            vm((BX, BY, SIG, TILE), f32), vm((NB, SLOTS, TILE, TILE), bf), pltpu.SMEM((NB * SLOTS,), jnp.int32),
            vm((NX, 32, TILE), bf), vm((NX, SIG, TILE), bf), vm((NX, SIG, TILE), bf), vm((NX, SIG, TILE), bf),
            vm((DEG, NB, SIG, TILE), f32), vm((SCALES, NB, SIG, TILE), f32), vm((NB, 8, TILE), f32),
            vm((2, 3, 32, TILE), bf), vm((2, 3, SIG, TILE), bf), vm((2, 3, SIG, TILE), bf), vm((2, 3, SIG, TILE), bf),
            vm((8, 2, 3, 32, TILE), bf), vm((8, 2, 3, SIG, TILE), bf), vm((8, 2, 3, SIG, TILE), bf), vm((8, 2, 3, SIG, TILE), bf),
            vm((8, 1, TILE), f32), vm((16, 1, TILE), f32),
            dma((NB + 1,)), dma((4, 8)), dma((4, 8)), dma((7,)), dma((8,)), dma((15,)), dma((16,)), dma,
        ],
        compiler_params=pltpu.CompilerParams(collective_id=0, has_side_effects=True),
        name="wavelet",
    )(signals, tiles, jnp.swapaxes(tile_dir, 1, 2), jnp.swapaxes(tile_mask, 1, 2), live_rows, bound_rows,
      scale_coeffs, spectral_bound.reshape(1, 1))
    return out.reshape(SCALES, BX, BY, SIG, TILE), energy


def solution(mesh):
    torus = Mesh(mesh.devices.reshape(4, 4, 2, mesh.shape["gy"]), ("gx_0", "gx_1", "gx_2", "gy"))
    gxs = ("gx_0", "gx_1", "gx_2")
    placed = (
        P(gxs, "gy", None, None),
        P(gxs, "gy", None, None, None),
        P(gxs, "gy", None),
        P(gxs, "gy", None),
        P(gxs, "gy"),
        P(gxs, "gy"),
        P(),
        P(),
    )
    return jax.shard_map(
        shards,
        mesh=torus,
        in_specs=placed,
        out_specs=(P(None, gxs, "gy", None, None), P()),
        check_vma=False,
    )
```

time: 115 us -> 41.4 us (0.36); the launches traced: 113 us -> 40.9 us
  starting transfers between devices: 44.7 us -> 0 us
  blocking collectives: 39 us -> 0 us
  Pallas kernels: 0 us -> 36.3 us
  waiting for transfers between devices: 13.1 us -> 0 us
  other arithmetic: 11.6 us -> 0 us
  local copies, waits for them, and re-layouts: 0.2 us -> 3.33 us
  matrix products: 2.6 us -> 0 us
    ppermute x16 -> x0, starting transfers between devices: 44.7 us -> none  [the longest x8 31.9 us: with_halo(): before = lax.ppermute(last, axis, up)]
    psum x4 -> x0, blocking collectives: 39 us -> none  [over_axes(): array = lax.psum(array, axis)]
    pallas_call x0 -> x1, Pallas kernels: none -> 36.3 us  [shards(): pl.pallas_call(kernel, out_shape=(jax.ShapeDtypeStruct((SCALES, NB, SIG,...]
    ppermute x16 -> x0, waiting for transfers between devices: 13.1 us -> none  [the longest x8 10.6 us: with_halo(): after = lax.ppermute(first, axis, down)]
    select_n x16 -> x0, other arithmetic: 3.91 us -> none  [adjacency(): picked = jnp.where(kept, picked, jnp.zeros_like(picked))]
    unnamed x27 -> x2, local copies, waits for them, and re-layouts: 0.16 us -> 3.33 us
    dot_general x4 -> x0, matrix products: 2.6 us -> none  [adjacency(): lax.dot_general(flat_inputs, flat_tiles, (((1, 3), (1, 3)), ((0,), (0,)))...]
    eq x3 -> x0, other arithmetic: 2.5 us -> none  [the longest x2 1.66 us: adjacency(): matches = (tile_dir[:, :, slot_index] == direction)[:, :, None, None]]
  transfers between devices with their start and end apart: 16 -> 0, of which waited for: 8 -> 0; matrix products, arithmetic and copies ran while one was open for 3% -> 0% of each run, Pallas kernels for 0% -> 0%
where the time goes in v1:
time: 41.4 us; the launch traced here: 40.9 us
  Pallas kernels  36.3 us (88%)
  local copies, waits for them, and re-layouts  3.33 us (8%)
  between operations  1.29 us (3%)
    pallas_call x1, Pallas kernels, shards(): pl.pallas_call(kernel, out_shape=(jax.ShapeDtypeStruct((SCALES, NB, SIG,...  36.3 us
    unnamed x2, local copies, waits for them, and re-layouts  3.33 us

profile of v1, /device:TPU:1, one launch (start us, length us, event | category | flops | bytes accessed | tf_op | source)
XLA Modules:
  0.0 40.9 jit_solution(17155701918694955257)
XLA Ops:
  1.3 36.3 %wavelet.1 = (f32[6,16,16,128]{3,2,1,0:T(8,128)}, f32[6,16]{1,0:T(8,128)}) custom-call(f32[2,8,16,128]{3,2,1,0:T(8,128)} %sig_h.1, bf16[2,8,4,128,128]{4,3,2,1,0:T(8,128)(2,1)} %til_h.1, s32[2,4,8]{2,1,0:T(4,128)} %bitcast.6, s32[2,4,8]{2,1,0:T(4,128)} %bitcast.7, s32[2,8]{1,0:T(2,128)} %liv_s.1, s32[2,8]{1,0:T(2,128)} %bnd_s.1, f32[6,5]{1,0:T(8,128)} %cof_s.1, ...), custom_call_target="tpu_custom_call" | custom-call | tf_op jit(solution)/shard_map/wavelet/pallas_call | solution.py:296
  37.6 2.1 %copy.13 = f32[6,2,8,16,128]{4,3,2,1,0:T(8,128)} copy(f32[6,2,8,16,128]{4,3,2,1,0:T(8,128)} %bitcast.5) | data formatting | bytes 1572864
  39.7 1.3 %copy.14 = f32[6,16]{1,0:T(8,128)} copy(f32[6,16]{1,0:T(8,128)} %get-tuple-element.9) | data formatting | bytes 768

commit v2 on v1

v2 whole, which is shorter than its diff:
```python
import functools

import jax
import jax.numpy as jnp
from jax import lax
from jax.experimental import pallas as pl
from jax.experimental.pallas import tpu as pltpu
from jax.sharding import Mesh
from jax.sharding import PartitionSpec as P

MESH = pl.DeviceIdType.MESH
SIG, SCALES, DEG, SLOTS, TILE = 16, 6, 4, 4, 128
BX, BY = 2, 8
NB = BX * BY
GXN, GYN = 32, 4
ZERO = NB + (BX + 2) * (BY + 2)
NX = ZERO + 1
NODES = 64 * 32 * 128
DIRS = [(-1, 0), (1, 0), (0, -1), (0, 1), (-1, -1), (-1, 1), (1, -1), (1, 1)]
OPP = [DIRS.index((-dx, -dy)) for dx, dy in DIRS]


def coords(gx, gy):
    return (gx // 8, (gx // 2) % 4, gx % 2, gy)


def kernel(sig_h, til_h, dir_s, msk_s, liv_s, bnd_s, cof_s, spb_s,
           out_h, en_ref,
           sig, til, idx, loc, x1, x2, x3, x4, cheb, tot, amul, op1, op3, sp1, sp3, tp,
           rv1, rv3, rs1, rs3, tr, ga, gb,
           ld_sem, vs, vr, ss, sr, ts, tr_sem, sa, ra, sb, rb, o_sem):
    x, y, c, z = (lax.axis_index(a) for a in ("gx_0", "gx_1", "gx_2", "gy"))
    gx = (x * 4 + y) * 2 + c
    gy = z
    sig_cp = pltpu.make_async_copy(sig_h, sig, ld_sem.at[NB])
    sig_cp.start()
    til_cp = []
    for b in range(NB):
        cp = pltpu.make_async_copy(til_h.at[b // BY, b % BY], til.at[b], ld_sem.at[b])
        cp.start()
        til_cp.append(cp)

    def exists(d):
        dx, dy = DIRS[d]
        ok = None
        for step, pos, n in ((dx, gx, GXN), (dy, gy, GYN)):
            if step == 0:
                continue
            this = pos > 0 if step < 0 else pos < n - 1
            ok = this if ok is None else jnp.logical_and(ok, this)
        return ok

    have = [exists(d) for d in range(8)]
    peer = [coords(gx + dx, gy + dy) for dx, dy in DIRS]
    xy = x * 4 + y
    zc = z * 2 + c
    a_peer = []
    for o in range(1, 8):
        t = (zc + o) % 8
        a_peer.append((x, y, t % 2, t // 2))
    b_peer = []
    for o in range(1, 16):
        t = (xy + o) % 16
        b_peer.append((t // 4, t % 4, c, z))

    for buf in (rv1, rv3, rs1, rs3, tr):
        buf[...] = jnp.zeros_like(buf)
    bar = pltpu.get_barrier_semaphore()
    for d in range(8):
        @pl.when(have[d])
        def _(d=d):
            pl.semaphore_signal(bar, inc=1, device_id=peer[d], device_id_type=MESH)
    for p in a_peer + b_peer:
        pl.semaphore_signal(bar, inc=1, device_id=p, device_id_type=MESH)
    count = jnp.int32(22)
    for d in range(8):
        count = count + have[d].astype(jnp.int32)

    lane = lax.broadcasted_iota(jnp.int32, (1, TILE), 1)
    low = lane < 32
    f = 2.0 / spb_s[0, 0]
    bf16 = lambda a: a.astype(jnp.bfloat16)
    f32 = lambda a: a.astype(jnp.float32)

    for b in range(NB):
        i, j = b // BY, b % BY
        for s in range(SLOTS):
            d = dir_s[i, s, j]
            r = (d * 11) >> 5
            q = d - 3 * r
            off = NB + (i + r) * (BY + 2) + (j + q)
            off = jnp.where(d == 4, b, off)
            off = jnp.where(msk_s[i, s, j] == 1, off, ZERO)
            idx[b * SLOTS + s] = off
            away = r == 2 * i
            if j in (0, BY - 1):
                away = jnp.logical_or(away, q == (0 if j == 0 else 2))
            loc[b * SLOTS + s] = jnp.where(away, ZERO, off)

    def live_of(b):
        return (lane < liv_s[b // BY, b % BY]).astype(jnp.float32)

    def edge_of(b):
        return (lane < bnd_s[b // BY, b % BY]).astype(jnp.float32)

    RING = [(r, q) for r in (1, 4) for q in range(1, 11)] + [(r, q) for r in (2, 3) for q in (1, 10)]
    slot_of = lambda er, ec: NB + (er - 1) * (BY + 2) + ec - 1
    for xb in (x1, x2, x3, x4):
        xb[ZERO] = jnp.zeros(xb.shape[1:], xb.dtype)
    for xb in (x2, x4):
        for er, ec in RING:
            xb[slot_of(er, ec)] = jnp.zeros(xb.shape[1:], xb.dtype)

    def shift(v, q):
        q = q % 4
        return pltpu.roll(v, 32 * q, 1) if q else v

    def add_to(packs, i, j, v):
        key = (i, (j + 2) // 4)
        v = shift(v, j + 2)
        packs[key] = v if key not in packs else packs[key] + v

    def place(b, v, xb, packs=None):
        i, j = b // BY, b % BY
        xb[b] = bf16(v)
        e = v * edge_of(b)
        xb[slot_of(i + 2, j + 2)] = bf16(e)
        if packs is not None:
            add_to(packs, i, j, e)

    def flush(packs, buf, tile_first):
        for (i, t), v in packs.items():
            if tile_first:
                buf[t, i] = bf16(v)
            else:
                buf[i, t] = bf16(v)

    def part_v(dx, dy):
        return ({-1: pl.ds(0, 1), 1: pl.ds(2, 1), 0: pl.ds(0, 3)}[dy],)

    def part_s(dx, dy):
        return ({-1: pl.ds(0, 1), 1: pl.ds(1, 1), 0: pl.ds(0, 2)}[dx],
                {-1: pl.ds(0, 1), 1: pl.ds(2, 1), 0: pl.ds(0, 3)}[dy])

    def part_t(dx, dy):
        return ({-1: pl.ds(0, 1), 1: pl.ds(1, 1), 0: pl.ds(0, 2)}[dx],
                {-1: pl.ds(0, 2), 1: pl.ds(8, 2), 0: pl.ds(0, 10)}[dy])

    def descriptor(src, dst, part, s_sem, r_sem, d, o, at):
        return pltpu.make_async_remote_copy(
            src_ref=src.at[at], dst_ref=dst.at[(o,) + at], send_sem=s_sem.at[d],
            recv_sem=r_sem.at[o], device_id=peer[d], device_id_type=MESH)

    started = []

    def send(src, dst, part, s_sem, r_sem):
        started.append((src, dst, part, s_sem, r_sem))
        for d in (4, 5, 6, 7, 0, 1, 2, 3):
            @pl.when(have[d])
            def _(d=d):
                descriptor(src, dst, part, s_sem, r_sem, d, OPP[d], part(*DIRS[d])).start()

    def wait_recv(src, dst, part, s_sem, r_sem):
        for d in range(8):
            @pl.when(have[d])
            def _(d=d):
                descriptor(src, dst, part, s_sem, r_sem, d, d, part(*DIRS[OPP[d]])).wait_recv()

    v_args = ((op1, rv1, part_v, vs.at[0], vr.at[0]), (op3, rv3, part_v, vs.at[1], vr.at[1]))
    s_args = ((sp1, rs1, part_s, ss.at[0], sr.at[0]), (sp3, rs3, part_s, ss.at[1], sr.at[1]))
    t_args = (tp, tr, part_t, ts, tr_sem)
    U, D, L, R, UL, UR, DL, DR = range(8)
    left = lane < 64

    def rows_of(op, rv):
        rows = []
        for r in range(6):
            i = r % 2
            if r in (2, 3):
                lo, hi, mine = rv[L, 2, i], rv[R, 0, i], [op[t, i] for t in range(3)]
            else:
                u, ul, ur = (U, UL, UR) if r < 2 else (D, DL, DR)
                lo, hi, mine = rv[ul, 2, i], rv[ur, 0, i], [rv[u, t, i] for t in range(3)]
            mine = [f32(v) for v in mine]
            rows.append([jnp.where(left, f32(lo), mine[0]), mine[1], jnp.where(left, mine[2], f32(hi))])
        return rows

    def unpack(rows, xb):
        for er, ec in RING:
            v = jnp.where(low, shift(rows[er][ec // 4], -ec), 0.0)
            xb[slot_of(er, ec)] = bf16(v)

    def contract(lhs, rhs):
        return lax.dot_general(lhs, rhs, (((1,), (1,)), ((), ())), preferred_element_type=jnp.float32)

    def product(b, xb, table, rows=TILE):
        acc = None
        for h in range(2):
            pick = [xb[table[b * SLOTS + 2 * h + n]] for n in range(2)]
            rhs = [til[b, 2 * h + n, :rows] for n in range(2)]
            p = contract(jnp.concatenate(pick, axis=1), jnp.concatenate(rhs, axis=1))
            acc = p if acc is None else acc + p
        return acc

    sig_cp.wait()
    packs = {}
    pad = lax.broadcasted_iota(jnp.int32, (16, TILE), 0) == 0
    for b in range(NB):
        live = live_of(b)
        v = sig[b // BY, b % BY] * live
        cheb[0, b] = v
        place(b, jnp.concatenate([v, jnp.where(pad, live, 0.0)], axis=0), x1, packs)
    flush(packs, op1, True)

    def corner(b, wanted):
        i, j = b // BY, b % BY
        total = None
        for d, group in wanted:
            acc = None
            for s in range(SLOTS):
                on = jnp.logical_and(dir_s[i, s, j] == d, msk_s[i, s, j] == 1).astype(jnp.float32)
                t = f32(til[b, s, :32]) * on
                acc = t if acc is None else acc + t
            acc = shift(jnp.where(low, acc, 0.0), group)
            total = acc if total is None else total + acc
        inside = lax.broadcasted_iota(jnp.int32, (32, TILE), 0) < bnd_s[i, j]
        return bf16(jnp.where(inside, total, 0.0))

    def local_part(b, xb, scale, prev, first, packs):
        acc = product(b, xb, loc, 32)
        v = cheb[2 * (1 - first), b, :, :32]
        fl = scale * live_of(b)[:, :32]
        if first:
            am = fl * acc[SIG:SIG + 1] - 1.0
            out = am * v - fl * acc[:SIG]
        else:
            am = amul[b, :1, :32]
            out = 2.0 * am * v - fl * acc - prev
        out = out * edge_of(b)[:, :32]
        add_to(packs, b // BY, b % BY, jnp.concatenate([out, jnp.zeros((SIG, TILE - 32), jnp.float32)], axis=1))

    packs = {}
    for b in range(NB):
        til_cp[b].wait()
        i, j = b // BY, b % BY
        dx = 2 * i
        tp[i, 1 + j] = corner(b, [(3 * dx + q, j + 1 + q) for q in range(3)])
        if j == 0:
            tp[i, 0] = corner(b, [(3 - 3 * i, 1), (6 - 3 * i, 2)])
        if j == BY - 1:
            tp[i, 9] = corner(b, [(5 - 3 * i, 2), (8 - 3 * i, 3)])
        local_part(b, x1, f, None, 1, packs)
    flush(packs, sp1, False)

    pl.semaphore_wait(bar, count)
    send(*v_args[0])
    send(*s_args[0])
    send(*t_args)

    def add_totals(k):
        for s in range(SCALES):
            a = cof_s[s, k] * 0.5 if k == 0 else cof_s[s, k]
            for b in range(NB):
                t = a * cheb[k, b]
                tot[s, b] = t if k == 0 else tot[s, b] + t

    def advance_ring(rows, rs, xn, first):
        wide = [[bf16(v) for v in r] for r in rows]

        def row_input(er, ec):
            t, q = ec // 4, ec % 4
            if q == 0:
                return bf16(jnp.where(lane >= 96, rows[er][t - 1], rows[er][t]))
            if q == 3:
                return bf16(jnp.where(low, rows[er][t + 1], rows[er][t]))
            return wide[er][t]

        def column_input(er, ec):
            g = (ec + 1) % 4
            at = jnp.logical_and(lane >= 32 * g, lane < 32 * g + 32)
            return bf16(jnp.where(at, shift(rows[er + 1][ec // 4], 1), rows[er][ec // 4]))

        inputs = {}
        for er, ec in RING:
            side = 0 if ec == 1 else 2 if ec == 10 else 1
            level = 0 if er == 1 else 2 if er == 4 else 1
            owner = {(0, 0): UL, (0, 1): U, (0, 2): UR, (1, 0): L, (1, 2): R,
                     (2, 0): DL, (2, 1): D, (2, 2): DR}[(level, side)]
            i = {1: 1, 2: 0, 3: 1, 4: 0}[er]
            j = (ec - 2) % BY
            base = er - i
            lhs, rhs = row_input(er + (1 if i else -1), ec), tr[owner, i, 1 + j]
            if j in (0, BY - 1):
                col = ec - 1 if j == 0 else ec + 1
                if (base, col) not in inputs:
                    inputs[(base, col)] = column_input(base, col)
                lhs = jnp.concatenate([lhs, inputs[(base, col)]], axis=1)
                rhs = jnp.concatenate([rhs, tr[owner, i, 0 if j == 0 else 9]], axis=1)
            acc = contract(lhs, rhs)
            own = shift(f32(rs[owner, i, ((j + 2) // 4)]), -ec)[:, :32]
            if first:
                v = shift(rows[er][ec // 4], -ec)[:SIG, :32]
                new = own + f * (acc[SIG:SIG + 1] * v - acc[:SIG])
            else:
                new = own - (2.0 * f) * acc
            xn[slot_of(er, ec), :, pl.ds(0, 32)] = bf16(new)

    add_totals(0)
    wait_recv(*v_args[0])
    rows = rows_of(op1, rv1)
    unpack(rows, x1)
    for b in range(NB):
        acc = product(b, x1, idx)
        live = live_of(b)
        v = cheb[0, b]
        am = f * (acc[SIG:SIG + 1] * live) - 1.0
        amul[b] = jnp.broadcast_to(am, (8, TILE))
        cur = am * v - (f * live) * acc[:SIG]
        cheb[1, b] = cur
        place(b, cur, x2)
    wait_recv(*s_args[0])
    wait_recv(*t_args)
    advance_ring(rows, rs1, x2, 1)

    def step(b, k, xb):
        acc = product(b, xb, idx)
        am = amul[b]
        am = 2.0 * jnp.concatenate([am, am], axis=0)
        return am * cheb[k, b] - (2.0 * f * live_of(b)) * acc - cheb[k - 1, b]

    packs = {}
    for b in range(NB):
        cur = step(b, 1, x2)
        cheb[2, b] = cur
        place(b, cur, x3, packs)
    flush(packs, op3, True)
    send(*v_args[1])
    packs = {}
    for b in range(NB):
        local_part(b, x3, 2.0 * f, cheb[1, b, :, :32], 0, packs)
    flush(packs, sp3, False)
    send(*s_args[1])
    add_totals(1)
    add_totals(2)

    wait_recv(*v_args[1])
    rows = rows_of(op3, rv3)
    unpack(rows, x3)
    for b in range(NB):
        cur = step(b, 2, x3)
        cheb[3, b] = cur
        place(b, cur, x4)
    wait_recv(*s_args[1])
    advance_ring(rows, rs3, x4, 0)
    sq = [None] * SCALES
    for b in range(NB):
        cur = step(b, 3, x4)
        for s in range(SCALES):
            t = tot[s, b] + cof_s[s, 3] * cheb[3, b] + cof_s[s, 4] * cur
            tot[s, b] = t
            sq[s] = t * t if sq[s] is None else sq[s] + t * t

    out_cp = pltpu.make_async_copy(tot, out_h, o_sem)
    out_cp.start()

    m = jnp.concatenate(sq, axis=0)
    hi = m.astype(jnp.bfloat16)
    r1 = m - hi.astype(jnp.float32)
    mid = r1.astype(jnp.bfloat16)
    lo = (r1 - mid.astype(jnp.float32)).astype(jnp.bfloat16)
    ones = jnp.ones((16, TILE), jnp.bfloat16)
    row = None
    for part in (lo, mid, hi):
        p = lax.dot_general(ones, part, (((1,), (1,)), ((), ())), preferred_element_type=jnp.float32)
        row = p if row is None else row + p
    row = jnp.concatenate([row[0:1], jnp.zeros((1, TILE - SCALES * SIG), jnp.float32)], axis=1)

    def phase(buf, mine, n, peers, s_sem, r_sem, value):
        buf[mine] = value
        for o, p in enumerate(peers):
            pltpu.make_async_remote_copy(
                src_ref=buf.at[mine], dst_ref=buf.at[mine], send_sem=s_sem.at[o],
                recv_sem=r_sem.at[mine], device_id=p, device_id_type=MESH).start()
        for o, p in enumerate(peers):
            src = (mine + o + 1) % n
            pltpu.make_async_remote_copy(
                src_ref=buf.at[mine], dst_ref=buf.at[src], send_sem=s_sem.at[o],
                recv_sem=r_sem.at[src], device_id=p, device_id_type=MESH).wait_recv()
        total = buf[0]
        for q in range(1, n):
            total = total + buf[q]
        return total

    part = phase(ga, zc, 8, a_peer, sa, ra, row)
    full = phase(gb, xy, 16, b_peer, sb, rb, part) * (1.0 / NODES)
    res = jnp.zeros((8, TILE), jnp.float32)
    sub = lax.broadcasted_iota(jnp.int32, (8, TILE), 0)
    full8 = jnp.broadcast_to(full, (8, TILE))
    for s in range(SCALES):
        v = pltpu.roll(full8, TILE - 16 * s, 1) if s else full8
        res = jnp.where(sub == s, v, res)
    en_ref[...] = res[:SCALES, :SIG]

    out_cp.wait()
    for src, dst, part, s_sem, r_sem in started:
        for d in range(8):
            @pl.when(have[d])
            def _(src=src, dst=dst, part=part, s_sem=s_sem, r_sem=r_sem, d=d):
                descriptor(src, dst, part, s_sem, r_sem, d, OPP[d], part(*DIRS[d])).wait_send()
    for o, p in enumerate(a_peer):
        pltpu.make_async_remote_copy(
            src_ref=ga.at[zc], dst_ref=ga.at[zc], send_sem=sa.at[o], recv_sem=ra.at[zc],
            device_id=p, device_id_type=MESH).wait_send()
    for o, p in enumerate(b_peer):
        pltpu.make_async_remote_copy(
            src_ref=gb.at[xy], dst_ref=gb.at[xy], send_sem=sb.at[o], recv_sem=rb.at[xy],
            device_id=p, device_id_type=MESH).wait_send()


def shards(signals, tiles, tile_dir, tile_mask, live_rows, bound_rows, scale_coeffs, spectral_bound):
    bf, f32 = jnp.bfloat16, jnp.float32
    vm = pltpu.VMEM
    smem = pl.BlockSpec(memory_space=pltpu.SMEM)
    hbm = pl.BlockSpec(memory_space=pl.ANY)
    dma = pltpu.SemaphoreType.DMA
    out, energy = pl.pallas_call(
        kernel,
        out_shape=(jax.ShapeDtypeStruct((SCALES, NB, SIG, TILE), f32),
                   jax.ShapeDtypeStruct((SCALES, SIG), f32)),
        in_specs=[hbm, hbm] + [smem] * 6,
        out_specs=(hbm, pl.BlockSpec(memory_space=pltpu.VMEM)),
        scratch_shapes=[
            vm((BX, BY, SIG, TILE), f32), vm((NB, SLOTS, TILE, TILE), bf),
            pltpu.SMEM((NB * SLOTS,), jnp.int32), pltpu.SMEM((NB * SLOTS,), jnp.int32),
            vm((NX, 32, TILE), bf), vm((NX, SIG, TILE), bf), vm((NX, SIG, TILE), bf), vm((NX, SIG, TILE), bf),
            vm((DEG, NB, SIG, TILE), f32), vm((SCALES, NB, SIG, TILE), f32), vm((NB, 8, TILE), f32),
            vm((3, 2, 32, TILE), bf), vm((3, 2, SIG, TILE), bf),
            vm((2, 3, SIG, TILE), bf), vm((2, 3, SIG, TILE), bf), vm((2, 10, 32, TILE), bf),
            vm((8, 3, 2, 32, TILE), bf), vm((8, 3, 2, SIG, TILE), bf),
            vm((8, 2, 3, SIG, TILE), bf), vm((8, 2, 3, SIG, TILE), bf), vm((8, 2, 10, 32, TILE), bf),
            vm((8, 1, TILE), f32), vm((16, 1, TILE), f32),
            dma((NB + 1,)), dma((2, 8)), dma((2, 8)), dma((2, 8)), dma((2, 8)), dma((8,)), dma((8,)),
            dma((7,)), dma((8,)), dma((15,)), dma((16,)), dma,
        ],
        compiler_params=pltpu.CompilerParams(collective_id=0, has_side_effects=True),
        name="wavelet",
    )(signals, tiles, jnp.swapaxes(tile_dir, 1, 2), jnp.swapaxes(tile_mask, 1, 2), live_rows, bound_rows,
      scale_coeffs, spectral_bound.reshape(1, 1))
    return out.reshape(SCALES, BX, BY, SIG, TILE), energy


def solution(mesh):
    torus = Mesh(mesh.devices.reshape(4, 4, 2, mesh.shape["gy"]), ("gx_0", "gx_1", "gx_2", "gy"))
    gxs = ("gx_0", "gx_1", "gx_2")
    placed = (
        P(gxs, "gy", None, None),
        P(gxs, "gy", None, None, None),
        P(gxs, "gy", None),
        P(gxs, "gy", None),
        P(gxs, "gy"),
        P(gxs, "gy"),
        P(),
        P(),
    )
    return jax.shard_map(
        shards,
        mesh=torus,
        in_specs=placed,
        out_specs=(P(None, gxs, "gy", None, None), P()),
        check_vma=False,
    )
```

time: 41.4 us -> 36 us (0.87)
  Pallas kernels: 36.3 us -> 31 us
    pallas_call x1, Pallas kernels: 36.3 us -> 31 us  [shards(): pl.pallas_call(kernel, out_shape=(jax.ShapeDtypeStruct((SCALES, NB, SIG,...]
where the time goes in v2:
time: 36 us; the launch traced here: 35.6 us
  Pallas kernels  31 us (86%)
  local copies, waits for them, and re-layouts  3.33 us (9%)
  between operations  1.29 us (4%)
    pallas_call x1, Pallas kernels, shards(): pl.pallas_call(kernel, out_shape=(jax.ShapeDtypeStruct((SCALES, NB, SIG,...  31 us
    unnamed x2, local copies, waits for them, and re-layouts  3.33 us

profile of v2, /device:TPU:1, one launch (start us, length us, event | category | flops | bytes accessed | tf_op | source)
XLA Modules:
  0.0 35.6 jit_solution(6746586214435423575)
XLA Ops:
  1.3 31.0 %wavelet.1 = (f32[6,16,16,128]{3,2,1,0:T(8,128)}, f32[6,16]{1,0:T(8,128)}) custom-call(f32[2,8,16,128]{3,2,1,0:T(8,128)} %sig_h.1, bf16[2,8,4,128,128]{4,3,2,1,0:T(8,128)(2,1)} %til_h.1, s32[2,4,8]{2,1,0:T(4,128)} %bitcast.6, s32[2,4,8]{2,1,0:T(4,128)} %bitcast.7, s32[2,8]{1,0:T(2,128)} %liv_s.1, s32[2,8]{1,0:T(2,128)} %bnd_s.1, f32[6,5]{1,0:T(8,128)} %cof_s.1, ...), custom_call_target="tpu_custom_call" | custom-call | tf_op jit(solution)/shard_map/wavelet/pallas_call | solution.py:426
  32.3 2.1 %copy.13 = f32[6,2,8,16,128]{4,3,2,1,0:T(8,128)} copy(f32[6,2,8,16,128]{4,3,2,1,0:T(8,128)} %bitcast.5) | data formatting | bytes 1572864
  34.3 1.3 %copy.14 = f32[6,16]{1,0:T(8,128)} copy(f32[6,16]{1,0:T(8,128)} %get-tuple-element.9) | data formatting | bytes 768

commit v3 on v2

--- a/solution.py
+++ b/solution.py
@@ -24,21 +24,20 @@
     return (gx // 8, (gx // 2) % 4, gx % 2, gy)
 
 
-def kernel(sig_h, til_h, dir_s, msk_s, liv_s, bnd_s, cof_s, spb_s,
-           out_h, en_ref,
-           sig, til, idx, loc, x1, x2, x3, x4, cheb, tot, amul, op1, op3, sp1, sp3, tp,
+def kernel(sig_h, til_h, dir_h, msk_h, liv_h, bnd_h, cof_h, spb_h,
+           tot, en_ref,
+           dir_s, msk_s, liv_s, bnd_s, cof_s, spb_s, sig, til, idx, loc, x1, x2, x3, x4, cheb, amul, op1, op3, sp1, sp3, tp,
            rv1, rv3, rs1, rs3, tr, ga, gb,
-           ld_sem, vs, vr, ss, sr, ts, tr_sem, sa, ra, sb, rb, o_sem):
+           ld_sem, vs, vr, ss, sr, ts, tr_sem, sa, ra, sb, rb):
     x, y, c, z = (lax.axis_index(a) for a in ("gx_0", "gx_1", "gx_2", "gy"))
     gx = (x * 4 + y) * 2 + c
     gy = z
-    sig_cp = pltpu.make_async_copy(sig_h, sig, ld_sem.at[NB])
-    sig_cp.start()
-    til_cp = []
-    for b in range(NB):
-        cp = pltpu.make_async_copy(til_h.at[b // BY, b % BY], til.at[b], ld_sem.at[b])
+    early = []
+    for n, (src, dst) in enumerate(((sig_h, sig), (liv_h, liv_s), (bnd_h, bnd_s), (dir_h, dir_s), (msk_h, msk_s),
+                                    (cof_h, cof_s), (spb_h, spb_s))):
+        cp = pltpu.make_async_copy(src, dst, ld_sem.at[n])
         cp.start()
-        til_cp.append(cp)
+        early.append(cp)
 
     def exists(d):
         dx, dy = DIRS[d]
@@ -63,10 +62,8 @@
         t = (xy + o) % 16
         b_peer.append((t // 4, t % 4, c, z))
 
-    for buf in (rv1, rv3, rs1, rs3, tr):
-        buf[...] = jnp.zeros_like(buf)
     bar = pltpu.get_barrier_semaphore()
-    for d in range(8):
+    for d in (4, 5, 6, 7, 0, 1, 2, 3):
         @pl.when(have[d])
         def _(d=d):
             pl.semaphore_signal(bar, inc=1, device_id=peer[d], device_id_type=MESH)
@@ -75,12 +72,135 @@
     count = jnp.int32(22)
     for d in range(8):
         count = count + have[d].astype(jnp.int32)
+    til_cp = []
+    for n in range(4):
+        cp = pltpu.make_async_copy(til_h.at[n // 2, pl.ds(4 * (n % 2), 4)], til.at[pl.ds(4 * n, 4)], ld_sem.at[7 + n])
+        cp.start()
+        til_cp.append(cp)
+    for cp in early:
+        cp.wait()
 
     lane = lax.broadcasted_iota(jnp.int32, (1, TILE), 1)
     low = lane < 32
-    f = 2.0 / spb_s[0, 0]
+    f = 2.0 / spb_s[0]
     bf16 = lambda a: a.astype(jnp.bfloat16)
     f32 = lambda a: a.astype(jnp.float32)
+
+    def live_of(b):
+        return (lane < liv_s[b // BY, b % BY]).astype(jnp.float32)
+
+    def edge_of(b):
+        return (lane < bnd_s[b // BY, b % BY]).astype(jnp.float32)
+
+    RING = [(r, q) for r in (1, 4) for q in range(1, 11)] + [(r, q) for r in (2, 3) for q in (1, 10)]
+    slot_of = lambda er, ec: NB + (er - 1) * (BY + 2) + ec - 1
+    def shift(v, q):
+        q = q % 4
+        return pltpu.roll(v, 32 * q, 1) if q else v
+
+    def add_to(packs, i, j, v):
+        key = (i, (j + 2) // 4)
+        v = shift(v, j + 2)
+        packs[key] = v if key not in packs else packs[key] + v
+
+    def place(b, v, xb, packs=None):
+        i, j = b // BY, b % BY
+        xb[b] = bf16(v)
+        e = v * edge_of(b)
+        xb[slot_of(i + 2, j + 2)] = bf16(e)
+        if packs is not None:
+            add_to(packs, i, j, e)
+
+    def flush(packs, buf, tile_first):
+        for (i, t), v in packs.items():
+            if tile_first:
+                buf[t, i] = bf16(v)
+            else:
+                buf[i, t] = v
+
+    def part_v(dx, dy):
+        return ({-1: pl.ds(0, 1), 1: pl.ds(2, 1), 0: pl.ds(0, 3)}[dy],)
+
+    def part_s(dx, dy):
+        return ({-1: pl.ds(0, 1), 1: pl.ds(1, 1), 0: pl.ds(0, 2)}[dx],
+                {-1: pl.ds(0, 1), 1: pl.ds(2, 1), 0: pl.ds(0, 3)}[dy])
+
+    def part_t(dx, dy):
+        return ({-1: pl.ds(0, 1), 1: pl.ds(1, 1), 0: pl.ds(0, 2)}[dx],
+                {-1: pl.ds(0, 2), 1: pl.ds(8, 2), 0: pl.ds(0, 10)}[dy])
+
+    def descriptor(src, dst, part, s_sem, r_sem, d, o, at):
+        return pltpu.make_async_remote_copy(
+            src_ref=src.at[at], dst_ref=dst.at[(o,) + at], send_sem=s_sem.at[d],
+            recv_sem=r_sem.at[o], device_id=peer[d], device_id_type=MESH)
+
+    started = []
+
+    def send(src, dst, part, s_sem, r_sem):
+        started.append((src, dst, part, s_sem, r_sem))
+        for d in (4, 5, 6, 7, 0, 1, 2, 3):
+            @pl.when(have[d])
+            def _(d=d):
+                descriptor(src, dst, part, s_sem, r_sem, d, OPP[d], part(*DIRS[d])).start()
+
+    def wait_recv(src, dst, part, s_sem, r_sem):
+        for d in range(8):
+            @pl.when(have[d])
+            def _(d=d):
+                descriptor(src, dst, part, s_sem, r_sem, d, d, part(*DIRS[OPP[d]])).wait_recv()
+
+    v_args = ((op1, rv1, part_v, vs.at[0], vr.at[0]), (op3, rv3, part_v, vs.at[1], vr.at[1]))
+    s_args = ((sp1, rs1, part_s, ss.at[0], sr.at[0]), (sp3, rs3, part_s, ss.at[1], sr.at[1]))
+    t_args = (tp, tr, part_t, ts, tr_sem)
+    U, D, L, R, UL, UR, DL, DR = range(8)
+    left = lane < 64
+
+    def rows_of(op, rv):
+        rows = []
+        for r in range(6):
+            i = r % 2
+            if r in (2, 3):
+                lo, hi, mine = rv[L, 2, i], rv[R, 0, i], [op[t, i] for t in range(3)]
+            else:
+                u, ul, ur = (U, UL, UR) if r < 2 else (D, DL, DR)
+                lo, hi, mine = rv[ul, 2, i], rv[ur, 0, i], [rv[u, t, i] for t in range(3)]
+            mine = [f32(v) for v in mine]
+            rows.append([jnp.where(left, f32(lo), mine[0]), mine[1], jnp.where(left, mine[2], f32(hi))])
+        return rows
+
+    def unpack(rows, xb):
+        for er, ec in RING:
+            v = jnp.where(low, shift(rows[er][ec // 4], -ec), 0.0)
+            xb[slot_of(er, ec)] = bf16(v)
+
+    def contract(lhs, rhs):
+        return lax.dot_general(lhs, rhs, (((1,), (1,)), ((), ())), preferred_element_type=jnp.float32)
+
+    def product(b, xb, table, rows=TILE):
+        acc = None
+        for h in range(2):
+            pick = [xb[table[b * SLOTS + 2 * h + n]] for n in range(2)]
+            rhs = [til[b, 2 * h + n, :rows] for n in range(2)]
+            p = contract(jnp.concatenate(pick, axis=1), jnp.concatenate(rhs, axis=1))
+            acc = p if acc is None else acc + p
+        return acc
+
+    packs = {}
+    pad = lax.broadcasted_iota(jnp.int32, (16, TILE), 0) == 0
+    for b in range(NB):
+        live = live_of(b)
+        v = sig[b // BY, b % BY] * live
+        cheb[0, b] = v
+        place(b, jnp.concatenate([v, jnp.where(pad, live, 0.0)], axis=0), x1, packs)
+    flush(packs, op1, True)
+    pl.semaphore_wait(bar, count)
+    send(*v_args[0])
+
+    for d in range(8):
+        @pl.when(jnp.logical_not(have[d]))
+        def _(d=d):
+            for buf in (rv1, rv3, rs1, rs3, tr):
+                buf[d] = jnp.zeros(buf.shape[1:], buf.dtype)
 
     for b in range(NB):
         i, j = b // BY, b % BY
@@ -97,120 +217,12 @@
                 away = jnp.logical_or(away, q == (0 if j == 0 else 2))
             loc[b * SLOTS + s] = jnp.where(away, ZERO, off)
 
-    def live_of(b):
-        return (lane < liv_s[b // BY, b % BY]).astype(jnp.float32)
-
-    def edge_of(b):
-        return (lane < bnd_s[b // BY, b % BY]).astype(jnp.float32)
-
-    RING = [(r, q) for r in (1, 4) for q in range(1, 11)] + [(r, q) for r in (2, 3) for q in (1, 10)]
-    slot_of = lambda er, ec: NB + (er - 1) * (BY + 2) + ec - 1
     for xb in (x1, x2, x3, x4):
         xb[ZERO] = jnp.zeros(xb.shape[1:], xb.dtype)
     for xb in (x2, x4):
         for er, ec in RING:
             xb[slot_of(er, ec)] = jnp.zeros(xb.shape[1:], xb.dtype)
 
-    def shift(v, q):
-        q = q % 4
-        return pltpu.roll(v, 32 * q, 1) if q else v
-
-    def add_to(packs, i, j, v):
-        key = (i, (j + 2) // 4)
-        v = shift(v, j + 2)
-        packs[key] = v if key not in packs else packs[key] + v
-
-    def place(b, v, xb, packs=None):
-        i, j = b // BY, b % BY
-        xb[b] = bf16(v)
-        e = v * edge_of(b)
-        xb[slot_of(i + 2, j + 2)] = bf16(e)
-        if packs is not None:
-            add_to(packs, i, j, e)
-
-    def flush(packs, buf, tile_first):
-        for (i, t), v in packs.items():
-            if tile_first:
-                buf[t, i] = bf16(v)
-            else:
-                buf[i, t] = bf16(v)
-
-    def part_v(dx, dy):
-        return ({-1: pl.ds(0, 1), 1: pl.ds(2, 1), 0: pl.ds(0, 3)}[dy],)
-
-    def part_s(dx, dy):
-        return ({-1: pl.ds(0, 1), 1: pl.ds(1, 1), 0: pl.ds(0, 2)}[dx],
-                {-1: pl.ds(0, 1), 1: pl.ds(2, 1), 0: pl.ds(0, 3)}[dy])
-
-    def part_t(dx, dy):
-        return ({-1: pl.ds(0, 1), 1: pl.ds(1, 1), 0: pl.ds(0, 2)}[dx],
-                {-1: pl.ds(0, 2), 1: pl.ds(8, 2), 0: pl.ds(0, 10)}[dy])
-
-    def descriptor(src, dst, part, s_sem, r_sem, d, o, at):
-        return pltpu.make_async_remote_copy(
-            src_ref=src.at[at], dst_ref=dst.at[(o,) + at], send_sem=s_sem.at[d],
-            recv_sem=r_sem.at[o], device_id=peer[d], device_id_type=MESH)
-
-    started = []
-
-    def send(src, dst, part, s_sem, r_sem):
-        started.append((src, dst, part, s_sem, r_sem))
-        for d in (4, 5, 6, 7, 0, 1, 2, 3):
-            @pl.when(have[d])
-            def _(d=d):
-                descriptor(src, dst, part, s_sem, r_sem, d, OPP[d], part(*DIRS[d])).start()
-
-    def wait_recv(src, dst, part, s_sem, r_sem):
-        for d in range(8):
-            @pl.when(have[d])
-            def _(d=d):
-                descriptor(src, dst, part, s_sem, r_sem, d, d, part(*DIRS[OPP[d]])).wait_recv()
-
-    v_args = ((op1, rv1, part_v, vs.at[0], vr.at[0]), (op3, rv3, part_v, vs.at[1], vr.at[1]))
-    s_args = ((sp1, rs1, part_s, ss.at[0], sr.at[0]), (sp3, rs3, part_s, ss.at[1], sr.at[1]))
-    t_args = (tp, tr, part_t, ts, tr_sem)
-    U, D, L, R, UL, UR, DL, DR = range(8)
-    left = lane < 64
-
-    def rows_of(op, rv):
-        rows = []
-        for r in range(6):
-            i = r % 2
-            if r in (2, 3):
-                lo, hi, mine = rv[L, 2, i], rv[R, 0, i], [op[t, i] for t in range(3)]
-            else:
-                u, ul, ur = (U, UL, UR) if r < 2 else (D, DL, DR)
-                lo, hi, mine = rv[ul, 2, i], rv[ur, 0, i], [rv[u, t, i] for t in range(3)]
-            mine = [f32(v) for v in mine]
-            rows.append([jnp.where(left, f32(lo), mine[0]), mine[1], jnp.where(left, mine[2], f32(hi))])
-        return rows
-
-    def unpack(rows, xb):
-        for er, ec in RING:
-            v = jnp.where(low, shift(rows[er][ec // 4], -ec), 0.0)
-            xb[slot_of(er, ec)] = bf16(v)
-
-    def contract(lhs, rhs):
-        return lax.dot_general(lhs, rhs, (((1,), (1,)), ((), ())), preferred_element_type=jnp.float32)
-
-    def product(b, xb, table, rows=TILE):
-        acc = None
-        for h in range(2):
-            pick = [xb[table[b * SLOTS + 2 * h + n]] for n in range(2)]
-            rhs = [til[b, 2 * h + n, :rows] for n in range(2)]
-            p = contract(jnp.concatenate(pick, axis=1), jnp.concatenate(rhs, axis=1))
-            acc = p if acc is None else acc + p
-        return acc
-
-    sig_cp.wait()
-    packs = {}
-    pad = lax.broadcasted_iota(jnp.int32, (16, TILE), 0) == 0
-    for b in range(NB):
-        live = live_of(b)
-        v = sig[b // BY, b % BY] * live
-        cheb[0, b] = v
-        place(b, jnp.concatenate([v, jnp.where(pad, live, 0.0)], axis=0), x1, packs)
-    flush(packs, op1, True)
 
     def corner(b, wanted):
         i, j = b // BY, b % BY
@@ -240,8 +252,9 @@
         add_to(packs, b // BY, b % BY, jnp.concatenate([out, jnp.zeros((SIG, TILE - 32), jnp.float32)], axis=1))
 
     packs = {}
-    for b in range(NB):
-        til_cp[b].wait()
+    for cp in til_cp:
+        cp.wait()
+    for b in range(NB):
         i, j = b // BY, b % BY
         dx = 2 * i
         tp[i, 1 + j] = corner(b, [(3 * dx + q, j + 1 + q) for q in range(3)])
@@ -252,8 +265,6 @@
         local_part(b, x1, f, None, 1, packs)
     flush(packs, sp1, False)
 
-    pl.semaphore_wait(bar, count)
-    send(*v_args[0])
     send(*s_args[0])
     send(*t_args)
 
@@ -297,7 +308,7 @@
                 lhs = jnp.concatenate([lhs, inputs[(base, col)]], axis=1)
                 rhs = jnp.concatenate([rhs, tr[owner, i, 0 if j == 0 else 9]], axis=1)
             acc = contract(lhs, rhs)
-            own = shift(f32(rs[owner, i, ((j + 2) // 4)]), -ec)[:, :32]
+            own = shift(rs[owner, i, (j + 2) // 4], -ec)[:, :32]
             if first:
                 v = shift(rows[er][ec // 4], -ec)[:SIG, :32]
                 new = own + f * (acc[SIG:SIG + 1] * v - acc[:SIG])
@@ -359,9 +370,6 @@
             t = tot[s, b] + cof_s[s, 3] * cheb[3, b] + cof_s[s, 4] * cur
             tot[s, b] = t
             sq[s] = t * t if sq[s] is None else sq[s] + t * t
-
-    out_cp = pltpu.make_async_copy(tot, out_h, o_sem)
-    out_cp.start()
 
     m = jnp.concatenate(sq, axis=0)
     hi = m.astype(jnp.bfloat16)
@@ -401,7 +409,6 @@
         res = jnp.where(sub == s, v, res)
     en_ref[...] = res[:SCALES, :SIG]
 
-    out_cp.wait()
     for src, dst, part, s_sem, r_sem in started:
         for d in range(8):
             @pl.when(have[d])
@@ -417,35 +424,53 @@
             device_id=p, device_id_type=MESH).wait_send()
 
 
+def finish(tot, en, out_h, en_h, sem):
+    a = pltpu.make_async_copy(tot, out_h, sem.at[0])
+    b = pltpu.make_async_copy(en, en_h, sem.at[1])
+    a.start()
+    b.start()
+    a.wait()
+    b.wait()
+
+
 def shards(signals, tiles, tile_dir, tile_mask, live_rows, bound_rows, scale_coeffs, spectral_bound):
-    bf, f32 = jnp.bfloat16, jnp.float32
-    vm = pltpu.VMEM
-    smem = pl.BlockSpec(memory_space=pltpu.SMEM)
+    bf, f32, i32 = jnp.bfloat16, jnp.float32, jnp.int32
+    vm, sm = pltpu.VMEM, pltpu.SMEM
+    in_vmem = pl.BlockSpec(memory_space=pltpu.VMEM)
     hbm = pl.BlockSpec(memory_space=pl.ANY)
     dma = pltpu.SemaphoreType.DMA
-    out, energy = pl.pallas_call(
+    tot, energy = pl.pallas_call(
         kernel,
-        out_shape=(jax.ShapeDtypeStruct((SCALES, NB, SIG, TILE), f32),
-                   jax.ShapeDtypeStruct((SCALES, SIG), f32)),
-        in_specs=[hbm, hbm] + [smem] * 6,
-        out_specs=(hbm, pl.BlockSpec(memory_space=pltpu.VMEM)),
+        out_shape=(pltpu.VMEM((SCALES, NB, SIG, TILE), f32), pltpu.VMEM((SCALES, SIG), f32)),
+        in_specs=[hbm] * 7 + [pl.BlockSpec(memory_space=pltpu.HBM)],
+        out_specs=(in_vmem, in_vmem),
         scratch_shapes=[
+            sm((BX, SLOTS, BY), i32), sm((BX, SLOTS, BY), i32), sm((BX, BY), i32), sm((BX, BY), i32),
+            sm((SCALES, DEG + 1), f32), sm((1,), f32),
             vm((BX, BY, SIG, TILE), f32), vm((NB, SLOTS, TILE, TILE), bf),
-            pltpu.SMEM((NB * SLOTS,), jnp.int32), pltpu.SMEM((NB * SLOTS,), jnp.int32),
+            sm((NB * SLOTS,), i32), sm((NB * SLOTS,), i32),
             vm((NX, 32, TILE), bf), vm((NX, SIG, TILE), bf), vm((NX, SIG, TILE), bf), vm((NX, SIG, TILE), bf),
-            vm((DEG, NB, SIG, TILE), f32), vm((SCALES, NB, SIG, TILE), f32), vm((NB, 8, TILE), f32),
+            vm((DEG, NB, SIG, TILE), f32), vm((NB, 8, TILE), f32),
             vm((3, 2, 32, TILE), bf), vm((3, 2, SIG, TILE), bf),
-            vm((2, 3, SIG, TILE), bf), vm((2, 3, SIG, TILE), bf), vm((2, 10, 32, TILE), bf),
+            vm((2, 3, SIG, TILE), f32), vm((2, 3, SIG, TILE), f32), vm((2, 10, 32, TILE), bf),
             vm((8, 3, 2, 32, TILE), bf), vm((8, 3, 2, SIG, TILE), bf),
-            vm((8, 2, 3, SIG, TILE), bf), vm((8, 2, 3, SIG, TILE), bf), vm((8, 2, 10, 32, TILE), bf),
+            vm((8, 2, 3, SIG, TILE), f32), vm((8, 2, 3, SIG, TILE), f32), vm((8, 2, 10, 32, TILE), bf),
             vm((8, 1, TILE), f32), vm((16, 1, TILE), f32),
-            dma((NB + 1,)), dma((2, 8)), dma((2, 8)), dma((2, 8)), dma((2, 8)), dma((8,)), dma((8,)),
-            dma((7,)), dma((8,)), dma((15,)), dma((16,)), dma,
+            dma((11,)), dma((2, 8)), dma((2, 8)), dma((2, 8)), dma((2, 8)), dma((8,)), dma((8,)),
+            dma((7,)), dma((8,)), dma((15,)), dma((16,)),
         ],
         compiler_params=pltpu.CompilerParams(collective_id=0, has_side_effects=True),
         name="wavelet",
     )(signals, tiles, jnp.swapaxes(tile_dir, 1, 2), jnp.swapaxes(tile_mask, 1, 2), live_rows, bound_rows,
-      scale_coeffs, spectral_bound.reshape(1, 1))
+      scale_coeffs, spectral_bound)
+    out, energy = pl.pallas_call(
+        finish,
+        out_shape=(jax.ShapeDtypeStruct((SCALES, NB, SIG, TILE), f32), jax.ShapeDtypeStruct((SCALES, SIG), f32)),
+        in_specs=[in_vmem, in_vmem],
+        out_specs=(hbm, hbm),
+        scratch_shapes=[dma((2,))],
+        name="finish",
+    )(pltpu.with_memory_space_constraint(tot, pltpu.VMEM), pltpu.with_memory_space_constraint(energy, pltpu.VMEM))
     return out.reshape(SCALES, BX, BY, SIG, TILE), energy
 
 

time: 36 us -> 31.3 us (0.87)
  local copies, waits for them, and re-layouts: 3.33 us -> 0 us
  Pallas kernels: 31 us -> 29.7 us
    unnamed x2 -> x0, local copies, waits for them, and re-layouts: 3.33 us -> none
    pallas_call x1 -> x2, Pallas kernels: 31 us -> 29.7 us  [the longest x1 28.8 us: shards(): pl.pallas_call(kernel, out_shape=(pltpu.VMEM((SCALES, NB, SIG, TILE), f32...]
where the time goes in v3:
time: 31.3 us; the launch traced here: 31 us
  Pallas kernels  29.7 us (95%)
  between operations  1.29 us (4%)
    pallas_call x1, Pallas kernels, shards(): pl.pallas_call(kernel, out_shape=(pltpu.VMEM((SCALES, NB, SIG, TILE), f32...  28.8 us
    pallas_call x1, Pallas kernels, shards(): pl.pallas_call(finish, out_shape=(jax.ShapeDtypeStruct((SCALES, NB, SIG,...  0.9 us

profile of v3, /device:TPU:1, one launch (start us, length us, event | category | flops | bytes accessed | tf_op | source)
XLA Modules:
  0.0 31.0 jit_solution(17485199064456771130)
XLA Ops:
  1.3 28.8 %wavelet.1 = (f32[6,16,16,128]{3,2,1,0:T(8,128)S(1)}, f32[6,16]{1,0:T(8,128)S(1)}) custom-call(f32[2,8,16,128]{3,2,1,0:T(8,128)} %sig_h.1, bf16[2,8,4,128,128]{4,3,2,1,0:T(8,128)(2,1)} %til_h.1, s32[2,4,8]{2,1,0:T(4,128)} %bitcast.3, s32[2,4,8]{2,1,0:T(4,128)} %bitcast.4, s32[2,8]{1,0:T(2,128)} %liv_h.1, s32[2,8]{1,0:T(2,128)} %bnd_h.1, f32[6,5]{1,0:T(8,128)} %cof_h.1, ...), custom_call_target="tpu_custom_call" | custom-call | tf_op jit(solution)/shard_map/wavelet/pallas_call | solution.py:442
  30.1 0.9 %finish.1 = (f32[6,16,16,128]{3,2,1,0:T(8,128)}, f32[6,16]{1,0:T(8,128)}) custom-call(f32[6,16,16,128]{3,2,1,0:T(8,128)S(1)} %get-tuple-element.6.tot, f32[6,16]{1,0:T(8,128)S(1)} %get-tuple-element.7.en), custom_call_target="tpu_custom_call" | custom-call | tf_op jit(solution)/shard_map/finish/pallas_call | solution.py:466

commit v4 on v3

--- a/solution.py
+++ b/solution.py
@@ -1,11 +1,8 @@
-import functools
-
 import jax
 import jax.numpy as jnp
 from jax import lax
 from jax.experimental import pallas as pl
 from jax.experimental.pallas import tpu as pltpu
-from jax.sharding import Mesh
 from jax.sharding import PartitionSpec as P
 
 MESH = pl.DeviceIdType.MESH
@@ -20,18 +17,22 @@
 OPP = [DIRS.index((-dx, -dy)) for dx, dy in DIRS]
 
 
-def coords(gx, gy):
-    return (gx // 8, (gx // 2) % 4, gx % 2, gy)
+def hops(o):
+    ring = (0, 1, 2, 1)
+    return ring[o & 3] + ring[o >> 3 & 3] + ring[o >> 5 & 3] + 0.1 * (o >> 2 & 1)
+
+
+DEVICES = 128
+FAR_FIRST = sorted(range(1, DEVICES), key=lambda o: (-hops(o), o))
 
 
 def kernel(sig_h, til_h, dir_h, msk_h, liv_h, bnd_h, cof_h, spb_h,
            tot, en_ref,
            dir_s, msk_s, liv_s, bnd_s, cof_s, spb_s, sig, til, idx, loc, x1, x2, x3, x4, cheb, amul, op1, op3, sp1, sp3, tp,
-           rv1, rv3, rs1, rs3, tr, ga, gb,
-           ld_sem, vs, vr, ss, sr, ts, tr_sem, sa, ra, sb, rb):
-    x, y, c, z = (lax.axis_index(a) for a in ("gx_0", "gx_1", "gx_2", "gy"))
-    gx = (x * 4 + y) * 2 + c
-    gy = z
+           rv1, rv3, rs1, rs3, tr, ga,
+           ld_sem, vs, vr, ss, sr, ts, tr_sem, sa, ra, in_y, in_xy):
+    gx, gy = lax.axis_index("gx"), lax.axis_index("gy")
+    me = gx * GYN + gy
     early = []
     for n, (src, dst) in enumerate(((sig_h, sig), (liv_h, liv_s), (bnd_h, bnd_s), (dir_h, dir_s), (msk_h, msk_s),
                                     (cof_h, cof_s), (spb_h, spb_s))):
@@ -50,26 +51,21 @@
         return ok
 
     have = [exists(d) for d in range(8)]
-    peer = [coords(gx + dx, gy + dy) for dx, dy in DIRS]
-    xy = x * 4 + y
-    zc = z * 2 + c
-    a_peer = []
-    for o in range(1, 8):
-        t = (zc + o) % 8
-        a_peer.append((x, y, t % 2, t // 2))
-    b_peer = []
-    for o in range(1, 16):
-        t = (xy + o) % 16
-        b_peer.append((t // 4, t % 4, c, z))
-
+    peer = [(gx + dx, gy + dy) for dx, dy in DIRS]
+    flip = lambda v: (v, v + 1 - 2 * (v % 2), (v + 2) % 4, 3 - v)
+    xs, ys, zs = flip(gx // 8), flip(gx // 2 % 4), flip(gy)
+    xyc = [8 * u + 2 * v + w for u in xs for v in ys for w in (gx % 2, 1 - gx % 2)]
+    other = lambda o: (xyc[(o >> 5) * 8 + (o >> 3) % 4 * 2 + (o >> 2) % 2], zs[o % 4])
+    rest = (1, 2, 3, 4, 5, 6, 7)
+    ring_y, ring_x = (8, 16, 24), (32, 64, 96)
     bar = pltpu.get_barrier_semaphore()
     for d in (4, 5, 6, 7, 0, 1, 2, 3):
         @pl.when(have[d])
         def _(d=d):
             pl.semaphore_signal(bar, inc=1, device_id=peer[d], device_id_type=MESH)
-    for p in a_peer + b_peer:
-        pl.semaphore_signal(bar, inc=1, device_id=p, device_id_type=MESH)
-    count = jnp.int32(22)
+    for o in ring_x + ring_y + rest:
+        pl.semaphore_signal(bar, inc=1, device_id=other(o), device_id_type=MESH)
+    count = jnp.int32(13)
     for d in range(8):
         count = count + have[d].astype(jnp.int32)
     til_cp = []
@@ -195,6 +191,8 @@
     flush(packs, op1, True)
     pl.semaphore_wait(bar, count)
     send(*v_args[0])
+    for o in ring_x:
+        pl.semaphore_signal(in_y, inc=1, device_id=other(o), device_id_type=MESH)
 
     for d in range(8):
         @pl.when(jnp.logical_not(have[d]))
@@ -317,6 +315,9 @@
             xn[slot_of(er, ec), :, pl.ds(0, 32)] = bf16(new)
 
     add_totals(0)
+    pl.semaphore_wait(in_y, 3)
+    for o in rest:
+        pl.semaphore_signal(in_xy, inc=1, device_id=other(o), device_id_type=MESH)
     wait_recv(*v_args[0])
     rows = rows_of(op1, rv1)
     unpack(rows, x1)
@@ -383,24 +384,19 @@
         row = p if row is None else row + p
     row = jnp.concatenate([row[0:1], jnp.zeros((1, TILE - SCALES * SIG), jnp.float32)], axis=1)
 
-    def phase(buf, mine, n, peers, s_sem, r_sem, value):
-        buf[mine] = value
-        for o, p in enumerate(peers):
-            pltpu.make_async_remote_copy(
-                src_ref=buf.at[mine], dst_ref=buf.at[mine], send_sem=s_sem.at[o],
-                recv_sem=r_sem.at[mine], device_id=p, device_id_type=MESH).start()
-        for o, p in enumerate(peers):
-            src = (mine + o + 1) % n
-            pltpu.make_async_remote_copy(
-                src_ref=buf.at[mine], dst_ref=buf.at[src], send_sem=s_sem.at[o],
-                recv_sem=r_sem.at[src], device_id=p, device_id_type=MESH).wait_recv()
-        total = buf[0]
-        for q in range(1, n):
-            total = total + buf[q]
-        return total
-
-    part = phase(ga, zc, 8, a_peer, sa, ra, row)
-    full = phase(gb, xy, 16, b_peer, sb, rb, part) * (1.0 / NODES)
+    ga[me] = row
+    pl.semaphore_wait(in_xy, 7)
+    for o in FAR_FIRST:
+        pltpu.make_async_remote_copy(
+            src_ref=ga.at[me], dst_ref=ga.at[me], send_sem=sa, recv_sem=ra,
+            device_id=other(o), device_id_type=MESH).start()
+    many = ga.at[pl.ds(0, DEVICES - 1)]
+    pltpu.make_async_remote_copy(
+        src_ref=many, dst_ref=many, send_sem=sa, recv_sem=ra, device_id=other(1), device_id_type=MESH).wait_recv()
+    sums = [ga[q] for q in range(DEVICES)]
+    while len(sums) > 1:
+        sums = [u + v for u, v in zip(sums[::2], sums[1::2])]
+    full = sums[0] * (1.0 / NODES)
     res = jnp.zeros((8, TILE), jnp.float32)
     sub = lax.broadcasted_iota(jnp.int32, (8, TILE), 0)
     full8 = jnp.broadcast_to(full, (8, TILE))
@@ -414,14 +410,8 @@
             @pl.when(have[d])
             def _(src=src, dst=dst, part=part, s_sem=s_sem, r_sem=r_sem, d=d):
                 descriptor(src, dst, part, s_sem, r_sem, d, OPP[d], part(*DIRS[d])).wait_send()
-    for o, p in enumerate(a_peer):
-        pltpu.make_async_remote_copy(
-            src_ref=ga.at[zc], dst_ref=ga.at[zc], send_sem=sa.at[o], recv_sem=ra.at[zc],
-            device_id=p, device_id_type=MESH).wait_send()
-    for o, p in enumerate(b_peer):
-        pltpu.make_async_remote_copy(
-            src_ref=gb.at[xy], dst_ref=gb.at[xy], send_sem=sb.at[o], recv_sem=rb.at[xy],
-            device_id=p, device_id_type=MESH).wait_send()
+    pltpu.make_async_remote_copy(
+        src_ref=many, dst_ref=many, send_sem=sa, recv_sem=ra, device_id=other(1), device_id_type=MESH).wait_send()
 
 
 def finish(tot, en, out_h, en_h, sem):
@@ -455,9 +445,9 @@
             vm((2, 3, SIG, TILE), f32), vm((2, 3, SIG, TILE), f32), vm((2, 10, 32, TILE), bf),
             vm((8, 3, 2, 32, TILE), bf), vm((8, 3, 2, SIG, TILE), bf),
             vm((8, 2, 3, SIG, TILE), f32), vm((8, 2, 3, SIG, TILE), f32), vm((8, 2, 10, 32, TILE), bf),
-            vm((8, 1, TILE), f32), vm((16, 1, TILE), f32),
+            vm((DEVICES, 1, TILE), f32),
             dma((11,)), dma((2, 8)), dma((2, 8)), dma((2, 8)), dma((2, 8)), dma((8,)), dma((8,)),
-            dma((7,)), dma((8,)), dma((15,)), dma((16,)),
+            dma, dma, pltpu.SemaphoreType.REGULAR, pltpu.SemaphoreType.REGULAR,
         ],
         compiler_params=pltpu.CompilerParams(collective_id=0, has_side_effects=True),
         name="wavelet",
@@ -475,22 +465,20 @@
 
 
 def solution(mesh):
-    torus = Mesh(mesh.devices.reshape(4, 4, 2, mesh.shape["gy"]), ("gx_0", "gx_1", "gx_2", "gy"))
-    gxs = ("gx_0", "gx_1", "gx_2")
     placed = (
-        P(gxs, "gy", None, None),
-        P(gxs, "gy", None, None, None),
-        P(gxs, "gy", None),
-        P(gxs, "gy", None),
-        P(gxs, "gy"),
-        P(gxs, "gy"),
+        P("gx", "gy", None, None),
+        P("gx", "gy", None, None, None),
+        P("gx", "gy", None),
+        P("gx", "gy", None),
+        P("gx", "gy"),
+        P("gx", "gy"),
         P(),
         P(),
     )
     return jax.shard_map(
         shards,
-        mesh=torus,
+        mesh=mesh,
         in_specs=placed,
-        out_specs=(P(None, gxs, "gy", None, None), P()),
+        out_specs=(P(None, "gx", "gy", None, None), P()),
         check_vma=False,
     )

time: 31.3 us -> 28.7 us (0.917)
  Pallas kernels: 29.7 us -> 27.3 us
    pallas_call x1, Pallas kernels: 28.8 us -> 26.4 us  [shards(): pl.pallas_call(kernel, out_shape=(pltpu.VMEM((SCALES, NB, SIG, TILE), f32...]
where the time goes in v4:
time: 28.7 us; the launch traced here: 28.6 us
  Pallas kernels  27.3 us (95%)
  between operations  1.29 us (4%)
    pallas_call x1, Pallas kernels, shards(): pl.pallas_call(kernel, out_shape=(pltpu.VMEM((SCALES, NB, SIG, TILE), f32...  26.4 us
    pallas_call x1, Pallas kernels, shards(): pl.pallas_call(finish, out_shape=(jax.ShapeDtypeStruct((SCALES, NB, SIG,...  0.9 us

profile of v4, /device:TPU:1, one launch (start us, length us, event | category | flops | bytes accessed | tf_op | source)
XLA Modules:
  0.0 28.6 jit_solution(11357297664297855302)
XLA Ops:
  1.3 26.4 %wavelet.1 = (f32[6,16,16,128]{3,2,1,0:T(8,128)S(1)}, f32[6,16]{1,0:T(8,128)S(1)}) custom-call(f32[2,8,16,128]{3,2,1,0:T(8,128)} %sig_h.1, bf16[2,8,4,128,128]{4,3,2,1,0:T(8,128)(2,1)} %til_h.1, s32[2,4,8]{2,1,0:T(4,128)} %bitcast.3, s32[2,4,8]{2,1,0:T(4,128)} %bitcast.4, s32[2,8]{1,0:T(2,128)} %liv_h.1, s32[2,8]{1,0:T(2,128)} %bnd_h.1, f32[6,5]{1,0:T(8,128)} %cof_h.1, ...), custom_call_target="tpu_custom_call" | custom-call | tf_op jit(solution)/shard_map/wavelet/pallas_call | solution.py:432
  27.7 0.9 %finish.1 = (f32[6,16,16,128]{3,2,1,0:T(8,128)}, f32[6,16]{1,0:T(8,128)}) custom-call(f32[6,16,16,128]{3,2,1,0:T(8,128)S(1)} %get-tuple-element.6.tot, f32[6,16]{1,0:T(8,128)S(1)} %get-tuple-element.7.en), custom_call_target="tpu_custom_call" | custom-call | tf_op jit(solution)/shard_map/finish/pallas_call | solution.py:456

commit v5 on v4

v5 whole, which is shorter than its diff:
```python
import jax
import jax.numpy as jnp
from jax import lax
from jax.experimental import pallas as pl
from jax.experimental.pallas import tpu as pltpu
from jax.sharding import PartitionSpec as P

MESH = pl.DeviceIdType.MESH
SIG, SCALES, DEG, SLOTS, TILE = 16, 6, 4, 4, 128
BX, BY = 2, 8
NB = BX * BY
GXN, GYN = 32, 4
ZERO = 2 * NB
NX = ZERO + 1
NODES = 64 * 32 * 128
DIRS = [(-1, 0), (1, 0), (0, -1), (0, 1), (-1, -1), (-1, 1), (1, -1), (1, 1)]
OPP = [DIRS.index((-dx, -dy)) for dx, dy in DIRS]


def hops(o):
    ring = (0, 1, 2, 1)
    return ring[o & 3] + ring[o >> 3 & 3] + ring[o >> 5 & 3] + 0.1 * (o >> 2 & 1)


DEVICES = 128
FAR_FIRST = sorted(range(1, DEVICES), key=lambda o: (-hops(o), o))


def kernel(sig_h, til_h, dir_h, msk_h, liv_h, bnd_h, cof_h, spb_h,
           tot, en_ref,
           dir_s, msk_s, liv_s, bnd_s, cof_s, spb_s, sig, til, loc, x1, x2, x3, x4, cheb, base, amul, dloc,
           pw, qw, op1, op3, eg, sp1, sp3, tp, rv1, rv3, re, rs1, rs3, tr, ga,
           ld_sem, vs, vr, es, er_sem, ss, sr, ts, tr_sem, sa, ra, in_y, in_xy):
    gx, gy = lax.axis_index("gx"), lax.axis_index("gy")
    me = gx * GYN + gy
    early = []
    for n, (src, dst) in enumerate(((sig_h, sig), (liv_h, liv_s), (bnd_h, bnd_s), (dir_h, dir_s), (msk_h, msk_s),
                                    (cof_h, cof_s), (spb_h, spb_s))):
        cp = pltpu.make_async_copy(src, dst, ld_sem.at[n])
        cp.start()
        early.append(cp)

    def exists(d):
        dx, dy = DIRS[d]
        ok = None
        for step, pos, n in ((dx, gx, GXN), (dy, gy, GYN)):
            if step == 0:
                continue
            this = pos > 0 if step < 0 else pos < n - 1
            ok = this if ok is None else jnp.logical_and(ok, this)
        return ok

    have = [exists(d) for d in range(8)]
    peer = [(gx + dx, gy + dy) for dx, dy in DIRS]
    flip = lambda v: (v, v + 1 - 2 * (v % 2), (v + 2) % 4, 3 - v)
    xs, ys, zs = flip(gx // 8), flip(gx // 2 % 4), flip(gy)
    xyc = [8 * u + 2 * v + w for u in xs for v in ys for w in (gx % 2, 1 - gx % 2)]
    other = lambda o: (xyc[(o >> 5) * 8 + (o >> 3) % 4 * 2 + (o >> 2) % 2], zs[o % 4])
    rest = (1, 2, 3, 4, 5, 6, 7)
    ring_y, ring_x = (8, 16, 24), (32, 64, 96)
    bar = pltpu.get_barrier_semaphore()
    for d in (4, 5, 6, 7, 0, 1, 2, 3):
        @pl.when(have[d])
        def _(d=d):
            pl.semaphore_signal(bar, inc=1, device_id=peer[d], device_id_type=MESH)
    for o in ring_x + ring_y + rest:
        pl.semaphore_signal(bar, inc=1, device_id=other(o), device_id_type=MESH)
    count = jnp.int32(13)
    for d in range(8):
        count = count + have[d].astype(jnp.int32)
    til_cp = []
    for n in range(4):
        cp = pltpu.make_async_copy(til_h.at[n // 2, pl.ds(4 * (n % 2), 4)], til.at[pl.ds(4 * n, 4)], ld_sem.at[7 + n])
        cp.start()
        til_cp.append(cp)
    for cp in early:
        cp.wait()

    lane = lax.broadcasted_iota(jnp.int32, (1, TILE), 1)
    low, high, left = lane < 32, lane >= 96, lane < 64
    middle = jnp.logical_and(lane >= 32, lane < 96)
    f = 2.0 / spb_s[0]
    bf16 = lambda a: a.astype(jnp.bfloat16)
    f32 = lambda a: a.astype(jnp.float32)
    for xb in (x1, x2, x3, x4):
        xb[ZERO] = jnp.zeros(xb.shape[1:], xb.dtype)

    def live_of(b):
        return (lane < liv_s[b // BY, b % BY]).astype(jnp.float32)

    def edge_of(b):
        return (lane < bnd_s[b // BY, b % BY]).astype(jnp.float32)

    def shift(v, q):
        q = q % 4
        return pltpu.roll(v, 32 * q, 1) if q else v

    def add_to(packs, i, j, v):
        key = (i, (j + 2) // 4)
        v = shift(v, j + 2)
        packs[key] = v if key not in packs else packs[key] + v

    def place(b, v, xb, packs=None):
        xb[b] = bf16(v)
        e = v * edge_of(b)
        xb[NB + b] = bf16(e)
        if packs is not None:
            add_to(packs, b // BY, b % BY, e[:SIG])

    def part_v(dx, dy):
        return ({-1: pl.ds(0, 1), 1: pl.ds(2, 1), 0: pl.ds(0, 3)}[dy],)

    def part_s(dx, dy):
        return ({-1: pl.ds(0, 1), 1: pl.ds(1, 1), 0: pl.ds(0, 2)}[dx],
                {-1: pl.ds(0, 1), 1: pl.ds(2, 1), 0: pl.ds(0, 3)}[dy])

    def part_t(dx, dy):
        return ({-1: pl.ds(0, 1), 1: pl.ds(1, 1), 0: pl.ds(0, 2)}[dx],
                {-1: pl.ds(0, 2), 1: pl.ds(8, 2), 0: pl.ds(0, 10)}[dy])

    def descriptor(src, dst, part, s_sem, r_sem, d, o, at):
        return pltpu.make_async_remote_copy(
            src_ref=src.at[at], dst_ref=dst.at[(o,) + at], send_sem=s_sem.at[d],
            recv_sem=r_sem.at[o], device_id=peer[d], device_id_type=MESH)

    started = []

    def send(*messages):
        started.extend(messages)
        for d in (4, 5, 6, 7, 0, 1, 2, 3):
            @pl.when(have[d])
            def _(d=d):
                for src, dst, part, s_sem, r_sem in messages:
                    descriptor(src, dst, part, s_sem, r_sem, d, OPP[d], part(*DIRS[d])).start()

    def wait_recv(*messages):
        for d in range(8):
            @pl.when(have[d])
            def _(d=d):
                for src, dst, part, s_sem, r_sem in messages:
                    descriptor(src, dst, part, s_sem, r_sem, d, d, part(*DIRS[OPP[d]])).wait_recv()

    v_args = ((op1, rv1, part_v, vs.at[0], vr.at[0]), (op3, rv3, part_v, vs.at[1], vr.at[1]))
    e_args = (eg, re, part_v, es, er_sem)
    s_args = ((sp1, rs1, part_s, ss.at[0], sr.at[0]), (sp3, rs3, part_s, ss.at[1], sr.at[1]))
    t_args = (tp, tr, part_t, ts, tr_sem)
    U, D, L, R, UL, UR, DL, DR = range(8)

    def contract(lhs, rhs):
        return lax.dot_general(lhs, rhs, (((1,), (1,)), ((), ())), preferred_element_type=jnp.float32)

    packs, epacks = {}, {}
    top = lax.broadcasted_iota(jnp.int32, (16, TILE), 0) == 0
    for b in range(NB):
        live = live_of(b)
        v = sig[b // BY, b % BY] * live
        cheb[0, b] = v
        place(b, jnp.concatenate([v, jnp.where(top, live, 0.0)], axis=0), x1, packs)
        add_to(epacks, b // BY, b % BY, edge_of(b))
    for (i, t), v in packs.items():
        op1[t, i] = bf16(v)
    for (i, t), v in epacks.items():
        eg[t, i] = v

    for b in range(NB):
        i, j = b // BY, b % BY
        for s in range(SLOTS):
            d = dir_s[i, s, j]
            r = (d * 11) >> 5
            q = d - 3 * r
            off = jnp.where(d == 4, b, NB + (i + r - 1) * BY + j + q - 1)
            off = jnp.where(msk_s[i, s, j] == 1, off, ZERO)
            away = r == 2 * i
            if j in (0, BY - 1):
                away = jnp.logical_or(away, q == (0 if j == 0 else 2))
            loc[b * SLOTS + s] = jnp.where(away, ZERO, off)

    def sorted_rows(b, wanted, first):
        i, j = b // BY, b % BY
        total = None
        tiles = [f32(til[b, s, pl.ds(first, 32)]) for s in range(SLOTS)]
        for d, group in wanted:
            acc = None
            for s in range(SLOTS):
                on = jnp.logical_and(dir_s[i, s, j] == d, msk_s[i, s, j] == 1).astype(jnp.float32)
                t = tiles[s] * on
                acc = t if acc is None else acc + t
            acc = shift(jnp.where(low, acc, 0.0), group)
            total = acc if total is None else total + acc
        return total

    def directions(b):
        i, j = b // BY, b % BY
        yield None, [(6 * i + q, j + 1 + q) for q in range(3)]
        if j == 0:
            yield 0, [(3 - 3 * i, 1), (6 - 3 * i, 0)]
        if j == BY - 1:
            yield 1, [(5 - 3 * i, 2), (8 - 3 * i, 3)]

    def sort_tiles(first):
        for b in range(NB):
            i, j = b // BY, b % BY
            for side, wanted in directions(b):
                rows = sorted_rows(b, wanted, first)
                kept = bf16(rows)
                if side is None:
                    pw[b, pl.ds(first, 32)] = kept
                else:
                    qw[i, side, pl.ds(first, 32)] = kept
                if first == 0:
                    inside = lax.broadcasted_iota(jnp.int32, (32, TILE), 0) < bnd_s[i, j]
                    tp[i, 1 + j if side is None else 9 * side] = bf16(jnp.where(inside, rows, 0.0))

    def own_product(b, xb):
        acc = None
        for h in range(2):
            pick = [xb[loc[b * SLOTS + 2 * h + n]] for n in range(2)]
            rhs = [til[b, 2 * h + n] for n in range(2)]
            p = contract(jnp.concatenate(pick, axis=1), jnp.concatenate(rhs, axis=1))
            acc = p if acc is None else acc + p
        return acc

    def own_part(k, xb, sp=None):
        packs = {}
        for b in range(NB):
            acc = own_product(b, xb)
            fl = f * live_of(b)
            if k == 0:
                deg = fl * acc[SIG:SIG + 1]
                dloc[b] = jnp.broadcast_to(deg, (8, TILE))
                out = (deg - 1.0) * cheb[0, b] - fl * acc[:SIG]
            else:
                am = amul[b]
                out = jnp.concatenate([am, am], axis=0) * cheb[k, b] - (2.0 * fl) * acc - cheb[k - 1, b]
            base[b] = out
            if sp is not None:
                add_to(packs, b // BY, b % BY, out * edge_of(b))
        for (i, t), v in packs.items():
            sp[i, t] = v

    for cp in til_cp:
        cp.wait()
    sort_tiles(0)
    own_part(0, x1, sp1)
    pl.semaphore_wait(bar, count)
    send(v_args[0], e_args, s_args[0])
    send(t_args)
    for o in ring_x:
        pl.semaphore_signal(in_y, inc=1, device_id=other(o), device_id_type=MESH)

    for d in range(8):
        @pl.when(jnp.logical_not(have[d]))
        def _(d=d):
            for buf in (rv1, rv3, re, rs1, rs3, tr):
                buf[d] = jnp.zeros(buf.shape[1:], buf.dtype)

    for first in (32, 64, 96):
        sort_tiles(first)

    def add_totals(k):
        for s in range(SCALES):
            a = cof_s[s, k] * 0.5 if k == 0 else cof_s[s, k]
            for b in range(NB):
                t = a * cheb[k, b]
                tot[s, b] = t if k == 0 else tot[s, b] + t

    def rows_of(op, rv):
        rows = []
        for r in range(6):
            i = r % 2
            if r in (2, 3):
                lo, hi, mine = rv[L, 2, i], rv[R, 0, i], [op[t, i] for t in range(3)]
            else:
                u, ul, ur = (U, UL, UR) if r < 2 else (D, DL, DR)
                lo, hi, mine = rv[ul, 2, i], rv[ur, 0, i], [rv[u, t, i] for t in range(3)]
            mine = [f32(v) for v in mine]
            rows.append([jnp.where(left, f32(lo), mine[0]), mine[1], jnp.where(left, mine[2], f32(hi))])
        return rows

    def with_edges(rows, edges):
        return [[jnp.concatenate([v, jnp.where(top, e, 0.0)], axis=0) for v, e in zip(r, q)]
                for r, q in zip(rows, edges)]

    class Inputs:
        def __init__(self, rows):
            self.rows, self.made = rows, {}

        def get(self, key, make):
            if key not in self.made:
                self.made[key] = bf16(make())
            return self.made[key]

        def plain(self, r, t):
            return self.get(("p", r, t), lambda: self.rows[r][t])

        def row(self, r, c):
            t, q, rows = c // 4, c % 4, self.rows[r]
            if q == 0:
                return self.get(("a", r, t), lambda: jnp.where(high, rows[t - 1], rows[t]))
            if q == 3:
                return self.get(("b", r, t), lambda: jnp.where(low, rows[t + 1], rows[t]))
            return self.plain(r, t)

        def crossing(self, r, t):
            rows = self.rows[r]
            before = rows[t - 1] if t > 0 else jnp.zeros_like(rows[t])
            after = rows[t + 1] if t < 2 else jnp.zeros_like(rows[t])
            return self.get(("x", r, t), lambda: jnp.where(left, after, before))

        def column(self, r, t):
            one, two = self.rows[r][t], self.rows[r + 1][t]
            return self.get(("c", r, t), lambda: jnp.where(
                middle, one, jnp.where(left, shift(two, -1), shift(two, 1))))

    def away_product(b, ins):
        i, j = b // BY, b % BY
        lhs, rhs = ins.row(1 if i == 0 else 4, j + 2), pw[b]
        if j in (0, BY - 1):
            side = 0 if j == 0 else 1
            lhs = jnp.concatenate([lhs, ins.column(2, 2 * side)], axis=1)
            rhs = jnp.concatenate([rhs, qw[i, side]], axis=1)
        return contract(lhs, rhs)

    r_iota = lax.broadcasted_iota(jnp.int32, (TILE, TILE), 0)
    c_iota = lax.broadcasted_iota(jnp.int32, (TILE, TILE), 1)
    across = jnp.logical_or(jnp.logical_and(r_iota < 32, c_iota >= 96), jnp.logical_and(r_iota >= 96, c_iota < 32))

    def advance_ring(rows, ins, rs, first):
        none = jnp.zeros((32, TILE), jnp.bfloat16)
        zero = jnp.zeros((TILE, TILE), jnp.float32)

        def update(own, lhs, rhs, v):
            acc = contract(jnp.concatenate(lhs, axis=1), jnp.concatenate(rhs, axis=1))
            if first:
                return own + f * (acc[SIG:SIG + 1] * v[:SIG] - acc[:SIG])
            return own - (2.0 * f) * acc

        new = [[None] * 3 for _ in range(6)]
        for er, u, ul, ur in ((1, U, UL, UR), (4, D, DL, DR)):
            i = 1 if er == 1 else 0
            feed = er + 1 if i else er - 1
            edge = er - i
            for t in range(3):
                if t == 1:
                    w = [tr[u, i, 3 + n] for n in range(4)]
                    own, wq = rs[u, i, 1], None
                elif t == 0:
                    w = [none, tr[ul, i, 8], tr[u, i, 1], tr[u, i, 2]]
                    wq = [none, tr[ul, i, 9], tr[u, i, 0], none]
                    own = jnp.where(left, rs[ul, i, 2], rs[u, i, 0])
                else:
                    w = [tr[u, i, 7], tr[u, i, 8], tr[ur, i, 1], none]
                    wq = [none, tr[u, i, 9], tr[ur, i, 0], none]
                    own = jnp.where(left, rs[u, i, 2], rs[ur, i, 0])
                w = f32(jnp.concatenate(w, axis=0))
                lhs = [ins.plain(feed, t), ins.crossing(feed, t)]
                rhs = [bf16(jnp.where(across, zero, w)), bf16(jnp.where(across, w, zero))]
                if wq is not None:
                    lhs.append(ins.column(edge, t))
                    rhs.append(jnp.concatenate(wq, axis=0))
                new[er][t] = update(own, lhs, rhs, rows[er][t])
        for er, i in ((2, 0), (3, 1)):
            feed = er - 1 if i == 0 else er + 1
            for t, o, p, q in ((0, L, 8, 9), (2, R, 1, 0)):
                at = 1 if t == 0 else 2
                pad = lambda w: jnp.concatenate([none] * at + [w] + [none] * (3 - at), axis=0)
                new[er][t] = update(rs[o, i, 2 - t], [ins.plain(feed, t), ins.column(2, t)],
                                    [pad(tr[o, i, p]), pad(tr[o, i, q])], rows[er][t])
        return new

    add_totals(0)
    pl.semaphore_wait(in_y, 3)
    for o in rest:
        pl.semaphore_signal(in_xy, inc=1, device_id=other(o), device_id_type=MESH)

    wait_recv(v_args[0], e_args)
    rows = with_edges(rows_of(op1, rv1), rows_of(eg, re))
    ins = Inputs(rows)
    for b in range(NB):
        acc = away_product(b, ins)
        fl = f * live_of(b)
        deg = fl * acc[SIG:SIG + 1]
        amul[b] = 2.0 * (dloc[b] + jnp.broadcast_to(deg, (8, TILE)) - 1.0)
        cur = base[b] + deg * cheb[0, b] - fl * acc[:SIG]
        cheb[1, b] = cur
        place(b, cur, x2)
    own_part(1, x2)
    wait_recv(s_args[0], t_args)
    ring = Inputs(advance_ring(rows, ins, rs1, 1))

    packs = {}
    for b in range(NB):
        cur = base[b] - (2.0 * f * live_of(b)) * away_product(b, ring)
        cheb[2, b] = cur
        place(b, cur, x3, packs)
    for (i, t), v in packs.items():
        op3[t, i] = bf16(v)
    send(v_args[1])
    own_part(2, x3, sp3)
    send(s_args[1])
    add_totals(1)
    add_totals(2)

    wait_recv(v_args[1])
    rows = rows_of(op3, rv3)
    ins = Inputs(rows)
    for b in range(NB):
        cur = base[b] - (2.0 * f * live_of(b)) * away_product(b, ins)
        cheb[3, b] = cur
        place(b, cur, x4)
    own_part(3, x4)
    wait_recv(s_args[1])
    ring = Inputs(advance_ring(rows, ins, rs3, 0))
    sq = [None] * SCALES
    for b in range(NB):
        cur = base[b] - (2.0 * f * live_of(b)) * away_product(b, ring)
        for s in range(SCALES):
            t = tot[s, b] + cof_s[s, 3] * cheb[3, b] + cof_s[s, 4] * cur
            tot[s, b] = t
            sq[s] = t * t if sq[s] is None else sq[s] + t * t

    m = jnp.concatenate(sq, axis=0)
    hi = m.astype(jnp.bfloat16)
    r1 = m - hi.astype(jnp.float32)
    mid = r1.astype(jnp.bfloat16)
    lo = (r1 - mid.astype(jnp.float32)).astype(jnp.bfloat16)
    ones = jnp.ones((16, TILE), jnp.bfloat16)
    row = None
    for part in (lo, mid, hi):
        p = lax.dot_general(ones, part, (((1,), (1,)), ((), ())), preferred_element_type=jnp.float32)
        row = p if row is None else row + p
    row = jnp.concatenate([row[0:1], jnp.zeros((1, TILE - SCALES * SIG), jnp.float32)], axis=1)

    ga[me] = row
    pl.semaphore_wait(in_xy, 7)
    for o in FAR_FIRST:
        pltpu.make_async_remote_copy(
            src_ref=ga.at[me], dst_ref=ga.at[me], send_sem=sa, recv_sem=ra,
            device_id=other(o), device_id_type=MESH).start()
    many = ga.at[pl.ds(0, DEVICES - 1)]
    pltpu.make_async_remote_copy(
        src_ref=many, dst_ref=many, send_sem=sa, recv_sem=ra, device_id=other(1), device_id_type=MESH).wait_recv()
    sums = [ga[q] for q in range(DEVICES)]
    while len(sums) > 1:
        sums = [u + v for u, v in zip(sums[::2], sums[1::2])]
    full = sums[0] * (1.0 / NODES)
    res = jnp.zeros((8, TILE), jnp.float32)
    sub = lax.broadcasted_iota(jnp.int32, (8, TILE), 0)
    full8 = jnp.broadcast_to(full, (8, TILE))
    for s in range(SCALES):
        v = pltpu.roll(full8, TILE - 16 * s, 1) if s else full8
        res = jnp.where(sub == s, v, res)
    en_ref[...] = res[:SCALES, :SIG]

    for src, dst, part, s_sem, r_sem in started:
        for d in range(8):
            @pl.when(have[d])
            def _(src=src, dst=dst, part=part, s_sem=s_sem, r_sem=r_sem, d=d):
                descriptor(src, dst, part, s_sem, r_sem, d, OPP[d], part(*DIRS[d])).wait_send()
    pltpu.make_async_remote_copy(
        src_ref=many, dst_ref=many, send_sem=sa, recv_sem=ra, device_id=other(1), device_id_type=MESH).wait_send()


def finish(tot, en, out_h, en_h, sem):
    a = pltpu.make_async_copy(tot, out_h, sem.at[0])
    b = pltpu.make_async_copy(en, en_h, sem.at[1])
    a.start()
    b.start()
    a.wait()
    b.wait()


def shards(signals, tiles, tile_dir, tile_mask, live_rows, bound_rows, scale_coeffs, spectral_bound):
    bf, f32, i32 = jnp.bfloat16, jnp.float32, jnp.int32
    vm, sm = pltpu.VMEM, pltpu.SMEM
    in_vmem = pl.BlockSpec(memory_space=pltpu.VMEM)
    hbm = pl.BlockSpec(memory_space=pl.ANY)
    dma = pltpu.SemaphoreType.DMA
    tot, energy = pl.pallas_call(
        kernel,
        out_shape=(pltpu.VMEM((SCALES, NB, SIG, TILE), f32), pltpu.VMEM((SCALES, SIG), f32)),
        in_specs=[hbm] * 7 + [pl.BlockSpec(memory_space=pltpu.HBM)],
        out_specs=(in_vmem, in_vmem),
        scratch_shapes=[
            sm((BX, SLOTS, BY), i32), sm((BX, SLOTS, BY), i32), sm((BX, BY), i32), sm((BX, BY), i32),
            sm((SCALES, DEG + 1), f32), sm((1,), f32),
            vm((BX, BY, SIG, TILE), f32), vm((NB, SLOTS, TILE, TILE), bf),
            sm((NB * SLOTS,), i32),
            vm((NX, 32, TILE), bf), vm((NX, SIG, TILE), bf), vm((NX, SIG, TILE), bf), vm((NX, SIG, TILE), bf),
            vm((DEG, NB, SIG, TILE), f32), vm((NB, SIG, TILE), f32), vm((NB, 8, TILE), f32), vm((NB, 8, TILE), f32),
            vm((NB, TILE, TILE), bf), vm((BX, 2, TILE, TILE), bf),
            vm((3, 2, SIG, TILE), bf), vm((3, 2, SIG, TILE), bf), vm((3, 2, 1, TILE), f32),
            vm((2, 3, SIG, TILE), f32), vm((2, 3, SIG, TILE), f32), vm((2, 10, 32, TILE), bf),
            vm((8, 3, 2, SIG, TILE), bf), vm((8, 3, 2, SIG, TILE), bf), vm((8, 3, 2, 1, TILE), f32),
            vm((8, 2, 3, SIG, TILE), f32), vm((8, 2, 3, SIG, TILE), f32), vm((8, 2, 10, 32, TILE), bf),
            vm((DEVICES, 1, TILE), f32),
            dma((11,)), dma((2, 8)), dma((2, 8)), dma((8,)), dma((8,)), dma((2, 8)), dma((2, 8)), dma((8,)), dma((8,)),
            dma, dma, pltpu.SemaphoreType.REGULAR, pltpu.SemaphoreType.REGULAR,
        ],
        compiler_params=pltpu.CompilerParams(collective_id=0, has_side_effects=True),
        name="wavelet",
    )(signals, tiles, jnp.swapaxes(tile_dir, 1, 2), jnp.swapaxes(tile_mask, 1, 2), live_rows, bound_rows,
      scale_coeffs, spectral_bound)
    out, energy = pl.pallas_call(
        finish,
        out_shape=(jax.ShapeDtypeStruct((SCALES, NB, SIG, TILE), f32), jax.ShapeDtypeStruct((SCALES, SIG), f32)),
        in_specs=[in_vmem, in_vmem],
        out_specs=(hbm, hbm),
        scratch_shapes=[dma((2,))],
        name="finish",
    )(pltpu.with_memory_space_constraint(tot, pltpu.VMEM), pltpu.with_memory_space_constraint(energy, pltpu.VMEM))
    return out.reshape(SCALES, BX, BY, SIG, TILE), energy


def solution(mesh):
    placed = (
        P("gx", "gy", None, None),
        P("gx", "gy", None, None, None),
        P("gx", "gy", None),
        P("gx", "gy", None),
        P("gx", "gy"),
        P("gx", "gy"),
        P(),
        P(),
    )
    return jax.shard_map(
        shards,
        mesh=mesh,
        in_specs=placed,
        out_specs=(P(None, "gx", "gy", None, None), P()),
        check_vma=False,
    )
```

time: 28.7 us -> 28.9 us (level)
  no operation moved by 1% of the time
where the time goes in v5:
time: 28.9 us; the launch traced here: 28.8 us
  Pallas kernels  27.5 us (95%)
  between operations  1.29 us (4%)
    pallas_call x1, Pallas kernels, shards(): pl.pallas_call(kernel, out_shape=(pltpu.VMEM((SCALES, NB, SIG, TILE), f32...  26.6 us
    pallas_call x1, Pallas kernels, shards(): pl.pallas_call(finish, out_shape=(jax.ShapeDtypeStruct((SCALES, NB, SIG,...  0.9 us

profile of v5, /device:TPU:1, one launch (start us, length us, event | category | flops | bytes accessed | tf_op | source)
XLA Modules:
  0.0 28.8 jit_solution(12727402582605811044)
XLA Ops:
  1.3 26.6 %wavelet.1 = (f32[6,16,16,128]{3,2,1,0:T(8,128)S(1)}, f32[6,16]{1,0:T(8,128)S(1)}) custom-call(f32[2,8,16,128]{3,2,1,0:T(8,128)} %sig_h.1, bf16[2,8,4,128,128]{4,3,2,1,0:T(8,128)(2,1)} %til_h.1, s32[2,4,8]{2,1,0:T(4,128)} %bitcast.3, s32[2,4,8]{2,1,0:T(4,128)} %bitcast.4, s32[2,8]{1,0:T(2,128)} %liv_h.1, s32[2,8]{1,0:T(2,128)} %bnd_h.1, f32[6,5]{1,0:T(8,128)} %cof_h.1, ...), custom_call_target="tpu_custom_call" | custom-call | tf_op jit(solution)/shard_map/wavelet/pallas_call | solution.py:479
  27.9 0.9 %finish.1 = (f32[6,16,16,128]{3,2,1,0:T(8,128)}, f32[6,16]{1,0:T(8,128)}) custom-call(f32[6,16,16,128]{3,2,1,0:T(8,128)S(1)} %get-tuple-element.6.tot, f32[6,16]{1,0:T(8,128)S(1)} %get-tuple-element.7.en), custom_call_target="tpu_custom_call" | custom-call | tf_op jit(solution)/shard_map/finish/pallas_call | solution.py:504

commit v6 on v5

--- a/solution.py
+++ b/solution.py
@@ -1,3 +1,6 @@
+import functools
+import operator
+
 import jax
 import jax.numpy as jnp
 from jax import lax
@@ -10,7 +13,7 @@
 BX, BY = 2, 8
 NB = BX * BY
 GXN, GYN = 32, 4
-ZERO = 2 * NB
+ZERO = NB + (BX + 2) * (BY + 2)
 NX = ZERO + 1
 NODES = 64 * 32 * 128
 DIRS = [(-1, 0), (1, 0), (0, -1), (0, 1), (-1, -1), (-1, 1), (1, -1), (1, 1)]
@@ -28,15 +31,15 @@
 
 def kernel(sig_h, til_h, dir_h, msk_h, liv_h, bnd_h, cof_h, spb_h,
            tot, en_ref,
-           dir_s, msk_s, liv_s, bnd_s, cof_s, spb_s, sig, til, loc, x1, x2, x3, x4, cheb, base, amul, dloc,
-           pw, qw, op1, op3, eg, sp1, sp3, tp, rv1, rv3, re, rs1, rs3, tr, ga,
-           ld_sem, vs, vr, es, er_sem, ss, sr, ts, tr_sem, sa, ra, in_y, in_xy):
+           dir_s, msk_s, liv_s, bnd_s, cof_s, spb_s, sig, til, idx, loc, x1, x2, x3, x4, cheb, amul,
+           op1, op3, eg, sp1, sp3, tp, rv1, rv3, re, rs1, rs3, tr, ga, units,
+           ld, r1, w1, r3, r4, w3, sa, ra, in_y, in_xy):
     gx, gy = lax.axis_index("gx"), lax.axis_index("gy")
     me = gx * GYN + gy
     early = []
     for n, (src, dst) in enumerate(((sig_h, sig), (liv_h, liv_s), (bnd_h, bnd_s), (dir_h, dir_s), (msk_h, msk_s),
                                     (cof_h, cof_s), (spb_h, spb_s))):
-        cp = pltpu.make_async_copy(src, dst, ld_sem.at[n])
+        cp = pltpu.make_async_copy(src, dst, ld.at[n])
         cp.start()
         early.append(cp)
 
@@ -70,7 +73,7 @@
         count = count + have[d].astype(jnp.int32)
     til_cp = []
     for n in range(4):
-        cp = pltpu.make_async_copy(til_h.at[n // 2, pl.ds(4 * (n % 2), 4)], til.at[pl.ds(4 * n, 4)], ld_sem.at[7 + n])
+        cp = pltpu.make_async_copy(til_h.at[n // 2, pl.ds(4 * (n % 2), 4)], til.at[pl.ds(4 * n, 4)], ld.at[7 + n])
         cp.start()
         til_cp.append(cp)
     for cp in early:
@@ -100,10 +103,13 @@
         v = shift(v, j + 2)
         packs[key] = v if key not in packs else packs[key] + v
 
+    RING = [(r, q) for r in (1, 4) for q in range(1, 11)] + [(r, q) for r in (2, 3) for q in (1, 10)]
+    slot_of = lambda er, ec: NB + (er - 1) * (BY + 2) + ec - 1
+
     def place(b, v, xb, packs=None):
         xb[b] = bf16(v)
         e = v * edge_of(b)
-        xb[NB + b] = bf16(e)
+        xb[slot_of(b // BY + 2, b % BY + 2)] = bf16(e)
         if packs is not None:
             add_to(packs, b // BY, b % BY, e[:SIG])
 
@@ -120,30 +126,44 @@
 
     def descriptor(src, dst, part, s_sem, r_sem, d, o, at):
         return pltpu.make_async_remote_copy(
-            src_ref=src.at[at], dst_ref=dst.at[(o,) + at], send_sem=s_sem.at[d],
-            recv_sem=r_sem.at[o], device_id=peer[d], device_id_type=MESH)
-
-    started = []
+            src_ref=src.at[at], dst_ref=dst.at[(o,) + at], send_sem=s_sem, recv_sem=r_sem,
+            device_id=peer[d], device_id_type=MESH)
 
     def send(*messages):
-        started.extend(messages)
         for d in (4, 5, 6, 7, 0, 1, 2, 3):
             @pl.when(have[d])
             def _(d=d):
                 for src, dst, part, s_sem, r_sem in messages:
                     descriptor(src, dst, part, s_sem, r_sem, d, OPP[d], part(*DIRS[d])).start()
 
-    def wait_recv(*messages):
-        for d in range(8):
-            @pl.when(have[d])
-            def _(d=d):
-                for src, dst, part, s_sem, r_sem in messages:
-                    descriptor(src, dst, part, s_sem, r_sem, d, d, part(*DIRS[OPP[d]])).wait_recv()
-
-    v_args = ((op1, rv1, part_v, vs.at[0], vr.at[0]), (op3, rv3, part_v, vs.at[1], vr.at[1]))
-    e_args = (eg, re, part_v, es, er_sem)
-    s_args = ((sp1, rs1, part_s, ss.at[0], sr.at[0]), (sp3, rs3, part_s, ss.at[1], sr.at[1]))
-    t_args = (tp, tr, part_t, ts, tr_sem)
+    inner_x = jnp.logical_and(gx > 0, gx < GXN - 1)
+    inner_y = jnp.logical_and(gy > 0, gy < GYN - 1)
+
+    def wait_all(sent, *messages):
+        def size(d):
+            n = 0
+            for src, _, part, _, _ in messages:
+                at = part(*DIRS[d])
+                shape = [p.size for p in at] + list(src.shape[len(at):])
+                n += src.dtype.itemsize * functools.reduce(operator.mul, shape) // 512
+            return n
+
+        _, _, _, s_sem, r_sem = messages[0]
+        for nx in (1, 2):
+            for ny in (1, 2):
+                n = nx * size(0) + ny * size(2) + nx * ny * size(4)
+                this = jnp.logical_and(inner_x == (nx == 2), inner_y == (ny == 2))
+
+                @pl.when(this)
+                def _(n=n):
+                    ref = units.at[pl.ds(0, n)]
+                    cp = pltpu.make_async_remote_copy(
+                        src_ref=ref, dst_ref=ref, send_sem=s_sem, recv_sem=r_sem,
+                        device_id=other(1), device_id_type=MESH)
+                    cp.wait_send() if sent else cp.wait_recv()
+
+    first = ((op1, rv1, part_v, w1, r1), (eg, re, part_v, w1, r1), (sp1, rs1, part_s, w1, r1), (tp, tr, part_t, w1, r1))
+    v3, s3 = (op3, rv3, part_v, w3, r3), (sp3, rs3, part_s, w3, r4)
     U, D, L, R, UL, UR, DL, DR = range(8)
 
     def contract(lhs, rhs):
@@ -168,17 +188,18 @@
             d = dir_s[i, s, j]
             r = (d * 11) >> 5
             q = d - 3 * r
-            off = jnp.where(d == 4, b, NB + (i + r - 1) * BY + j + q - 1)
+            off = jnp.where(d == 4, b, NB + (i + r) * (BY + 2) + (j + q))
             off = jnp.where(msk_s[i, s, j] == 1, off, ZERO)
+            idx[b * SLOTS + s] = off
             away = r == 2 * i
             if j in (0, BY - 1):
                 away = jnp.logical_or(away, q == (0 if j == 0 else 2))
             loc[b * SLOTS + s] = jnp.where(away, ZERO, off)
 
-    def sorted_rows(b, wanted, first):
+    def sorted_rows(b, wanted):
         i, j = b // BY, b % BY
         total = None
-        tiles = [f32(til[b, s, pl.ds(first, 32)]) for s in range(SLOTS)]
+        tiles = [f32(til[b, s, pl.ds(0, 32)]) for s in range(SLOTS)]
         for d, group in wanted:
             acc = None
             for s in range(SLOTS):
@@ -187,7 +208,8 @@
                 acc = t if acc is None else acc + t
             acc = shift(jnp.where(low, acc, 0.0), group)
             total = acc if total is None else total + acc
-        return total
+        inside = lax.broadcasted_iota(jnp.int32, (32, TILE), 0) < bnd_s[i, j]
+        return bf16(jnp.where(inside, total, 0.0))
 
     def directions(b):
         i, j = b // BY, b % BY
@@ -197,54 +219,38 @@
         if j == BY - 1:
             yield 1, [(5 - 3 * i, 2), (8 - 3 * i, 3)]
 
-    def sort_tiles(first):
-        for b in range(NB):
-            i, j = b // BY, b % BY
-            for side, wanted in directions(b):
-                rows = sorted_rows(b, wanted, first)
-                kept = bf16(rows)
-                if side is None:
-                    pw[b, pl.ds(first, 32)] = kept
-                else:
-                    qw[i, side, pl.ds(first, 32)] = kept
-                if first == 0:
-                    inside = lax.broadcasted_iota(jnp.int32, (32, TILE), 0) < bnd_s[i, j]
-                    tp[i, 1 + j if side is None else 9 * side] = bf16(jnp.where(inside, rows, 0.0))
-
-    def own_product(b, xb):
+    def product(b, xb, table, rows=TILE):
         acc = None
         for h in range(2):
-            pick = [xb[loc[b * SLOTS + 2 * h + n]] for n in range(2)]
-            rhs = [til[b, 2 * h + n] for n in range(2)]
+            pick = [xb[table[b * SLOTS + 2 * h + n]] for n in range(2)]
+            rhs = [til[b, 2 * h + n, :rows] for n in range(2)]
             p = contract(jnp.concatenate(pick, axis=1), jnp.concatenate(rhs, axis=1))
             acc = p if acc is None else acc + p
         return acc
 
-    def own_part(k, xb, sp=None):
+    def local_part(k, xb, sp):
         packs = {}
         for b in range(NB):
-            acc = own_product(b, xb)
-            fl = f * live_of(b)
+            acc = product(b, xb, loc, 32)
+            v = cheb[k, b, :, :32]
             if k == 0:
-                deg = fl * acc[SIG:SIG + 1]
-                dloc[b] = jnp.broadcast_to(deg, (8, TILE))
-                out = (deg - 1.0) * cheb[0, b] - fl * acc[:SIG]
+                out = (f * acc[SIG:SIG + 1] - 1.0) * v - f * acc[:SIG]
             else:
-                am = amul[b]
-                out = jnp.concatenate([am, am], axis=0) * cheb[k, b] - (2.0 * fl) * acc - cheb[k - 1, b]
-            base[b] = out
-            if sp is not None:
-                add_to(packs, b // BY, b % BY, out * edge_of(b))
+                out = amul[b, :1, :32] * v - (2.0 * f) * acc - cheb[k - 1, b, :, :32]
+            out = out * edge_of(b)[:, :32]
+            add_to(packs, b // BY, b % BY,
+                   jnp.concatenate([out, jnp.zeros((SIG, TILE - 32), jnp.float32)], axis=1))
         for (i, t), v in packs.items():
             sp[i, t] = v
 
     for cp in til_cp:
         cp.wait()
-    sort_tiles(0)
-    own_part(0, x1, sp1)
+    for b in range(NB):
+        for side, wanted in directions(b):
+            tp[b // BY, 1 + b % BY if side is None else 9 * side] = sorted_rows(b, wanted)
+    local_part(0, x1, sp1)
     pl.semaphore_wait(bar, count)
-    send(v_args[0], e_args, s_args[0])
-    send(t_args)
+    send(*first)
     for o in ring_x:
         pl.semaphore_signal(in_y, inc=1, device_id=other(o), device_id_type=MESH)
 
@@ -253,9 +259,6 @@
         def _(d=d):
             for buf in (rv1, rv3, re, rs1, rs3, tr):
                 buf[d] = jnp.zeros(buf.shape[1:], buf.dtype)
-
-    for first in (32, 64, 96):
-        sort_tiles(first)
 
     def add_totals(k):
         for s in range(SCALES):
@@ -312,20 +315,17 @@
             return self.get(("c", r, t), lambda: jnp.where(
                 middle, one, jnp.where(left, shift(two, -1), shift(two, 1))))
 
-    def away_product(b, ins):
-        i, j = b // BY, b % BY
-        lhs, rhs = ins.row(1 if i == 0 else 4, j + 2), pw[b]
-        if j in (0, BY - 1):
-            side = 0 if j == 0 else 1
-            lhs = jnp.concatenate([lhs, ins.column(2, 2 * side)], axis=1)
-            rhs = jnp.concatenate([rhs, qw[i, side]], axis=1)
-        return contract(lhs, rhs)
+    def unpack(rows, xb):
+        for er, ec in RING:
+            v = jnp.where(low, shift(rows[er][ec // 4], -ec), 0.0)
+            xb[slot_of(er, ec)] = bf16(v)
 
     r_iota = lax.broadcasted_iota(jnp.int32, (TILE, TILE), 0)
     c_iota = lax.broadcasted_iota(jnp.int32, (TILE, TILE), 1)
     across = jnp.logical_or(jnp.logical_and(r_iota < 32, c_iota >= 96), jnp.logical_and(r_iota >= 96, c_iota < 32))
 
-    def advance_ring(rows, ins, rs, first):
+    def advance_ring(rows, rs, first):
+        ins = Inputs(rows)
         none = jnp.zeros((32, TILE), jnp.bfloat16)
         zero = jnp.zeros((TILE, TILE), jnp.float32)
 
@@ -373,49 +373,55 @@
     for o in rest:
         pl.semaphore_signal(in_xy, inc=1, device_id=other(o), device_id_type=MESH)
 
-    wait_recv(v_args[0], e_args)
+    wait_all(False, *first)
     rows = with_edges(rows_of(op1, rv1), rows_of(eg, re))
-    ins = Inputs(rows)
-    for b in range(NB):
-        acc = away_product(b, ins)
+    unpack(rows, x1)
+    ring = advance_ring(rows, rs1, 1)
+    for b in range(NB):
+        acc = product(b, x1, idx)
         fl = f * live_of(b)
-        deg = fl * acc[SIG:SIG + 1]
-        amul[b] = 2.0 * (dloc[b] + jnp.broadcast_to(deg, (8, TILE)) - 1.0)
-        cur = base[b] + deg * cheb[0, b] - fl * acc[:SIG]
+        am = fl * acc[SIG:SIG + 1] - 1.0
+        amul[b] = jnp.broadcast_to(2.0 * am, (8, TILE))
+        cur = am * cheb[0, b] - fl * acc[:SIG]
         cheb[1, b] = cur
         place(b, cur, x2)
-    own_part(1, x2)
-    wait_recv(s_args[0], t_args)
-    ring = Inputs(advance_ring(rows, ins, rs1, 1))
+    unpack(ring, x2)
+
+    def step(b, k, xb):
+        acc = product(b, xb, idx)
+        am = amul[b]
+        am = jnp.concatenate([am, am], axis=0)
+        return am * cheb[k, b] - (2.0 * f * live_of(b)) * acc - cheb[k - 1, b]
 
     packs = {}
     for b in range(NB):
-        cur = base[b] - (2.0 * f * live_of(b)) * away_product(b, ring)
+        cur = step(b, 1, x2)
         cheb[2, b] = cur
         place(b, cur, x3, packs)
     for (i, t), v in packs.items():
         op3[t, i] = bf16(v)
-    send(v_args[1])
-    own_part(2, x3, sp3)
-    send(s_args[1])
+    send(v3)
+    local_part(2, x3, sp3)
+    send(s3)
     add_totals(1)
     add_totals(2)
-
-    wait_recv(v_args[1])
+    wait_all(True, *first)
+
+    wait_all(False, v3)
     rows = rows_of(op3, rv3)
-    ins = Inputs(rows)
-    for b in range(NB):
-        cur = base[b] - (2.0 * f * live_of(b)) * away_product(b, ins)
+    unpack(rows, x3)
+    for b in range(NB):
+        cur = step(b, 2, x3)
         cheb[3, b] = cur
         place(b, cur, x4)
-    own_part(3, x4)
-    wait_recv(s_args[1])
-    ring = Inputs(advance_ring(rows, ins, rs3, 0))
+    add_totals(3)
+    wait_all(False, s3)
+    unpack(advance_ring(rows, rs3, 0), x4)
     sq = [None] * SCALES
     for b in range(NB):
-        cur = base[b] - (2.0 * f * live_of(b)) * away_product(b, ring)
+        cur = step(b, 3, x4)
         for s in range(SCALES):
-            t = tot[s, b] + cof_s[s, 3] * cheb[3, b] + cof_s[s, 4] * cur
+            t = tot[s, b] + cof_s[s, 4] * cur
             tot[s, b] = t
             sq[s] = t * t if sq[s] is None else sq[s] + t * t
 
@@ -437,6 +443,7 @@
         pltpu.make_async_remote_copy(
             src_ref=ga.at[me], dst_ref=ga.at[me], send_sem=sa, recv_sem=ra,
             device_id=other(o), device_id_type=MESH).start()
+    wait_all(True, v3, s3)
     many = ga.at[pl.ds(0, DEVICES - 1)]
     pltpu.make_async_remote_copy(
         src_ref=many, dst_ref=many, send_sem=sa, recv_sem=ra, device_id=other(1), device_id_type=MESH).wait_recv()
@@ -452,11 +459,6 @@
         res = jnp.where(sub == s, v, res)
     en_ref[...] = res[:SCALES, :SIG]
 
-    for src, dst, part, s_sem, r_sem in started:
-        for d in range(8):
-            @pl.when(have[d])
-            def _(src=src, dst=dst, part=part, s_sem=s_sem, r_sem=r_sem, d=d):
-                descriptor(src, dst, part, s_sem, r_sem, d, OPP[d], part(*DIRS[d])).wait_send()
     pltpu.make_async_remote_copy(
         src_ref=many, dst_ref=many, send_sem=sa, recv_sem=ra, device_id=other(1), device_id_type=MESH).wait_send()
 
@@ -485,16 +487,15 @@
             sm((BX, SLOTS, BY), i32), sm((BX, SLOTS, BY), i32), sm((BX, BY), i32), sm((BX, BY), i32),
             sm((SCALES, DEG + 1), f32), sm((1,), f32),
             vm((BX, BY, SIG, TILE), f32), vm((NB, SLOTS, TILE, TILE), bf),
-            sm((NB * SLOTS,), i32),
+            sm((NB * SLOTS,), i32), sm((NB * SLOTS,), i32),
             vm((NX, 32, TILE), bf), vm((NX, SIG, TILE), bf), vm((NX, SIG, TILE), bf), vm((NX, SIG, TILE), bf),
-            vm((DEG, NB, SIG, TILE), f32), vm((NB, SIG, TILE), f32), vm((NB, 8, TILE), f32), vm((NB, 8, TILE), f32),
-            vm((NB, TILE, TILE), bf), vm((BX, 2, TILE, TILE), bf),
+            vm((DEG, NB, SIG, TILE), f32), vm((NB, 8, TILE), f32),
             vm((3, 2, SIG, TILE), bf), vm((3, 2, SIG, TILE), bf), vm((3, 2, 1, TILE), f32),
             vm((2, 3, SIG, TILE), f32), vm((2, 3, SIG, TILE), f32), vm((2, 10, 32, TILE), bf),
             vm((8, 3, 2, SIG, TILE), bf), vm((8, 3, 2, SIG, TILE), bf), vm((8, 3, 2, 1, TILE), f32),
             vm((8, 2, 3, SIG, TILE), f32), vm((8, 2, 3, SIG, TILE), f32), vm((8, 2, 10, 32, TILE), bf),
-            vm((DEVICES, 1, TILE), f32),
-            dma((11,)), dma((2, 8)), dma((2, 8)), dma((8,)), dma((8,)), dma((2, 8)), dma((2, 8)), dma((8,)), dma((8,)),
+            vm((DEVICES, 1, TILE), f32), vm((1024, 1, TILE), f32),
+            dma((11,)), dma, dma, dma, dma, dma,
             dma, dma, pltpu.SemaphoreType.REGULAR, pltpu.SemaphoreType.REGULAR,
         ],
         compiler_params=pltpu.CompilerParams(collective_id=0, has_side_effects=True),

time: 28.9 us -> 28.4 us (0.983)
  Pallas kernels: 27.5 us -> 26.9 us
    pallas_call x1, Pallas kernels: 26.6 us -> 26 us  [shards(): pl.pallas_call(kernel, out_shape=(pltpu.VMEM((SCALES, NB, SIG, TILE), f32...]
where the time goes in v6:
time: 28.4 us; the launch traced here: 28.2 us
  Pallas kernels  26.9 us (95%)
  between operations  1.29 us (5%)
    pallas_call x1, Pallas kernels, shards(): pl.pallas_call(kernel, out_shape=(pltpu.VMEM((SCALES, NB, SIG, TILE), f32...  26 us
    pallas_call x1, Pallas kernels, shards(): pl.pallas_call(finish, out_shape=(jax.ShapeDtypeStruct((SCALES, NB, SIG,...  0.9 us

profile of v6, /device:TPU:1, one launch (start us, length us, event | category | flops | bytes accessed | tf_op | source)
XLA Modules:
  0.0 28.2 jit_solution(9893303804673015928)
XLA Ops:
  1.3 26.0 %wavelet.1 = (f32[6,16,16,128]{3,2,1,0:T(8,128)S(1)}, f32[6,16]{1,0:T(8,128)S(1)}) custom-call(f32[2,8,16,128]{3,2,1,0:T(8,128)} %sig_h.1, bf16[2,8,4,128,128]{4,3,2,1,0:T(8,128)(2,1)} %til_h.1, s32[2,4,8]{2,1,0:T(4,128)} %bitcast.3, s32[2,4,8]{2,1,0:T(4,128)} %bitcast.4, s32[2,8]{1,0:T(2,128)} %liv_h.1, s32[2,8]{1,0:T(2,128)} %bnd_h.1, f32[6,5]{1,0:T(8,128)} %cof_h.1, ...), custom_call_target="tpu_custom_call" | custom-call | tf_op jit(solution)/shard_map/wavelet/pallas_call | solution.py:481
  27.3 0.9 %finish.1 = (f32[6,16,16,128]{3,2,1,0:T(8,128)}, f32[6,16]{1,0:T(8,128)}) custom-call(f32[6,16,16,128]{3,2,1,0:T(8,128)S(1)} %get-tuple-element.6.tot, f32[6,16]{1,0:T(8,128)S(1)} %get-tuple-element.7.en), custom_call_target="tpu_custom_call" | custom-call | tf_op jit(solution)/shard_map/finish/pallas_call | solution.py:505

commit v7 on v6

--- a/solution.py
+++ b/solution.py
@@ -33,7 +33,7 @@
            tot, en_ref,
            dir_s, msk_s, liv_s, bnd_s, cof_s, spb_s, sig, til, idx, loc, x1, x2, x3, x4, cheb, amul,
            op1, op3, eg, sp1, sp3, tp, rv1, rv3, re, rs1, rs3, tr, ga, units,
-           ld, r1, w1, r3, r4, w3, sa, ra, in_y, in_xy):
+           ld, r1, r2, w1, r3, r4, w3, sa, ra, in_y, in_xy):
     gx, gy = lax.axis_index("gx"), lax.axis_index("gy")
     me = gx * GYN + gy
     early = []
@@ -162,7 +162,7 @@
                         device_id=other(1), device_id_type=MESH)
                     cp.wait_send() if sent else cp.wait_recv()
 
-    first = ((op1, rv1, part_v, w1, r1), (eg, re, part_v, w1, r1), (sp1, rs1, part_s, w1, r1), (tp, tr, part_t, w1, r1))
+    first = ((op1, rv1, part_v, w1, r1), (eg, re, part_v, w1, r1), (sp1, rs1, part_s, w1, r2), (tp, tr, part_t, w1, r2))
     v3, s3 = (op3, rv3, part_v, w3, r3), (sp3, rs3, part_s, w3, r4)
     U, D, L, R, UL, UR, DL, DR = range(8)
 
@@ -250,7 +250,8 @@
             tp[b // BY, 1 + b % BY if side is None else 9 * side] = sorted_rows(b, wanted)
     local_part(0, x1, sp1)
     pl.semaphore_wait(bar, count)
-    send(*first)
+    for message in first:
+        send(message)
     for o in ring_x:
         pl.semaphore_signal(in_y, inc=1, device_id=other(o), device_id_type=MESH)
 
@@ -373,10 +374,9 @@
     for o in rest:
         pl.semaphore_signal(in_xy, inc=1, device_id=other(o), device_id_type=MESH)
 
-    wait_all(False, *first)
+    wait_all(False, *first[:2])
     rows = with_edges(rows_of(op1, rv1), rows_of(eg, re))
     unpack(rows, x1)
-    ring = advance_ring(rows, rs1, 1)
     for b in range(NB):
         acc = product(b, x1, idx)
         fl = f * live_of(b)
@@ -385,7 +385,8 @@
         cur = am * cheb[0, b] - fl * acc[:SIG]
         cheb[1, b] = cur
         place(b, cur, x2)
-    unpack(ring, x2)
+    wait_all(False, *first[2:])
+    unpack(advance_ring(rows, rs1, 1), x2)
 
     def step(b, k, xb):
         acc = product(b, xb, idx)
@@ -495,7 +496,7 @@
             vm((8, 3, 2, SIG, TILE), bf), vm((8, 3, 2, SIG, TILE), bf), vm((8, 3, 2, 1, TILE), f32),
             vm((8, 2, 3, SIG, TILE), f32), vm((8, 2, 3, SIG, TILE), f32), vm((8, 2, 10, 32, TILE), bf),
             vm((DEVICES, 1, TILE), f32), vm((1024, 1, TILE), f32),
-            dma((11,)), dma, dma, dma, dma, dma,
+            dma((11,)), dma, dma, dma, dma, dma, dma,
             dma, dma, pltpu.SemaphoreType.REGULAR, pltpu.SemaphoreType.REGULAR,
         ],
         compiler_params=pltpu.CompilerParams(collective_id=0, has_side_effects=True),

time: 28.4 us -> 27.8 us (0.979)
  Pallas kernels: 26.9 us -> 26.4 us
    pallas_call x1, Pallas kernels: 26 us -> 25.5 us  [shards(): pl.pallas_call(kernel, out_shape=(pltpu.VMEM((SCALES, NB, SIG, TILE), f32...]
where the time goes in v7:
time: 27.8 us; the launch traced here: 27.7 us
  Pallas kernels  26.4 us (95%)
  between operations  1.29 us (5%)
    pallas_call x1, Pallas kernels, shards(): pl.pallas_call(kernel, out_shape=(pltpu.VMEM((SCALES, NB, SIG, TILE), f32...  25.5 us
    pallas_call x1, Pallas kernels, shards(): pl.pallas_call(finish, out_shape=(jax.ShapeDtypeStruct((SCALES, NB, SIG,...  0.9 us

profile of v7, /device:TPU:1, one launch (start us, length us, event | category | flops | bytes accessed | tf_op | source)
XLA Modules:
  0.0 27.7 jit_solution(1446930350926713706)
XLA Ops:
  1.3 25.5 %wavelet.1 = (f32[6,16,16,128]{3,2,1,0:T(8,128)S(1)}, f32[6,16]{1,0:T(8,128)S(1)}) custom-call(f32[2,8,16,128]{3,2,1,0:T(8,128)} %sig_h.1, bf16[2,8,4,128,128]{4,3,2,1,0:T(8,128)(2,1)} %til_h.1, s32[2,4,8]{2,1,0:T(4,128)} %bitcast.3, s32[2,4,8]{2,1,0:T(4,128)} %bitcast.4, s32[2,8]{1,0:T(2,128)} %liv_h.1, s32[2,8]{1,0:T(2,128)} %bnd_h.1, f32[6,5]{1,0:T(8,128)} %cof_h.1, ...), custom_call_target="tpu_custom_call" | custom-call | tf_op jit(solution)/shard_map/wavelet/pallas_call | solution.py:482
  26.8 0.9 %finish.1 = (f32[6,16,16,128]{3,2,1,0:T(8,128)}, f32[6,16]{1,0:T(8,128)}) custom-call(f32[6,16,16,128]{3,2,1,0:T(8,128)S(1)} %get-tuple-element.6.tot, f32[6,16]{1,0:T(8,128)S(1)} %get-tuple-element.7.en), custom_call_target="tpu_custom_call" | custom-call | tf_op jit(solution)/shard_map/finish/pallas_call | solution.py:506

commit v8 on v7

--- a/solution.py
+++ b/solution.py
@@ -32,7 +32,8 @@
 def kernel(sig_h, til_h, dir_h, msk_h, liv_h, bnd_h, cof_h, spb_h,
            tot, en_ref,
            dir_s, msk_s, liv_s, bnd_s, cof_s, spb_s, sig, til, idx, loc, x1, x2, x3, x4, cheb, amul,
-           op1, op3, eg, sp1, sp3, tp, rv1, rv3, re, rs1, rs3, tr, ga, units,
+           op1, op3, eg, sp1, sp3, tp, oc1, oc3, ec1, sc1, sc3,
+           rv1, rv3, re, rs1, rs3, tr, rc1, rc3, rec, rsc1, rsc3, ga, units,
            ld, r1, r2, w1, r3, r4, w3, sa, ra, in_y, in_xy):
     gx, gy = lax.axis_index("gx"), lax.axis_index("gy")
     me = gx * GYN + gy
@@ -98,10 +99,25 @@
         q = q % 4
         return pltpu.roll(v, 32 * q, 1) if q else v
 
-    def add_to(packs, i, j, v):
-        key = (i, (j + 2) // 4)
-        v = shift(v, j + 2)
-        packs[key] = v if key not in packs else packs[key] + v
+    def add_to(packs, i, j, v, column):
+        for key, group in ((("m", i, (j + 2) // 4), j + 2),
+                           (("c", 0 if j < BY // 2 else 1), j + 2 + 2 * i)):
+            if key[0] == "c" and j not in column:
+                continue
+            w = shift(v, group)
+            packs[key] = w if key not in packs else packs[key] + w
+
+    def flush(packs, main, column, cast, tile_first):
+        for key, v in packs.items():
+            if key[0] == "c":
+                column[key[1]] = cast(v)
+            elif tile_first:
+                main[key[2], key[1]] = cast(v)
+            else:
+                main[key[1], key[2]] = cast(v)
+
+    same = lambda v: v
+    TWO, ONE = (0, 1, 6, 7), (0, 7)
 
     RING = [(r, q) for r in (1, 4) for q in range(1, 11)] + [(r, q) for r in (2, 3) for q in (1, 10)]
     slot_of = lambda er, ec: NB + (er - 1) * (BY + 2) + ec - 1
@@ -111,14 +127,16 @@
         e = v * edge_of(b)
         xb[slot_of(b // BY + 2, b % BY + 2)] = bf16(e)
         if packs is not None:
-            add_to(packs, b // BY, b % BY, e[:SIG])
+            add_to(packs, b // BY, b % BY, e[:SIG], TWO)
 
     def part_v(dx, dy):
-        return ({-1: pl.ds(0, 1), 1: pl.ds(2, 1), 0: pl.ds(0, 3)}[dy],)
+        return (pl.ds(0, 3),) if dy == 0 else None
 
     def part_s(dx, dy):
-        return ({-1: pl.ds(0, 1), 1: pl.ds(1, 1), 0: pl.ds(0, 2)}[dx],
-                {-1: pl.ds(0, 1), 1: pl.ds(2, 1), 0: pl.ds(0, 3)}[dy])
+        return ({-1: pl.ds(0, 1), 1: pl.ds(1, 1)}[dx], pl.ds(0, 3)) if dy == 0 else None
+
+    def part_c(dx, dy):
+        return (pl.ds((dy + 1) // 2, 1),) if dy != 0 else None
 
     def part_t(dx, dy):
         return ({-1: pl.ds(0, 1), 1: pl.ds(1, 1), 0: pl.ds(0, 2)}[dx],
@@ -134,7 +152,9 @@
             @pl.when(have[d])
             def _(d=d):
                 for src, dst, part, s_sem, r_sem in messages:
-                    descriptor(src, dst, part, s_sem, r_sem, d, OPP[d], part(*DIRS[d])).start()
+                    at = part(*DIRS[d])
+                    if at is not None:
+                        descriptor(src, dst, part, s_sem, r_sem, d, OPP[d], at).start()
 
     inner_x = jnp.logical_and(gx > 0, gx < GXN - 1)
     inner_y = jnp.logical_and(gy > 0, gy < GYN - 1)
@@ -144,6 +164,8 @@
             n = 0
             for src, _, part, _, _ in messages:
                 at = part(*DIRS[d])
+                if at is None:
+                    continue
                 shape = [p.size for p in at] + list(src.shape[len(at):])
                 n += src.dtype.itemsize * functools.reduce(operator.mul, shape) // 512
             return n
@@ -162,8 +184,10 @@
                         device_id=other(1), device_id_type=MESH)
                     cp.wait_send() if sent else cp.wait_recv()
 
-    first = ((op1, rv1, part_v, w1, r1), (eg, re, part_v, w1, r1), (sp1, rs1, part_s, w1, r2), (tp, tr, part_t, w1, r2))
-    v3, s3 = (op3, rv3, part_v, w3, r3), (sp3, rs3, part_s, w3, r4)
+    first = ((oc1, rc1, part_c, w1, r1), (op1, rv1, part_v, w1, r1), (eg, re, part_v, w1, r1), (ec1, rec, part_c, w1, r1),
+             (sp1, rs1, part_s, w1, r2), (sc1, rsc1, part_c, w1, r2), (tp, tr, part_t, w1, r2))
+    v3 = ((oc3, rc3, part_c, w3, r3), (op3, rv3, part_v, w3, r3))
+    s3 = ((sp3, rs3, part_s, w3, r4), (sc3, rsc3, part_c, w3, r4))
     U, D, L, R, UL, UR, DL, DR = range(8)
 
     def contract(lhs, rhs):
@@ -176,11 +200,9 @@
         v = sig[b // BY, b % BY] * live
         cheb[0, b] = v
         place(b, jnp.concatenate([v, jnp.where(top, live, 0.0)], axis=0), x1, packs)
-        add_to(epacks, b // BY, b % BY, edge_of(b))
-    for (i, t), v in packs.items():
-        op1[t, i] = bf16(v)
-    for (i, t), v in epacks.items():
-        eg[t, i] = v
+        add_to(epacks, b // BY, b % BY, edge_of(b), TWO)
+    flush(packs, op1, oc1, bf16, True)
+    flush(epacks, eg, ec1, same, True)
 
     for b in range(NB):
         i, j = b // BY, b % BY
@@ -228,7 +250,7 @@
             acc = p if acc is None else acc + p
         return acc
 
-    def local_part(k, xb, sp):
+    def local_part(k, xb, sp, sc):
         packs = {}
         for b in range(NB):
             acc = product(b, xb, loc, 32)
@@ -239,16 +261,15 @@
                 out = amul[b, :1, :32] * v - (2.0 * f) * acc - cheb[k - 1, b, :, :32]
             out = out * edge_of(b)[:, :32]
             add_to(packs, b // BY, b % BY,
-                   jnp.concatenate([out, jnp.zeros((SIG, TILE - 32), jnp.float32)], axis=1))
-        for (i, t), v in packs.items():
-            sp[i, t] = v
+                   jnp.concatenate([out, jnp.zeros((SIG, TILE - 32), jnp.float32)], axis=1), ONE)
+        flush(packs, sp, sc, same, False)
 
     for cp in til_cp:
         cp.wait()
     for b in range(NB):
         for side, wanted in directions(b):
             tp[b // BY, 1 + b % BY if side is None else 9 * side] = sorted_rows(b, wanted)
-    local_part(0, x1, sp1)
+    local_part(0, x1, sp1, sc1)
     pl.semaphore_wait(bar, count)
     for message in first:
         send(message)
@@ -258,7 +279,7 @@
     for d in range(8):
         @pl.when(jnp.logical_not(have[d]))
         def _(d=d):
-            for buf in (rv1, rv3, re, rs1, rs3, tr):
+            for buf in (rv1, rv3, re, rs1, rs3, tr, rc1, rc3, rec, rsc1, rsc3):
                 buf[d] = jnp.zeros(buf.shape[1:], buf.dtype)
 
     def add_totals(k):
@@ -268,17 +289,22 @@
                 t = a * cheb[k, b]
                 tot[s, b] = t if k == 0 else tot[s, b] + t
 
-    def rows_of(op, rv):
+    def beside(rc, i, o):
+        side = 1 if o in (L, UL, DL) else 0
+        return shift(f32(rc[o, side]), 2 * i)
+
+    def rows_of(op, rv, rc):
         rows = []
         for r in range(6):
             i = r % 2
             if r in (2, 3):
-                lo, hi, mine = rv[L, 2, i], rv[R, 0, i], [op[t, i] for t in range(3)]
+                ul, ur, mine = L, R, [op[t, i] for t in range(3)]
             else:
                 u, ul, ur = (U, UL, UR) if r < 2 else (D, DL, DR)
-                lo, hi, mine = rv[ul, 2, i], rv[ur, 0, i], [rv[u, t, i] for t in range(3)]
+                mine = [rv[u, t, i] for t in range(3)]
             mine = [f32(v) for v in mine]
-            rows.append([jnp.where(left, f32(lo), mine[0]), mine[1], jnp.where(left, mine[2], f32(hi))])
+            rows.append([jnp.where(left, beside(rc, i, ul), mine[0]), mine[1],
+                         jnp.where(left, mine[2], beside(rc, i, ur))])
         return rows
 
     def with_edges(rows, edges):
@@ -316,16 +342,20 @@
             return self.get(("c", r, t), lambda: jnp.where(
                 middle, one, jnp.where(left, shift(two, -1), shift(two, 1))))
 
-    def unpack(rows, xb):
+    def unpack(rows, xb, columns=None):
         for er, ec in RING:
-            v = jnp.where(low, shift(rows[er][ec // 4], -ec), 0.0)
+            tile, group = rows[er][ec // 4], ec
+            if columns is not None and ec in (1, 10):
+                o = {1: {1: UL, 10: UR}, 2: {1: L, 10: R}, 3: {1: L, 10: R}, 4: {1: DL, 10: DR}}[er][ec]
+                tile, group = columns(o), ec + 2 * (er % 2)
+            v = jnp.where(low, shift(tile, -group), 0.0)
             xb[slot_of(er, ec)] = bf16(v)
 
     r_iota = lax.broadcasted_iota(jnp.int32, (TILE, TILE), 0)
     c_iota = lax.broadcasted_iota(jnp.int32, (TILE, TILE), 1)
     across = jnp.logical_or(jnp.logical_and(r_iota < 32, c_iota >= 96), jnp.logical_and(r_iota >= 96, c_iota < 32))
 
-    def advance_ring(rows, rs, first):
+    def advance_ring(rows, rs, rsc, first):
         ins = Inputs(rows)
         none = jnp.zeros((32, TILE), jnp.bfloat16)
         zero = jnp.zeros((TILE, TILE), jnp.float32)
@@ -348,11 +378,11 @@
                 elif t == 0:
                     w = [none, tr[ul, i, 8], tr[u, i, 1], tr[u, i, 2]]
                     wq = [none, tr[ul, i, 9], tr[u, i, 0], none]
-                    own = jnp.where(left, rs[ul, i, 2], rs[u, i, 0])
+                    own = jnp.where(left, beside(rsc, i, ul), rs[u, i, 0])
                 else:
                     w = [tr[u, i, 7], tr[u, i, 8], tr[ur, i, 1], none]
                     wq = [none, tr[u, i, 9], tr[ur, i, 0], none]
-                    own = jnp.where(left, rs[u, i, 2], rs[ur, i, 0])
+                    own = jnp.where(left, rs[u, i, 2], beside(rsc, i, ur))
                 w = f32(jnp.concatenate(w, axis=0))
                 lhs = [ins.plain(feed, t), ins.crossing(feed, t)]
                 rhs = [bf16(jnp.where(across, zero, w)), bf16(jnp.where(across, w, zero))]
@@ -365,7 +395,7 @@
             for t, o, p, q in ((0, L, 8, 9), (2, R, 1, 0)):
                 at = 1 if t == 0 else 2
                 pad = lambda w: jnp.concatenate([none] * at + [w] + [none] * (3 - at), axis=0)
-                new[er][t] = update(rs[o, i, 2 - t], [ins.plain(feed, t), ins.column(2, t)],
+                new[er][t] = update(beside(rsc, i, o), [ins.plain(feed, t), ins.column(2, t)],
                                     [pad(tr[o, i, p]), pad(tr[o, i, q])], rows[er][t])
         return new
 
@@ -374,9 +404,14 @@
     for o in rest:
         pl.semaphore_signal(in_xy, inc=1, device_id=other(o), device_id_type=MESH)
 
-    wait_all(False, *first[:2])
-    rows = with_edges(rows_of(op1, rv1), rows_of(eg, re))
-    unpack(rows, x1)
+    wait_all(False, *first[:4])
+    rows = with_edges(rows_of(op1, rv1, rc1), rows_of(eg, re, rec))
+
+    def column1(o):
+        side = 1 if o in (L, UL, DL) else 0
+        return jnp.concatenate([f32(rc1[o, side]), jnp.where(top, rec[o, side], 0.0)], axis=0)
+
+    unpack(rows, x1, column1)
     for b in range(NB):
         acc = product(b, x1, idx)
         fl = f * live_of(b)
@@ -385,8 +420,8 @@
         cur = am * cheb[0, b] - fl * acc[:SIG]
         cheb[1, b] = cur
         place(b, cur, x2)
-    wait_all(False, *first[2:])
-    unpack(advance_ring(rows, rs1, 1), x2)
+    wait_all(False, *first[4:])
+    unpack(advance_ring(rows, rs1, rsc1, 1), x2)
 
     def step(b, k, xb):
         acc = product(b, xb, idx)
@@ -399,25 +434,26 @@
         cur = step(b, 1, x2)
         cheb[2, b] = cur
         place(b, cur, x3, packs)
-    for (i, t), v in packs.items():
-        op3[t, i] = bf16(v)
-    send(v3)
-    local_part(2, x3, sp3)
-    send(s3)
+    flush(packs, op3, oc3, bf16, True)
+    for message in v3:
+        send(message)
+    local_part(2, x3, sp3, sc3)
+    for message in s3:
+        send(message)
     add_totals(1)
     add_totals(2)
     wait_all(True, *first)
 
-    wait_all(False, v3)
-    rows = rows_of(op3, rv3)
-    unpack(rows, x3)
+    wait_all(False, *v3)
+    rows = rows_of(op3, rv3, rc3)
+    unpack(rows, x3, lambda o: f32(rc3[o, 1 if o in (L, UL, DL) else 0]))
     for b in range(NB):
         cur = step(b, 2, x3)
         cheb[3, b] = cur
         place(b, cur, x4)
     add_totals(3)
-    wait_all(False, s3)
-    unpack(advance_ring(rows, rs3, 0), x4)
+    wait_all(False, *s3)
+    unpack(advance_ring(rows, rs3, rsc3, 0), x4)
     sq = [None] * SCALES
     for b in range(NB):
         cur = step(b, 3, x4)
@@ -444,7 +480,7 @@
         pltpu.make_async_remote_copy(
             src_ref=ga.at[me], dst_ref=ga.at[me], send_sem=sa, recv_sem=ra,
             device_id=other(o), device_id_type=MESH).start()
-    wait_all(True, v3, s3)
+    wait_all(True, *v3, *s3)
     many = ga.at[pl.ds(0, DEVICES - 1)]
     pltpu.make_async_remote_copy(
         src_ref=many, dst_ref=many, send_sem=sa, recv_sem=ra, device_id=other(1), device_id_type=MESH).wait_recv()
@@ -493,8 +529,11 @@
             vm((DEG, NB, SIG, TILE), f32), vm((NB, 8, TILE), f32),
             vm((3, 2, SIG, TILE), bf), vm((3, 2, SIG, TILE), bf), vm((3, 2, 1, TILE), f32),
             vm((2, 3, SIG, TILE), f32), vm((2, 3, SIG, TILE), f32), vm((2, 10, 32, TILE), bf),
+            vm((2, SIG, TILE), bf), vm((2, SIG, TILE), bf), vm((2, 1, TILE), f32), vm((2, SIG, TILE), f32), vm((2, SIG, TILE), f32),
             vm((8, 3, 2, SIG, TILE), bf), vm((8, 3, 2, SIG, TILE), bf), vm((8, 3, 2, 1, TILE), f32),
             vm((8, 2, 3, SIG, TILE), f32), vm((8, 2, 3, SIG, TILE), f32), vm((8, 2, 10, 32, TILE), bf),
+            vm((8, 2, SIG, TILE), bf), vm((8, 2, SIG, TILE), bf), vm((8, 2, 1, TILE), f32),
+            vm((8, 2, SIG, TILE), f32), vm((8, 2, SIG, TILE), f32),
             vm((DEVICES, 1, TILE), f32), vm((1024, 1, TILE), f32),
             dma((11,)), dma, dma, dma, dma, dma, dma,
             dma, dma, pltpu.SemaphoreType.REGULAR, pltpu.SemaphoreType.REGULAR,

time: 27.8 us -> 27.9 us (level)
  no operation moved by 1% of the time
where the time goes in v8:
time: 27.9 us; the launch traced here: 27.7 us
  Pallas kernels  26.4 us (95%)
  between operations  1.29 us (5%)
    pallas_call x1, Pallas kernels, shards(): pl.pallas_call(kernel, out_shape=(pltpu.VMEM((SCALES, NB, SIG, TILE), f32...  25.5 us
    pallas_call x1, Pallas kernels, shards(): pl.pallas_call(finish, out_shape=(jax.ShapeDtypeStruct((SCALES, NB, SIG,...  0.9 us

profile of v8, /device:TPU:1, one launch (start us, length us, event | category | flops | bytes accessed | tf_op | source)
XLA Modules:
  0.0 27.7 jit_solution(9523844344576432780)
XLA Ops:
  1.3 25.5 %wavelet.1 = (f32[6,16,16,128]{3,2,1,0:T(8,128)S(1)}, f32[6,16]{1,0:T(8,128)S(1)}) custom-call(f32[2,8,16,128]{3,2,1,0:T(8,128)} %sig_h.1, bf16[2,8,4,128,128]{4,3,2,1,0:T(8,128)(2,1)} %til_h.1, s32[2,4,8]{2,1,0:T(4,128)} %bitcast.3, s32[2,4,8]{2,1,0:T(4,128)} %bitcast.4, s32[2,8]{1,0:T(2,128)} %liv_h.1, s32[2,8]{1,0:T(2,128)} %bnd_h.1, f32[6,5]{1,0:T(8,128)} %cof_h.1, ...), custom_call_target="tpu_custom_call" | custom-call | tf_op jit(solution)/shard_map/wavelet/pallas_call | solution.py:518
  26.8 0.9 %finish.1 = (f32[6,16,16,128]{3,2,1,0:T(8,128)}, f32[6,16]{1,0:T(8,128)}) custom-call(f32[6,16,16,128]{3,2,1,0:T(8,128)S(1)} %get-tuple-element.6.tot, f32[6,16]{1,0:T(8,128)S(1)} %get-tuple-element.7.en), custom_call_target="tpu_custom_call" | custom-call | tf_op jit(solution)/shard_map/finish/pallas_call | solution.py:545

commit v9 on v8

--- a/solution.py
+++ b/solution.py
@@ -14,6 +14,7 @@
 NB = BX * BY
 GXN, GYN = 32, 4
 ZERO = NB + (BX + 2) * (BY + 2)
+NR = 24
 NX = ZERO + 1
 NODES = 64 * 32 * 128
 DIRS = [(-1, 0), (1, 0), (0, -1), (0, 1), (-1, -1), (-1, 1), (1, -1), (1, 1)]
@@ -31,7 +32,7 @@
 
 def kernel(sig_h, til_h, dir_h, msk_h, liv_h, bnd_h, cof_h, spb_h,
            tot, en_ref,
-           dir_s, msk_s, liv_s, bnd_s, cof_s, spb_s, sig, til, idx, loc, x1, x2, x3, x4, cheb, amul,
+           dir_s, msk_s, liv_s, bnd_s, cof_s, spb_s, sig, til, idx, far, loc, x1, x2, x3, x4, y1, y3, cheb, base, amul, dloc, wr,
            op1, op3, eg, sp1, sp3, tp, oc1, oc3, ec1, sc1, sc3,
            rv1, rv3, re, rs1, rs3, tr, rc1, rc3, rec, rsc1, rsc3, ga, units,
            ld, r1, r2, w1, r3, r4, w3, sa, ra, in_y, in_xy):
@@ -88,6 +89,8 @@
     f32 = lambda a: a.astype(jnp.float32)
     for xb in (x1, x2, x3, x4):
         xb[ZERO] = jnp.zeros(xb.shape[1:], xb.dtype)
+    for yb in (y1, y3):
+        yb[NR] = jnp.zeros(yb.shape[1:], yb.dtype)
 
     def live_of(b):
         return (lane < liv_s[b // BY, b % BY]).astype(jnp.float32)
@@ -204,19 +207,28 @@
     flush(packs, op1, oc1, bf16, True)
     flush(epacks, eg, ec1, same, True)
 
-    for b in range(NB):
-        i, j = b // BY, b % BY
-        for s in range(SLOTS):
-            d = dir_s[i, s, j]
-            r = (d * 11) >> 5
-            q = d - 3 * r
-            off = jnp.where(d == 4, b, NB + (i + r) * (BY + 2) + (j + q))
-            off = jnp.where(msk_s[i, s, j] == 1, off, ZERO)
-            idx[b * SLOTS + s] = off
-            away = r == 2 * i
-            if j in (0, BY - 1):
-                away = jnp.logical_or(away, q == (0 if j == 0 else 2))
-            loc[b * SLOTS + s] = jnp.where(away, ZERO, off)
+    def tables(own):
+        for b in range(NB):
+            i, j = b // BY, b % BY
+            for s in range(SLOTS):
+                d = dir_s[i, s, j]
+                r = (d * 11) >> 5
+                q = d - 3 * r
+                used = msk_s[i, s, j] == 1
+                off = jnp.where(d == 4, b, NB + (i + r) * (BY + 2) + (j + q))
+                ring = 10 * i + j + q
+                away = r == 2 * i
+                if j in (0, BY - 1):
+                    beyond = q == (0 if j == 0 else 2)
+                    ring = jnp.where(away, ring, 20 + 2 * (i + r - 1) + (0 if j == 0 else 1))
+                    away = jnp.logical_or(away, beyond)
+                if own:
+                    loc[b * SLOTS + s] = jnp.where(jnp.logical_and(used, jnp.logical_not(away)), off, ZERO)
+                else:
+                    idx[b * SLOTS + s] = jnp.where(used, off, ZERO)
+                    far[b * SLOTS + s] = jnp.where(jnp.logical_and(used, away), ring, NR)
+
+    tables(True)
 
     def sorted_rows(b, wanted):
         i, j = b // BY, b % BY
@@ -250,6 +262,23 @@
             acc = p if acc is None else acc + p
         return acc
 
+    def own_part(k, xb):
+        for b in range(NB):
+            acc = product(b, xb, loc)
+            fl = f * live_of(b)
+            if k == 0:
+                deg = fl * acc[SIG:SIG + 1]
+                dloc[b] = jnp.broadcast_to(deg, (8, TILE))
+                base[b] = (deg - 1.0) * cheb[0, b] - fl * acc[:SIG]
+            else:
+                am = amul[b]
+                am = jnp.concatenate([am, am], axis=0)
+                base[b] = am * cheb[k, b] - (2.0 * fl) * acc - cheb[k - 1, b]
+
+    def far_product(b, yb):
+        parts = [yb[far[b * SLOTS + s], s] for s in range(SLOTS)]
+        return contract((parts[0] + parts[1]) + (parts[2] + parts[3]), wr[b])
+
     def local_part(k, xb, sp, sc):
         packs = {}
         for b in range(NB):
@@ -262,7 +291,7 @@
             out = out * edge_of(b)[:, :32]
             add_to(packs, b // BY, b % BY,
                    jnp.concatenate([out, jnp.zeros((SIG, TILE - 32), jnp.float32)], axis=1), ONE)
-        flush(packs, sp, sc, same, False)
+        flush(packs, sp, sc, same if k == 0 else bf16, False)
 
     for cp in til_cp:
         cp.wait()
@@ -342,14 +371,28 @@
             return self.get(("c", r, t), lambda: jnp.where(
                 middle, one, jnp.where(left, shift(two, -1), shift(two, 1))))
 
-    def unpack(rows, xb, columns=None):
+    groups = [jnp.logical_and(lane >= 32 * s, lane < 32 * s + 32) for s in range(SLOTS)]
+
+    groups = [jnp.logical_and(lane >= 32 * s, lane < 32 * s + 32) for s in range(SLOTS)]
+
+    def unpack(rows, xb):
         for er, ec in RING:
-            tile, group = rows[er][ec // 4], ec
-            if columns is not None and ec in (1, 10):
+            v = jnp.where(low, shift(rows[er][ec // 4], -ec), 0.0)
+            xb[slot_of(er, ec)] = bf16(v)
+
+    def unpack_far(rows, yb, columns):
+        made = {}
+        for n, (er, ec) in enumerate(RING):
+            group = ec
+            if ec in (1, 10):
                 o = {1: {1: UL, 10: UR}, 2: {1: L, 10: R}, 3: {1: L, 10: R}, 4: {1: DL, 10: DR}}[er][ec]
-                tile, group = columns(o), ec + 2 * (er % 2)
-            v = jnp.where(low, shift(tile, -group), 0.0)
-            xb[slot_of(er, ec)] = bf16(v)
+                key, group = o, ec + 2 * (er % 2)
+                made[key] = columns(o) if key not in made else made[key]
+            else:
+                key = (er, ec // 4)
+                made[key] = bf16(rows[er][ec // 4]) if key not in made else made[key]
+            for s in range(SLOTS):
+                yb[n, s] = jnp.where(groups[s], shift(made[key], s - group), jnp.bfloat16(0))
 
     r_iota = lax.broadcasted_iota(jnp.int32, (TILE, TILE), 0)
     c_iota = lax.broadcasted_iota(jnp.int32, (TILE, TILE), 1)
@@ -374,15 +417,15 @@
             for t in range(3):
                 if t == 1:
                     w = [tr[u, i, 3 + n] for n in range(4)]
-                    own, wq = rs[u, i, 1], None
+                    own, wq = f32(rs[u, i, 1]), None
                 elif t == 0:
                     w = [none, tr[ul, i, 8], tr[u, i, 1], tr[u, i, 2]]
                     wq = [none, tr[ul, i, 9], tr[u, i, 0], none]
-                    own = jnp.where(left, beside(rsc, i, ul), rs[u, i, 0])
+                    own = jnp.where(left, beside(rsc, i, ul), f32(rs[u, i, 0]))
                 else:
                     w = [tr[u, i, 7], tr[u, i, 8], tr[ur, i, 1], none]
                     wq = [none, tr[u, i, 9], tr[ur, i, 0], none]
-                    own = jnp.where(left, rs[u, i, 2], beside(rsc, i, ur))
+                    own = jnp.where(left, f32(rs[u, i, 2]), beside(rsc, i, ur))
                 w = f32(jnp.concatenate(w, axis=0))
                 lhs = [ins.plain(feed, t), ins.crossing(feed, t)]
                 rhs = [bf16(jnp.where(across, zero, w)), bf16(jnp.where(across, w, zero))]
@@ -399,7 +442,12 @@
                                     [pad(tr[o, i, p]), pad(tr[o, i, q])], rows[er][t])
         return new
 
+    tables(False)
     add_totals(0)
+    for b in range(NB):
+        packed = [shift(jnp.where(low, f32(til[b, s]), 0.0), s) for s in range(SLOTS)]
+        wr[b] = bf16((packed[0] + packed[1]) + (packed[2] + packed[3]))
+    own_part(0, x1)
     pl.semaphore_wait(in_y, 3)
     for o in rest:
         pl.semaphore_signal(in_xy, inc=1, device_id=other(o), device_id_type=MESH)
@@ -409,15 +457,15 @@
 
     def column1(o):
         side = 1 if o in (L, UL, DL) else 0
-        return jnp.concatenate([f32(rc1[o, side]), jnp.where(top, rec[o, side], 0.0)], axis=0)
-
-    unpack(rows, x1, column1)
+        return jnp.concatenate([rc1[o, side], bf16(jnp.where(top, rec[o, side], 0.0))], axis=0)
+
+    unpack_far(rows, y1, column1)
     for b in range(NB):
-        acc = product(b, x1, idx)
+        acc = far_product(b, y1)
         fl = f * live_of(b)
-        am = fl * acc[SIG:SIG + 1] - 1.0
-        amul[b] = jnp.broadcast_to(2.0 * am, (8, TILE))
-        cur = am * cheb[0, b] - fl * acc[:SIG]
+        deg = fl * acc[SIG:SIG + 1]
+        amul[b] = 2.0 * (dloc[b] + jnp.broadcast_to(deg, (8, TILE)) - 1.0)
+        cur = base[b] + deg * cheb[0, b] - fl * acc[:SIG]
         cheb[1, b] = cur
         place(b, cur, x2)
     wait_all(False, *first[4:])
@@ -440,15 +488,16 @@
     local_part(2, x3, sp3, sc3)
     for message in s3:
         send(message)
+    own_part(2, x3)
     add_totals(1)
     add_totals(2)
     wait_all(True, *first)
 
     wait_all(False, *v3)
     rows = rows_of(op3, rv3, rc3)
-    unpack(rows, x3, lambda o: f32(rc3[o, 1 if o in (L, UL, DL) else 0]))
+    unpack_far(rows, y3, lambda o: rc3[o, 1 if o in (L, UL, DL) else 0])
     for b in range(NB):
-        cur = step(b, 2, x3)
+        cur = base[b] - (2.0 * f * live_of(b)) * far_product(b, y3)
         cheb[3, b] = cur
         place(b, cur, x4)
     add_totals(3)
@@ -524,16 +573,18 @@
             sm((BX, SLOTS, BY), i32), sm((BX, SLOTS, BY), i32), sm((BX, BY), i32), sm((BX, BY), i32),
             sm((SCALES, DEG + 1), f32), sm((1,), f32),
             vm((BX, BY, SIG, TILE), f32), vm((NB, SLOTS, TILE, TILE), bf),
-            sm((NB * SLOTS,), i32), sm((NB * SLOTS,), i32),
+            sm((NB * SLOTS,), i32), sm((NB * SLOTS,), i32), sm((NB * SLOTS,), i32),
             vm((NX, 32, TILE), bf), vm((NX, SIG, TILE), bf), vm((NX, SIG, TILE), bf), vm((NX, SIG, TILE), bf),
-            vm((DEG, NB, SIG, TILE), f32), vm((NB, 8, TILE), f32),
+            vm((NR + 1, SLOTS, 32, TILE), bf), vm((NR + 1, SLOTS, SIG, TILE), bf),
+            vm((DEG, NB, SIG, TILE), f32), vm((NB, SIG, TILE), f32), vm((NB, 8, TILE), f32), vm((NB, 8, TILE), f32),
+            vm((NB, TILE, TILE), bf),
             vm((3, 2, SIG, TILE), bf), vm((3, 2, SIG, TILE), bf), vm((3, 2, 1, TILE), f32),
-            vm((2, 3, SIG, TILE), f32), vm((2, 3, SIG, TILE), f32), vm((2, 10, 32, TILE), bf),
-            vm((2, SIG, TILE), bf), vm((2, SIG, TILE), bf), vm((2, 1, TILE), f32), vm((2, SIG, TILE), f32), vm((2, SIG, TILE), f32),
+            vm((2, 3, SIG, TILE), f32), vm((2, 3, SIG, TILE), bf), vm((2, 10, 32, TILE), bf),
+            vm((2, SIG, TILE), bf), vm((2, SIG, TILE), bf), vm((2, 1, TILE), f32), vm((2, SIG, TILE), f32), vm((2, SIG, TILE), bf),
             vm((8, 3, 2, SIG, TILE), bf), vm((8, 3, 2, SIG, TILE), bf), vm((8, 3, 2, 1, TILE), f32),
-            vm((8, 2, 3, SIG, TILE), f32), vm((8, 2, 3, SIG, TILE), f32), vm((8, 2, 10, 32, TILE), bf),
+            vm((8, 2, 3, SIG, TILE), f32), vm((8, 2, 3, SIG, TILE), bf), vm((8, 2, 10, 32, TILE), bf),
             vm((8, 2, SIG, TILE), bf), vm((8, 2, SIG, TILE), bf), vm((8, 2, 1, TILE), f32),
-            vm((8, 2, SIG, TILE), f32), vm((8, 2, SIG, TILE), f32),
+            vm((8, 2, SIG, TILE), f32), vm((8, 2, SIG, TILE), bf),
             vm((DEVICES, 1, TILE), f32), vm((1024, 1, TILE), f32),
             dma((11,)), dma, dma, dma, dma, dma, dma,
             dma, dma, pltpu.SemaphoreType.REGULAR, pltpu.SemaphoreType.REGULAR,

time: 27.9 us -> 27.6 us (0.989)
  Pallas kernels: 26.4 us -> 26.1 us
where the time goes in v9:
time: 27.6 us; the launch traced here: 27.4 us
  Pallas kernels  26.1 us (95%)
  between operations  1.29 us (5%)
    pallas_call x1, Pallas kernels, shards(): pl.pallas_call(kernel, out_shape=(pltpu.VMEM((SCALES, NB, SIG, TILE), f32...  25.2 us
    pallas_call x1, Pallas kernels, shards(): pl.pallas_call(finish, out_shape=(jax.ShapeDtypeStruct((SCALES, NB, SIG,...  0.9 us

profile of v9, /device:TPU:1, one launch (start us, length us, event | category | flops | bytes accessed | tf_op | source)
XLA Modules:
  0.0 27.4 jit_solution(11738695945387873595)
XLA Ops:
  1.3 25.2 %wavelet.1 = (f32[6,16,16,128]{3,2,1,0:T(8,128)S(1)}, f32[6,16]{1,0:T(8,128)S(1)}) custom-call(f32[2,8,16,128]{3,2,1,0:T(8,128)} %sig_h.1, bf16[2,8,4,128,128]{4,3,2,1,0:T(8,128)(2,1)} %til_h.1, s32[2,4,8]{2,1,0:T(4,128)} %bitcast.3, s32[2,4,8]{2,1,0:T(4,128)} %bitcast.4, s32[2,8]{1,0:T(2,128)} %liv_h.1, s32[2,8]{1,0:T(2,128)} %bnd_h.1, f32[6,5]{1,0:T(8,128)} %cof_h.1, ...), custom_call_target="tpu_custom_call" | custom-call | tf_op jit(solution)/shard_map/wavelet/pallas_call | solution.py:567
  26.5 0.9 %finish.1 = (f32[6,16,16,128]{3,2,1,0:T(8,128)}, f32[6,16]{1,0:T(8,128)}) custom-call(f32[6,16,16,128]{3,2,1,0:T(8,128)S(1)} %get-tuple-element.6.tot, f32[6,16]{1,0:T(8,128)S(1)} %get-tuple-element.7.en), custom_call_target="tpu_custom_call" | custom-call | tf_op jit(solution)/shard_map/finish/pallas_call | solution.py:596

commit v10 on v9

--- a/solution.py
+++ b/solution.py
@@ -103,8 +103,8 @@
         return pltpu.roll(v, 32 * q, 1) if q else v
 
     def add_to(packs, i, j, v, column):
-        for key, group in ((("m", i, (j + 2) // 4), j + 2),
-                           (("c", 0 if j < BY // 2 else 1), j + 2 + 2 * i)):
+        for key, group in ((("m", i, j // 4), j),
+                           (("c", 0 if j < BY // 2 else 1), j + 2 * i)):
             if key[0] == "c" and j not in column:
                 continue
             w = shift(v, group)
@@ -122,28 +122,28 @@
     same = lambda v: v
     TWO, ONE = (0, 1, 6, 7), (0, 7)
 
-    RING = [(r, q) for r in (1, 4) for q in range(1, 11)] + [(r, q) for r in (2, 3) for q in (1, 10)]
-    slot_of = lambda er, ec: NB + (er - 1) * (BY + 2) + ec - 1
+    RING = [(r, q) for r in (1, 4) for q in range(3, 13)] + [(r, q) for r in (2, 3) for q in (3, 12)]
+    slot_of = lambda er, ec: NB + (er - 1) * (BY + 2) + ec - 3
 
     def place(b, v, xb, packs=None):
         xb[b] = bf16(v)
         e = v * edge_of(b)
-        xb[slot_of(b // BY + 2, b % BY + 2)] = bf16(e)
+        xb[slot_of(b // BY + 2, b % BY + 4)] = bf16(e)
         if packs is not None:
             add_to(packs, b // BY, b % BY, e[:SIG], TWO)
 
     def part_v(dx, dy):
-        return (pl.ds(0, 3),) if dy == 0 else None
+        return (pl.ds(0, 2),) if dy == 0 else None
 
     def part_s(dx, dy):
-        return ({-1: pl.ds(0, 1), 1: pl.ds(1, 1)}[dx], pl.ds(0, 3)) if dy == 0 else None
+        return ({-1: pl.ds(0, 1), 1: pl.ds(1, 1)}[dx], pl.ds(0, 2)) if dy == 0 else None
 
     def part_c(dx, dy):
         return (pl.ds((dy + 1) // 2, 1),) if dy != 0 else None
 
     def part_t(dx, dy):
         return ({-1: pl.ds(0, 1), 1: pl.ds(1, 1), 0: pl.ds(0, 2)}[dx],
-                {-1: pl.ds(0, 2), 1: pl.ds(8, 2), 0: pl.ds(0, 10)}[dy])
+                {-1: pl.ds(0, 2), 1: pl.ds(8, 2), 0: pl.ds(0, 9)}[dy])
 
     def descriptor(src, dst, part, s_sem, r_sem, d, o, at):
         return pltpu.make_async_remote_copy(
@@ -247,11 +247,11 @@
 
     def directions(b):
         i, j = b // BY, b % BY
-        yield None, [(6 * i + q, j + 1 + q) for q in range(3)]
+        yield None, [(6 * i + q, j + q - 1) for q in range(3)]
         if j == 0:
-            yield 0, [(3 - 3 * i, 1), (6 - 3 * i, 0)]
+            yield 0, [(3 - 3 * i, 3), (6 - 3 * i, 2)]
         if j == BY - 1:
-            yield 1, [(5 - 3 * i, 2), (8 - 3 * i, 3)]
+            yield 1, [(5 - 3 * i, 0), (8 - 3 * i, 1)]
 
     def product(b, xb, table, rows=TILE):
         acc = None
@@ -295,9 +295,18 @@
 
     for cp in til_cp:
         cp.wait()
+    ends = {}
     for b in range(NB):
         for side, wanted in directions(b):
-            tp[b // BY, 1 + b % BY if side is None else 9 * side] = sorted_rows(b, wanted)
+            rows = sorted_rows(b, wanted)
+            if side is None:
+                tp[b // BY, 1 + b % BY] = rows
+            else:
+                ends[b // BY, side] = rows
+    for i in range(BX):
+        both = ends[i, 0] + ends[i, 1]
+        tp[i, 0] = both
+        tp[i, 9] = both
     local_part(0, x1, sp1, sc1)
     pl.semaphore_wait(bar, count)
     for message in first:
@@ -327,13 +336,11 @@
         for r in range(6):
             i = r % 2
             if r in (2, 3):
-                ul, ur, mine = L, R, [op[t, i] for t in range(3)]
+                ul, ur, mine = L, R, [op[t, i] for t in range(2)]
             else:
                 u, ul, ur = (U, UL, UR) if r < 2 else (D, DL, DR)
-                mine = [rv[u, t, i] for t in range(3)]
-            mine = [f32(v) for v in mine]
-            rows.append([jnp.where(left, beside(rc, i, ul), mine[0]), mine[1],
-                         jnp.where(left, mine[2], beside(rc, i, ur))])
+                mine = [rv[u, t, i] for t in range(2)]
+            rows.append([beside(rc, i, ul), f32(mine[0]), f32(mine[1]), beside(rc, i, ur)])
         return rows
 
     def with_edges(rows, edges):
@@ -363,13 +370,13 @@
         def crossing(self, r, t):
             rows = self.rows[r]
             before = rows[t - 1] if t > 0 else jnp.zeros_like(rows[t])
-            after = rows[t + 1] if t < 2 else jnp.zeros_like(rows[t])
+            after = rows[t + 1] if t < 3 else jnp.zeros_like(rows[t])
             return self.get(("x", r, t), lambda: jnp.where(left, after, before))
 
         def column(self, r, t):
             one, two = self.rows[r][t], self.rows[r + 1][t]
             return self.get(("c", r, t), lambda: jnp.where(
-                middle, one, jnp.where(left, shift(two, -1), shift(two, 1))))
+                middle, jnp.where(left, shift(two, 1), shift(two, -1)), one))
 
     groups = [jnp.logical_and(lane >= 32 * s, lane < 32 * s + 32) for s in range(SLOTS)]
 
@@ -384,8 +391,8 @@
         made = {}
         for n, (er, ec) in enumerate(RING):
             group = ec
-            if ec in (1, 10):
-                o = {1: {1: UL, 10: UR}, 2: {1: L, 10: R}, 3: {1: L, 10: R}, 4: {1: DL, 10: DR}}[er][ec]
+            if ec in (3, 12):
+                o = {1: {3: UL, 12: UR}, 2: {3: L, 12: R}, 3: {3: L, 12: R}, 4: {3: DL, 12: DR}}[er][ec]
                 key, group = o, ec + 2 * (er % 2)
                 made[key] = columns(o) if key not in made else made[key]
             else:
@@ -409,37 +416,31 @@
                 return own + f * (acc[SIG:SIG + 1] * v[:SIG] - acc[:SIG])
             return own - (2.0 * f) * acc
 
-        new = [[None] * 3 for _ in range(6)]
-        for er, u, ul, ur in ((1, U, UL, UR), (4, D, DL, DR)):
-            i = 1 if er == 1 else 0
-            feed = er + 1 if i else er - 1
+        def at(w, group):
+            return jnp.concatenate([none] * group + [w] + [none] * (3 - group), axis=0)
+
+        def end(q, right):
+            return jnp.where(left if right else jnp.logical_not(left), q, jnp.bfloat16(0))
+
+        new = [[None] * 4 for _ in range(6)]
+        for er, u, ul, ur in ((1, U, UL, UR), (2, None, L, R), (3, None, L, R), (4, D, DL, DR)):
+            i = er % 2
+            feed = er + 1 if er in (1, 3) else er - 1
             edge = er - i
-            for t in range(3):
-                if t == 1:
-                    w = [tr[u, i, 3 + n] for n in range(4)]
-                    own, wq = f32(rs[u, i, 1]), None
-                elif t == 0:
-                    w = [none, tr[ul, i, 8], tr[u, i, 1], tr[u, i, 2]]
-                    wq = [none, tr[ul, i, 9], tr[u, i, 0], none]
-                    own = jnp.where(left, beside(rsc, i, ul), f32(rs[u, i, 0]))
-                else:
-                    w = [tr[u, i, 7], tr[u, i, 8], tr[ur, i, 1], none]
-                    wq = [none, tr[u, i, 9], tr[ur, i, 0], none]
-                    own = jnp.where(left, f32(rs[u, i, 2]), beside(rsc, i, ur))
-                w = f32(jnp.concatenate(w, axis=0))
-                lhs = [ins.plain(feed, t), ins.crossing(feed, t)]
-                rhs = [bf16(jnp.where(across, zero, w)), bf16(jnp.where(across, w, zero))]
-                if wq is not None:
-                    lhs.append(ins.column(edge, t))
-                    rhs.append(jnp.concatenate(wq, axis=0))
-                new[er][t] = update(own, lhs, rhs, rows[er][t])
-        for er, i in ((2, 0), (3, 1)):
-            feed = er - 1 if i == 0 else er + 1
-            for t, o, p, q in ((0, L, 8, 9), (2, R, 1, 0)):
-                at = 1 if t == 0 else 2
-                pad = lambda w: jnp.concatenate([none] * at + [w] + [none] * (3 - at), axis=0)
-                new[er][t] = update(beside(rsc, i, o), [ins.plain(feed, t), ins.column(2, t)],
-                                    [pad(tr[o, i, p]), pad(tr[o, i, q])], rows[er][t])
+            for t in range(4):
+                if t == 0:
+                    new[er][t] = update(beside(rsc, i, ul), [ins.row(feed, 3), ins.column(edge, 1)],
+                                        [at(tr[ul, i, 8], 3), at(end(tr[ul, i, 9], True), 3)], rows[er][t])
+                elif t == 3:
+                    new[er][t] = update(beside(rsc, i, ur), [ins.row(feed, 12), ins.column(edge, 2)],
+                                        [at(tr[ur, i, 1], 0), at(end(tr[ur, i, 0], False), 0)], rows[er][t])
+                elif u is not None:
+                    w = f32(jnp.concatenate([tr[u, i, 4 * t - 3 + n] for n in range(4)], axis=0))
+                    q = at(end(tr[u, i, 0], t == 2), 0 if t == 1 else 3)
+                    new[er][t] = update(
+                        f32(rs[u, i, t - 1]),
+                        [ins.plain(feed, t), ins.crossing(feed, t), ins.column(edge, 0 if t == 1 else 3)],
+                        [bf16(jnp.where(across, zero, w)), bf16(jnp.where(across, w, zero)), q], rows[er][t])
         return new
 
     tables(False)
@@ -578,11 +579,11 @@
             vm((NR + 1, SLOTS, 32, TILE), bf), vm((NR + 1, SLOTS, SIG, TILE), bf),
             vm((DEG, NB, SIG, TILE), f32), vm((NB, SIG, TILE), f32), vm((NB, 8, TILE), f32), vm((NB, 8, TILE), f32),
             vm((NB, TILE, TILE), bf),
-            vm((3, 2, SIG, TILE), bf), vm((3, 2, SIG, TILE), bf), vm((3, 2, 1, TILE), f32),
-            vm((2, 3, SIG, TILE), f32), vm((2, 3, SIG, TILE), bf), vm((2, 10, 32, TILE), bf),
+            vm((2, 2, SIG, TILE), bf), vm((2, 2, SIG, TILE), bf), vm((2, 2, 1, TILE), f32),
+            vm((2, 2, SIG, TILE), f32), vm((2, 2, SIG, TILE), bf), vm((2, 10, 32, TILE), bf),
             vm((2, SIG, TILE), bf), vm((2, SIG, TILE), bf), vm((2, 1, TILE), f32), vm((2, SIG, TILE), f32), vm((2, SIG, TILE), bf),
-            vm((8, 3, 2, SIG, TILE), bf), vm((8, 3, 2, SIG, TILE), bf), vm((8, 3, 2, 1, TILE), f32),
-            vm((8, 2, 3, SIG, TILE), f32), vm((8, 2, 3, SIG, TILE), bf), vm((8, 2, 10, 32, TILE), bf),
+            vm((8, 2, 2, SIG, TILE), bf), vm((8, 2, 2, SIG, TILE), bf), vm((8, 2, 2, 1, TILE), f32),
+            vm((8, 2, 2, SIG, TILE), f32), vm((8, 2, 2, SIG, TILE), bf), vm((8, 2, 10, 32, TILE), bf),
             vm((8, 2, SIG, TILE), bf), vm((8, 2, SIG, TILE), bf), vm((8, 2, 1, TILE), f32),
             vm((8, 2, SIG, TILE), f32), vm((8, 2, SIG, TILE), bf),
             vm((DEVICES, 1, TILE), f32), vm((1024, 1, TILE), f32),

time: 27.6 us -> 27.3 us (0.989)
  Pallas kernels: 26.1 us -> 25.8 us
    pallas_call x1, Pallas kernels: 25.2 us -> 24.9 us  [shards(): pl.pallas_call(kernel, out_shape=(pltpu.VMEM((SCALES, NB, SIG, TILE), f32...]
where the time goes in v10:
time: 27.3 us; the launch traced here: 27.1 us
  Pallas kernels  25.8 us (95%)
  between operations  1.29 us (5%)
    pallas_call x1, Pallas kernels, shards(): pl.pallas_call(kernel, out_shape=(pltpu.VMEM((SCALES, NB, SIG, TILE), f32...  24.9 us
    pallas_call x1, Pallas kernels, shards(): pl.pallas_call(finish, out_shape=(jax.ShapeDtypeStruct((SCALES, NB, SIG,...  0.9 us

profile of v10, /device:TPU:1, one launch (start us, length us, event | category | flops | bytes accessed | tf_op | source)
XLA Modules:
  0.0 27.1 jit_solution(18270750556517128622)
XLA Ops:
  1.3 24.9 %wavelet.1 = (f32[6,16,16,128]{3,2,1,0:T(8,128)S(1)}, f32[6,16]{1,0:T(8,128)S(1)}) custom-call(f32[2,8,16,128]{3,2,1,0:T(8,128)} %sig_h.1, bf16[2,8,4,128,128]{4,3,2,1,0:T(8,128)(2,1)} %til_h.1, s32[2,4,8]{2,1,0:T(4,128)} %bitcast.3, s32[2,4,8]{2,1,0:T(4,128)} %bitcast.4, s32[2,8]{1,0:T(2,128)} %liv_h.1, s32[2,8]{1,0:T(2,128)} %bnd_h.1, f32[6,5]{1,0:T(8,128)} %cof_h.1, ...), custom_call_target="tpu_custom_call" | custom-call | tf_op jit(solution)/shard_map/wavelet/pallas_call | solution.py:568
  26.2 0.9 %finish.1 = (f32[6,16,16,128]{3,2,1,0:T(8,128)}, f32[6,16]{1,0:T(8,128)}) custom-call(f32[6,16,16,128]{3,2,1,0:T(8,128)S(1)} %get-tuple-element.6.tot, f32[6,16]{1,0:T(8,128)S(1)} %get-tuple-element.7.en), custom_call_target="tpu_custom_call" | custom-call | tf_op jit(solution)/shard_map/finish/pallas_call | solution.py:597

commit v11 on v10

--- a/solution.py
+++ b/solution.py
@@ -84,6 +84,7 @@
     lane = lax.broadcasted_iota(jnp.int32, (1, TILE), 1)
     low, high, left = lane < 32, lane >= 96, lane < 64
     middle = jnp.logical_and(lane >= 32, lane < 96)
+    groups = [jnp.logical_and(lane >= 32 * s, lane < 32 * s + 32) for s in range(SLOTS)]
     f = 2.0 / spb_s[0]
     bf16 = lambda a: a.astype(jnp.bfloat16)
     f32 = lambda a: a.astype(jnp.float32)
@@ -143,7 +144,7 @@
 
     def part_t(dx, dy):
         return ({-1: pl.ds(0, 1), 1: pl.ds(1, 1), 0: pl.ds(0, 2)}[dx],
-                {-1: pl.ds(0, 2), 1: pl.ds(8, 2), 0: pl.ds(0, 9)}[dy])
+                {-1: pl.ds(0, 2), 1: pl.ds(7, 2), 0: pl.ds(0, 7)}[dy])
 
     def descriptor(src, dst, part, s_sem, r_sem, d, o, at):
         return pltpu.make_async_remote_copy(
@@ -295,18 +296,23 @@
 
     for cp in til_cp:
         cp.wait()
-    ends = {}
+    ends, p = {}, {}
     for b in range(NB):
         for side, wanted in directions(b):
             rows = sorted_rows(b, wanted)
             if side is None:
-                tp[b // BY, 1 + b % BY] = rows
+                p[b // BY, b % BY] = rows
             else:
                 ends[b // BY, side] = rows
     for i in range(BX):
+        for h in range(2):
+            for n in range(3):
+                spare = jnp.where(groups[(n + 2) % 4], p[i, 4 * h + 3], jnp.bfloat16(0))
+                tp[i, 1 + 3 * h + n] = p[i, 4 * h + n] + spare
         both = ends[i, 0] + ends[i, 1]
         tp[i, 0] = both
-        tp[i, 9] = both
+        tp[i, 7] = p[i, 7]
+        tp[i, 8] = both
     local_part(0, x1, sp1, sc1)
     pl.semaphore_wait(bar, count)
     for message in first:
@@ -377,10 +383,6 @@
             one, two = self.rows[r][t], self.rows[r + 1][t]
             return self.get(("c", r, t), lambda: jnp.where(
                 middle, jnp.where(left, shift(two, 1), shift(two, -1)), one))
-
-    groups = [jnp.logical_and(lane >= 32 * s, lane < 32 * s + 32) for s in range(SLOTS)]
-
-    groups = [jnp.logical_and(lane >= 32 * s, lane < 32 * s + 32) for s in range(SLOTS)]
 
     def unpack(rows, xb):
         for er, ec in RING:
@@ -409,6 +411,7 @@
         ins = Inputs(rows)
         none = jnp.zeros((32, TILE), jnp.bfloat16)
         zero = jnp.zeros((TILE, TILE), jnp.float32)
+        nil = jnp.bfloat16(0)
 
         def update(own, lhs, rhs, v):
             acc = contract(jnp.concatenate(lhs, axis=1), jnp.concatenate(rhs, axis=1))
@@ -430,12 +433,15 @@
             for t in range(4):
                 if t == 0:
                     new[er][t] = update(beside(rsc, i, ul), [ins.row(feed, 3), ins.column(edge, 1)],
-                                        [at(tr[ul, i, 8], 3), at(end(tr[ul, i, 9], True), 3)], rows[er][t])
+                                        [at(tr[ul, i, 7], 3), at(end(tr[ul, i, 8], True), 3)], rows[er][t])
                 elif t == 3:
                     new[er][t] = update(beside(rsc, i, ur), [ins.row(feed, 12), ins.column(edge, 2)],
-                                        [at(tr[ur, i, 1], 0), at(end(tr[ur, i, 0], False), 0)], rows[er][t])
+                                        [at(jnp.where(groups[2], nil, tr[ur, i, 1]), 0), at(end(tr[ur, i, 0], False), 0)], rows[er][t])
                 elif u is not None:
-                    w = f32(jnp.concatenate([tr[u, i, 4 * t - 3 + n] for n in range(4)], axis=0))
+                    held = [tr[u, i, 3 * t - 2 + n] for n in range(3)]
+                    w = [jnp.where(groups[(n + 2) % 4], nil, held[n]) for n in range(3)]
+                    w.append(jnp.where(groups[2], held[0], jnp.where(groups[3], held[1], jnp.where(groups[0], held[2], nil))))
+                    w = f32(jnp.concatenate(w, axis=0))
                     q = at(end(tr[u, i, 0], t == 2), 0 if t == 1 else 3)
                     new[er][t] = update(
                         f32(rs[u, i, t - 1]),
@@ -580,10 +586,10 @@
             vm((DEG, NB, SIG, TILE), f32), vm((NB, SIG, TILE), f32), vm((NB, 8, TILE), f32), vm((NB, 8, TILE), f32),
             vm((NB, TILE, TILE), bf),
             vm((2, 2, SIG, TILE), bf), vm((2, 2, SIG, TILE), bf), vm((2, 2, 1, TILE), f32),
-            vm((2, 2, SIG, TILE), f32), vm((2, 2, SIG, TILE), bf), vm((2, 10, 32, TILE), bf),
+            vm((2, 2, SIG, TILE), f32), vm((2, 2, SIG, TILE), bf), vm((2, 9, 32, TILE), bf),
             vm((2, SIG, TILE), bf), vm((2, SIG, TILE), bf), vm((2, 1, TILE), f32), vm((2, SIG, TILE), f32), vm((2, SIG, TILE), bf),
             vm((8, 2, 2, SIG, TILE), bf), vm((8, 2, 2, SIG, TILE), bf), vm((8, 2, 2, 1, TILE), f32),
-            vm((8, 2, 2, SIG, TILE), f32), vm((8, 2, 2, SIG, TILE), bf), vm((8, 2, 10, 32, TILE), bf),
+            vm((8, 2, 2, SIG, TILE), f32), vm((8, 2, 2, SIG, TILE), bf), vm((8, 2, 9, 32, TILE), bf),
             vm((8, 2, SIG, TILE), bf), vm((8, 2, SIG, TILE), bf), vm((8, 2, 1, TILE), f32),
             vm((8, 2, SIG, TILE), f32), vm((8, 2, SIG, TILE), bf),
             vm((DEVICES, 1, TILE), f32), vm((1024, 1, TILE), f32),

time: 27.3 us -> 27.1 us (level)
  no operation moved by 1% of the time
where the time goes in v11:
time: 27.1 us; the launch traced here: 27 us
  Pallas kernels  25.7 us (95%)
  between operations  1.29 us (5%)
    pallas_call x1, Pallas kernels, shards(): pl.pallas_call(kernel, out_shape=(pltpu.VMEM((SCALES, NB, SIG, TILE), f32...  24.8 us
    pallas_call x1, Pallas kernels, shards(): pl.pallas_call(finish, out_shape=(jax.ShapeDtypeStruct((SCALES, NB, SIG,...  0.9 us

profile of v11, /device:TPU:1, one launch (start us, length us, event | category | flops | bytes accessed | tf_op | source)
XLA Modules:
  0.0 27.0 jit_solution(11340860672343853481)
XLA Ops:
  1.3 24.8 %wavelet.1 = (f32[6,16,16,128]{3,2,1,0:T(8,128)S(1)}, f32[6,16]{1,0:T(8,128)S(1)}) custom-call(f32[2,8,16,128]{3,2,1,0:T(8,128)} %sig_h.1, bf16[2,8,4,128,128]{4,3,2,1,0:T(8,128)(2,1)} %til_h.1, s32[2,4,8]{2,1,0:T(4,128)} %bitcast.3, s32[2,4,8]{2,1,0:T(4,128)} %bitcast.4, s32[2,8]{1,0:T(2,128)} %liv_h.1, s32[2,8]{1,0:T(2,128)} %bnd_h.1, f32[6,5]{1,0:T(8,128)} %cof_h.1, ...), custom_call_target="tpu_custom_call" | custom-call | tf_op jit(solution)/shard_map/wavelet/pallas_call | solution.py:574
  26.1 0.9 %finish.1 = (f32[6,16,16,128]{3,2,1,0:T(8,128)}, f32[6,16]{1,0:T(8,128)}) custom-call(f32[6,16,16,128]{3,2,1,0:T(8,128)S(1)} %get-tuple-element.6.tot, f32[6,16]{1,0:T(8,128)S(1)} %get-tuple-element.7.en), custom_call_target="tpu_custom_call" | custom-call | tf_op jit(solution)/shard_map/finish/pallas_call | solution.py:603

commit v12 on v11

--- a/solution.py
+++ b/solution.py
@@ -38,13 +38,6 @@
            ld, r1, r2, w1, r3, r4, w3, sa, ra, in_y, in_xy):
     gx, gy = lax.axis_index("gx"), lax.axis_index("gy")
     me = gx * GYN + gy
-    early = []
-    for n, (src, dst) in enumerate(((sig_h, sig), (liv_h, liv_s), (bnd_h, bnd_s), (dir_h, dir_s), (msk_h, msk_s),
-                                    (cof_h, cof_s), (spb_h, spb_s))):
-        cp = pltpu.make_async_copy(src, dst, ld.at[n])
-        cp.start()
-        early.append(cp)
-
     def exists(d):
         dx, dy = DIRS[d]
         ok = None
@@ -57,10 +50,6 @@
 
     have = [exists(d) for d in range(8)]
     peer = [(gx + dx, gy + dy) for dx, dy in DIRS]
-    flip = lambda v: (v, v + 1 - 2 * (v % 2), (v + 2) % 4, 3 - v)
-    xs, ys, zs = flip(gx // 8), flip(gx // 2 % 4), flip(gy)
-    xyc = [8 * u + 2 * v + w for u in xs for v in ys for w in (gx % 2, 1 - gx % 2)]
-    other = lambda o: (xyc[(o >> 5) * 8 + (o >> 3) % 4 * 2 + (o >> 2) % 2], zs[o % 4])
     rest = (1, 2, 3, 4, 5, 6, 7)
     ring_y, ring_x = (8, 16, 24), (32, 64, 96)
     bar = pltpu.get_barrier_semaphore()
@@ -68,6 +57,16 @@
         @pl.when(have[d])
         def _(d=d):
             pl.semaphore_signal(bar, inc=1, device_id=peer[d], device_id_type=MESH)
+    flip = lambda v: (v, v + 1 - 2 * (v % 2), (v + 2) % 4, 3 - v)
+    xs, ys, zs = flip(gx // 8), flip(gx // 2 % 4), flip(gy)
+    xyc = [8 * u + 2 * v + w for u in xs for v in ys for w in (gx % 2, 1 - gx % 2)]
+    other = lambda o: (xyc[(o >> 5) * 8 + (o >> 3) % 4 * 2 + (o >> 2) % 2], zs[o % 4])
+    early = []
+    for n, (src, dst) in enumerate(((sig_h, sig), (liv_h, liv_s), (bnd_h, bnd_s), (dir_h, dir_s), (msk_h, msk_s),
+                                    (cof_h, cof_s), (spb_h, spb_s))):
+        cp = pltpu.make_async_copy(src, dst, ld.at[n])
+        cp.start()
+        early.append(cp)
     for o in ring_x + ring_y + rest:
         pl.semaphore_signal(bar, inc=1, device_id=other(o), device_id_type=MESH)
     count = jnp.int32(13)

time: 27.1 us -> 27.1 us (level)
  no operation moved by 1% of the time
where the time goes in v12:
time: 27.1 us; the launch traced here: 27 us
  Pallas kernels  25.7 us (95%)
  between operations  1.29 us (5%)
    pallas_call x1, Pallas kernels, shards(): pl.pallas_call(kernel, out_shape=(pltpu.VMEM((SCALES, NB, SIG, TILE), f32...  24.8 us
    pallas_call x1, Pallas kernels, shards(): pl.pallas_call(finish, out_shape=(jax.ShapeDtypeStruct((SCALES, NB, SIG,...  0.9 us

profile of v12, /device:TPU:1, one launch (start us, length us, event | category | flops | bytes accessed | tf_op | source)
XLA Modules:
  0.0 27.0 jit_solution(14258907078731487583)
XLA Ops:
  1.3 24.8 %wavelet.1 = (f32[6,16,16,128]{3,2,1,0:T(8,128)S(1)}, f32[6,16]{1,0:T(8,128)S(1)}) custom-call(f32[2,8,16,128]{3,2,1,0:T(8,128)} %sig_h.1, bf16[2,8,4,128,128]{4,3,2,1,0:T(8,128)(2,1)} %til_h.1, s32[2,4,8]{2,1,0:T(4,128)} %bitcast.3, s32[2,4,8]{2,1,0:T(4,128)} %bitcast.4, s32[2,8]{1,0:T(2,128)} %liv_h.1, s32[2,8]{1,0:T(2,128)} %bnd_h.1, f32[6,5]{1,0:T(8,128)} %cof_h.1, ...), custom_call_target="tpu_custom_call" | custom-call | tf_op jit(solution)/shard_map/wavelet/pallas_call | solution.py:573
  26.1 0.9 %finish.1 = (f32[6,16,16,128]{3,2,1,0:T(8,128)}, f32[6,16]{1,0:T(8,128)}) custom-call(f32[6,16,16,128]{3,2,1,0:T(8,128)S(1)} %get-tuple-element.6.tot, f32[6,16]{1,0:T(8,128)S(1)} %get-tuple-element.7.en), custom_call_target="tpu_custom_call" | custom-call | tf_op jit(solution)/shard_map/finish/pallas_call | solution.py:602
